TPU v7x, 256 devices: a whole 4x4x8 slice. The times are simulated.
256 devices in a mesh: seq: 64 (over x, z, core), head: 4 (over y).
Axes of the slice: x: 4, y: 4, z: 8, core: 2. Of those that a mesh axis runs over, the one named last changes fastest.
Arguments:
- tokens: bfloat16 [2, 8192, 1024], P(None, 'seq', 'head'), may hold values from -6 to 6
- input_norm_gain: float32 [1024], replicated, may hold values from 0.1 to 1.9
- query_key_value_weight: bfloat16 [1024, 3, 1024], P(None, None, 'head'), may hold values from -0.1875 to 0.1875
- forget_gate_weight: bfloat16 [1024, 1024], P(None, 'head'), may hold values from -0.1875 to 0.1875
- convolution_filter_taps: float32 [2, 4, 3, 1024], P(None, None, None, 'head'), may hold values from -3 to 3
- slot_forget_rate: float32 [16, 64], P('head'), may hold values from 2.4414063e-06 to 0.04
- extra_forget_log: float32 [2, 8192], P(None, 'seq'), may hold values from 0 to 1.4, as said below
- head_norm_gain: float32 [16, 64], P('head'), may hold values from 0.1 to 1.9
- output_projection_weight: bfloat16 [1024, 1024], P('head'), may hold values from -0.1875 to 0.1875
- feedforward_norm_gain: float32 [1024], replicated, may hold values from 0.1 to 1.9
- up_projection_weight: bfloat16 [1024, 4096], P(None, 'head'), may hold values from -0.1875 to 0.1875
- down_projection_weight: bfloat16 [4096, 1024], P('head'), may hold values from -0.09375 to 0.09375
Outputs:
- layer_out: bfloat16 [2, 8192, 1024], P(None, 'seq', 'head')
Inputs may be any that keep to these rules, and one draw needn't show every extreme that they name: `extra_forget_log`: one value per position of a sequence, zero at most positions.
All inputs are finite; a program needn't handle non-finite values.
Results may differ from a plain program's by a relative error of at most 0.01.
Values may be sent and summed in bfloat16 or wider, within the bound.
No kernel may reach another device: no remote copies, remote signals or barrier semaphores. Data moves between devices by JAX's collectives and lax.ppermute only.
A program may use at most 128 MiB of HBM per device.

v0:
```python
import jax
import jax.numpy as jnp
from jax import lax
from jax.sharding import Mesh
from jax.sharding import PartitionSpec as P

SPAN = 64
SEQ = ("seq_0", "seq_1", "seq_2")


EPSILON = 1e-06
HIGHEST = lax.Precision.HIGHEST


def nothing_yet(value, identity):
    return jax.tree.map(
        lambda a, e: jnp.broadcast_to(jnp.asarray(e, a.dtype), a.shape), value, identity
    )


def prefix_by_axis(value, axes, combine, identity):
    before = start = nothing_yet(value, identity)
    so_far = value
    for axis in reversed(axes):
        count, index = (lax.axis_size(axis), lax.axis_index(axis))
        pieces = jax.tree.map(lambda part: lax.all_gather(part, axis), so_far)
        inside, so_far = (start, start)
        for k in range(count):
            passed = k < index
            so_far = combine(so_far, jax.tree.map(lambda part: part[k], pieces))
            inside = jax.tree.map(lambda new, old: jnp.where(passed, new, old), so_far, inside)
        before = combine(inside, before)
    return before


def all_in_one(value, axis):
    leaves = jax.tree.leaves(value)
    order = sorted(range(len(leaves)), key=lambda k: -leaves[k].size)
    width = (1, *leaves[order[0]].shape)[-1]
    lines = [
        jnp.pad(leaves[k].reshape(-1), (0, -leaves[k].size % width)).reshape(-1, width)
        for k in order
    ]
    both, at, found = (lax.all_gather(jnp.concatenate(lines), axis), 0, {})
    for k, line in zip(order, lines):
        section = both[:, at : at + len(line)].reshape(len(both), -1)
        found[k] = section[:, : leaves[k].size].reshape(-1, *leaves[k].shape)
        at += len(line)
    numbers = iter(range(len(leaves)))
    return jax.tree.map(lambda _: found[next(numbers)], value)


def entering(value, axes, combine, identity):
    before = start = nothing_yet(value, identity)
    so_far = value
    for axis in reversed(axes):
        count, index = (lax.axis_size(axis), lax.axis_index(axis))
        pieces = all_in_one(so_far, axis)
        inside, so_far = (start, start)
        for k in reversed(range(count)):
            passed = k > index
            so_far = combine(so_far, jax.tree.map(lambda part: part[k], pieces))
            inside = jax.tree.map(lambda new, old: jnp.where(passed, new, old), so_far, inside)
        before = combine(inside, before)
    return before


def in_order(blocks, dim):
    blocks = jnp.moveaxis(blocks, 0, dim)
    dims = blocks.shape
    return blocks.reshape(*dims[:dim], dims[dim] * dims[dim + 1], *dims[dim + 2 :])


def copy_for_each(value, axis):
    copies = jnp.broadcast_to(value, (lax.axis_size(axis), *value.shape))
    return lax.all_to_all(copies, axis, split_axis=0, concat_axis=0, tiled=True)


def gathered_copies(value, axis, dim):
    return in_order(copy_for_each(value, axis), dim)


def with_halo(value, sides, width):
    for axis, dim in sides:
        count, length = (lax.axis_size(axis), value.shape[dim])
        up = [(i, (i + 1) % count) for i in range(count - 1)]
        down = [(j, i) for i, j in up]
        last = lax.slice_in_dim(value, length - width, length, axis=dim)
        first = lax.slice_in_dim(value, 0, width, axis=dim)
        before = lax.ppermute(last, axis, up)
        after = lax.ppermute(first, axis, down)
        value = jnp.concatenate([before, value, after], axis=dim)
    return value


def in_blocks(value, dim, count):
    before, after = (value.shape[:dim], value.shape[dim + 1 :])
    return jnp.moveaxis(value.reshape(*before, count, -1, *after), dim, 0)


def sent_and_summed(value, axis, dim):
    blocks = in_blocks(value, dim, lax.axis_size(axis))
    arrived = lax.all_to_all(blocks, axis, split_axis=0, concat_axis=0, tiled=True)
    return arrived.sum(axis=0)


def normalize(values, gain):
    return values * lax.rsqrt(jnp.mean(values * values, axis=-1, keepdims=True) + EPSILON) * gain


def convolve(padded, taps, backward):
    length = padded.shape[1] - 6
    running = jnp.zeros((padded.shape[0], length, padded.shape[2]), jnp.float32)
    for offset in range(4):
        first_row = 3 + offset if backward else 3 - offset
        running = running + taps[offset] * padded[:, first_row : first_row + length]
    return jax.nn.silu(running).astype(jnp.bfloat16)


def split_heads(mixed, head_count, head_size):
    grouped = mixed.astype(jnp.float32).reshape(
        mixed.shape[0], mixed.shape[1], 3, head_count, head_size
    )
    grouped = jnp.transpose(grouped, (2, 0, 3, 1, 4))
    return (grouped[0], grouped[1], grouped[2])


def log_decay_values(gate_scores, slot_forget_rate, extra_forget_log):
    head_count, slot_count = slot_forget_rate.shape
    gate_opening = jax.nn.sigmoid(
        gate_scores.reshape(gate_scores.shape[0], gate_scores.shape[1], head_count, slot_count)
    )
    log_decay_total = -2.0 * slot_forget_rate * gate_opening - extra_forget_log[:, :, None, None]
    return jnp.transpose(log_decay_total, (0, 2, 1, 3))


def flipped(array):
    return jnp.flip(array, axis=2)


def span_pass(state, block):
    queries, keys_in, values, log_decay_total = block
    state_key, state_value = state
    cumulative = jnp.cumsum(log_decay_total, axis=2)
    inflow = -jnp.expm1(log_decay_total)
    growth = jnp.exp(cumulative)
    shrink = jnp.exp(-cumulative) * inflow
    length = log_decay_total.shape[2]
    causal = (jnp.arange(length)[:, None] >= jnp.arange(length)[None, :]).astype(jnp.float32)
    intersection = jnp.einsum("bhtd,bhjd->bhtj", queries, keys_in, precision=HIGHEST) * causal
    scores = jnp.einsum("bhtj,bhjs->bhts", intersection, shrink, precision=HIGHEST)
    scores = growth * (
        scores + jnp.einsum("bhsd,bhtd->bhts", state_key, queries, precision=HIGHEST)
    )
    attend = jax.nn.softmax(scores, axis=-1)
    weighted = attend * growth
    mixing = jnp.einsum("bhts,bhjs->bhtj", weighted, shrink, precision=HIGHEST) * causal
    output = jnp.einsum("bhtj,bhjd->bhtd", mixing, values, precision=HIGHEST)
    output = output + jnp.einsum("bhts,bhsd->bhtd", weighted, state_value, precision=HIGHEST)
    ending = jnp.exp(cumulative[:, :, -1, :])
    remain = ending[:, :, None, :] * shrink
    state_key = ending[..., None] * state_key + jnp.einsum(
        "bhjs,bhjd->bhsd", remain, keys_in, precision=HIGHEST
    )
    state_value = ending[..., None] * state_value + jnp.einsum(
        "bhjs,bhjd->bhsd", remain, values, precision=HIGHEST
    )
    return ((state_key, state_value), output)


def recurrence(queries, keys_in, values, log_decay_total, state):
    batch_size, head_count, length = (queries.shape[0], queries.shape[1], queries.shape[2])
    blocks = length // SPAN

    def arrange(array):
        shaped = array.reshape(batch_size, head_count, blocks, SPAN, array.shape[3])
        return jnp.moveaxis(shaped, 2, 0)

    ignored, output = lax.scan(
        span_pass,
        state,
        (arrange(queries), arrange(keys_in), arrange(values), arrange(log_decay_total)),
    )
    return jnp.moveaxis(output, 0, 2).reshape(batch_size, head_count, length, output.shape[-1])


def summarize(keys_in, values, log_decay_total):
    cumulative = jnp.cumsum(log_decay_total, axis=2)
    totals = cumulative[:, :, -1, :]
    remain = jnp.exp(totals[:, :, None, :] - cumulative) * -jnp.expm1(log_decay_total)
    state_key = jnp.einsum("bhjs,bhjd->bhsd", remain, keys_in, precision=HIGHEST)
    state_value = jnp.einsum("bhjs,bhjd->bhsd", remain, values, precision=HIGHEST)
    return (totals, state_key, state_value)


def compose(earlier, latter):
    factor = jnp.exp(latter[0])[..., None]
    return (
        earlier[0] + latter[0],
        factor * earlier[1] + latter[1],
        factor * earlier[2] + latter[2],
    )


def forward_chain(summary):
    blank = (jnp.zeros_like(summary[0]), jnp.zeros_like(summary[1]), jnp.zeros_like(summary[2]))
    carried = prefix_by_axis((summary[0], summary[1], summary[2]), SEQ, compose, blank)
    return (carried[1], carried[2])


def reverse_chain(summary):
    blank = (jnp.zeros_like(summary[0]), jnp.zeros_like(summary[1]), jnp.zeros_like(summary[2]))
    carried = entering((summary[0], summary[1], summary[2]), SEQ, compose, blank)
    return (carried[1], carried[2])


def local(
    tokens,
    input_norm_gain,
    query_key_value_weight,
    forget_gate_weight,
    convolution_filter_taps,
    slot_forget_rate,
    extra_forget_log,
    head_norm_gain,
    output_projection_weight,
    feedforward_norm_gain,
    up_projection_weight,
    down_projection_weight,
):
    batch_size, row_count, part_width = tokens.shape
    head_count = slot_forget_rate.shape[0]
    head_size = head_norm_gain.shape[1]
    weight_flat = query_key_value_weight.reshape(query_key_value_weight.shape[0], -1)
    taps = convolution_filter_taps.reshape(2, 4, -1)
    whole_rows = gathered_copies(tokens, "head", 2)
    normed = normalize(whole_rows.astype(jnp.float32), input_norm_gain).astype(jnp.bfloat16)
    projected = jnp.dot(normed, weight_flat, preferred_element_type=jnp.float32).astype(
        jnp.bfloat16
    )
    padded = with_halo(projected, ((SEQ, 1),), 3).astype(jnp.float32)
    gate_scores = jnp.dot(normed, forget_gate_weight, preferred_element_type=jnp.float32)
    log_decay_total = log_decay_values(gate_scores, slot_forget_rate, extra_forget_log)
    reverse_decay = flipped(log_decay_total)
    forward_parts = split_heads(convolve(padded, taps[0], False), head_count, head_size)
    reverse_parts = [
        flipped(member)
        for member in split_heads(convolve(padded, taps[1], True), head_count, head_size)
    ]
    forward_state = forward_chain(summarize(forward_parts[1], forward_parts[2], log_decay_total))
    forward_out = recurrence(
        forward_parts[0], forward_parts[1], forward_parts[2], log_decay_total, forward_state
    )
    reverse_state = reverse_chain(summarize(reverse_parts[1], reverse_parts[2], reverse_decay))
    reverse_out = recurrence(
        reverse_parts[0], reverse_parts[1], reverse_parts[2], reverse_decay, reverse_state
    )
    gain_shape = head_norm_gain[None, :, None, :]
    combined = normalize(forward_out, gain_shape) + normalize(flipped(reverse_out), gain_shape)
    attention = (
        jnp.transpose(combined, (0, 2, 1, 3))
        .reshape(batch_size, row_count, head_count * head_size)
        .astype(jnp.bfloat16)
    )
    partial_sum = jnp.dot(attention, output_projection_weight, preferred_element_type=jnp.float32)
    shared = sent_and_summed(partial_sum, "head", 2)
    residual = (tokens.astype(jnp.float32) + shared).astype(jnp.bfloat16)
    resid_whole = gathered_copies(residual, "head", 2)
    mlp_in = normalize(resid_whole.astype(jnp.float32), feedforward_norm_gain).astype(jnp.bfloat16)
    hidden = jax.nn.gelu(
        jnp.dot(mlp_in, up_projection_weight, preferred_element_type=jnp.float32)
    ).astype(jnp.bfloat16)
    terms = jnp.dot(hidden, down_projection_weight, preferred_element_type=jnp.float32)
    update = sent_and_summed(terms, "head", 2)
    return (residual.astype(jnp.float32) + update).astype(jnp.bfloat16)


def solution(mesh):
    split = Mesh(
        mesh.devices.reshape(4, 8, 2, mesh.shape["head"]), ("seq_0", "seq_1", "seq_2", "head")
    )
    placed = (
        P(None, SEQ, "head"),
        P(),
        P(None, None, "head"),
        P(None, "head"),
        P(None, None, None, "head"),
        P("head", None),
        P(None, SEQ),
        P("head", None),
        P("head", None),
        P(),
        P(None, "head"),
        P("head", None),
    )
    return jax.shard_map(
        local, mesh=split, in_specs=placed, out_specs=P(None, SEQ, "head"), check_vma=False
    )
```

profile of v0, /device:TPU:2, one launch (start us, length us, event | category | flops | bytes accessed | tf_op | source)
XLA Modules:
  0.0 350.2 jit_solution(15143360726358103088)
XLA Ops:
  6.5 1.9 broadcast_in_dim.10
  8.4 4.6 %all-to-all-start = ((bf16[4,2,128,256]{3,2,1,0:T(8,128)(2,1)}), bf16[4,2,128,256]{3,2,1,0:T(8,128)(2,1)S(1)}, u32[]{:S(2)}, u32[]{:S(2)}) async-start(bf16[4,2,128,256]{3,2,1,0:T(8,128)(2,1)} %broadcast_in_dim.10), calls=%async_computation | async-start | bytes 1048576 | tf_op jit(solution)/shard_map/all_to_all | solution.py:76
  13.7 2.6 copy.200
  23.2 2.0 convolution_convert_fusion
  25.8 1.9 collective-permute-start
  27.8 6.6 %collective-permute-start.1 = (bf16[2,3,768]{2,1,0:T(4,128)(2,1)}, bf16[2,3,768]{2,1,0:T(4,128)(2,1)}, u32[]{:S(2)}, u32[]{:S(2)}) collective-permute-start(bf16[2,3,768]{2,1,0:T(4,128)(2,1)} %get-tuple-element.220), channel_id=1, source_target_pairs={{4,0},{8,4},{12,8},{16,12},{20,16},{24,20},{28,24},{32,28},{36,32}... | collective-permute-start | bytes 27656 | tf_op jit(solution)/shard_map/ppermute | solution.py:91
  35.7 1.5 reduce_window_sum.34
  37.3 1.8 all-gather
  40.2 2.4 multiply_convert_fusion.1
  42.6 1.9 copy.203
  44.5 2.0 fusion.141
  47.4 2.2 all-gather.1
  49.6 2.2 all-gather.2
  54.1 2.3 reduce_window_sum.35
  57.1 1.9 copy.212
  60.4 2.0 slice_bitcast_fusion
  68.4 2.2 all-gather.7
  74.2 2.1 copy.292
  78.6 2.0 copy.205
  80.6 2.1 copy.261
  82.7 25.3 %all-gather.6 = f32[16,4,1,64]{3,1,2,0:T(4,128)S(1)} all-gather(f32[2,4,1,64]{3,1,2,0:T(4,128)S(1)} %get-tuple-element.158), channel_id=8, replica_groups=mesh['seq_0'=4,'seq_1'=8,'seq_2'=2,'head'=4] {'seq_1'}, dimensions={0}, use_global_device_ids=true | all-gather | bytes 18432 | tf_op jit(solution)/shard_map/all_gather | solution.py:26
  108.1 12.3 %all_gather.59 = f32[4,2,4,64]{3,2,1,0:T(4,128)S(1)} all-gather(f32[1,2,4,64]{3,2,1,0:T(4,128)S(1)} %get-tuple-element.156), channel_id=1, replica_groups=mesh['seq_0'=4,'seq_1'=8,'seq_2'=2,'head'=4] {'seq_0'}, dimensions={0}, use_global_device_ids=true | all-gather | bytes 10240 | tf_op jit(solution)/shard_map/all_gather | solution.py:26
  122.6 2.0 fusion.149
  135.2 2.0 multiply_add_fusion
  137.3 15.4 %all_gather.67 = f32[4,2,4,64,64]{4,3,2,1,0:T(8,128)} all-gather(f32[1,2,4,64,64]{4,3,2,1,0:T(8,128)S(1)} %multiply_add_fusion), channel_id=1, replica_groups=mesh['seq_0'=4,'seq_1'=8,'seq_2'=2,'head'=4] {'seq_0'}, dimensions={0}, use_global_device_ids=true | all-gather | bytes 655360 | tf_op jit(solution)/shard_map/all_gather | solution.py:26
  152.6 2.2 multiply_add_fusion.1
  154.8 13.8 %all_gather.63 = f32[4,2,4,64,64]{4,3,2,1,0:T(8,128)S(1)} all-gather(f32[1,2,4,64,64]{4,3,2,1,0:T(8,128)S(1)} %multiply_add_fusion.1), channel_id=1, replica_groups=mesh['seq_0'=4,'seq_1'=8,'seq_2'=2,'head'=4] {'seq_0'}, dimensions={0}, use_global_device_ids=true | all-gather | bytes 655360 | tf_op jit(solution)/shard_map/all_gather | solution.py:26
  168.7 1.5 fusion.83
  170.4 1.5 fusion.90
  171.9 6.0 %all-gather.19.cloned.1.call-done = f32[8,1032,64]{1,2,0:T(8,128)} async-done(((f32[1,1032,64]{1,2,0:T(8,128)}), f32[8,1032,64]{1,2,0:T(8,128)}) %all-gather.19.cloned.1.call-update) | async-done | bytes 2113552 | tf_op jit(solution)/shard_map/all_gather | solution.py:44
  184.6 21.1 %while.28 = (s32[]{:T(128)}, f32[2,4,64,64]{3,2,1,0:T(8,128)S(1)}, f32[2,4,64,64]{3,2,1,0:T(8,128)S(1)}, f32[2,2,4,64,64]{4,3,2,1,0:T(8,128)}, f32[2,2,4,64,64]{...) while((s32[]{:T(128)}, f32[2,4,64,64]{3,2,1,0:T(8,128)S(1)}, ...), condition=%wide.region_6.7_spmd, body=%wide.region_2.6_spmd.sunk | while | flops 204054592 | bytes 12007153 | solution.py:179
  186.9 1.6 convolution_multiply_fusion.8
  190.0 1.7 fusion.245
  197.5 1.6 convolution_multiply_fusion.8
  200.5 1.7 fusion.245
  209.1 2.6 fusion.145
  211.6 1.7 copy.251
  213.4 1.8 copy.252
  215.1 1.7 copy.253
  216.9 1.7 copy.254
  228.8 2.2 fusion.147
  231.0 1.8 copy.247
  232.8 1.7 copy.248
  234.5 1.7 copy.249
  236.3 1.7 copy.250
  238.0 1.4 fusion.148
  239.4 1.4 copy.306
  242.1 1.4 copy.307
  244.8 1.4 copy.308
  247.5 1.4 copy.309
  250.2 1.7 copy.233
  252.0 1.7 copy.234
  253.7 1.8 copy.235
  256.6 3.6 %add_add_fusion = f32[2,4,64,64]{3,2,1,0:T(8,128)} fusion(f32[2,4,64,64]{3,2,1,0:T(8,128)S(1)} %bitcast.698, f32[2,4,64,64]{3,2,1,0:T(8,128)S(1)} %bitcast.697, f32[2,4,64,64]{3,2,1,0:T(8,128)} %bitcast.714, f32[2,4,64,64]{3,2,1,0:T(8,128)} %bitcast.713, f32[2,4,64,64]{3,2,1,0:T(8,128)} %bitcast.712, f32[2,4,64,64]{3,2,1,0:T(8,128)} %bitcast.711, ...), kind=kLoop, calls=%fused_computation.179 | loop fusion | flops 1409024 | bytes 1998862 | tf_op jit(solution)/shard_map/add | solution.py:201
  260.4 2.0 add_add_fusion.1
  263.3 29.4 %while.29 = (s32[]{:T(128)}, f32[2,4,64,64]{3,2,1,0:T(8,128)}, f32[2,4,64,64]{3,2,1,0:T(8,128)}, f32[2,2,4,64,64]{4,3,2,1,0:T(8,128)}, f32[2,2,4,64,64]{4,3,2,1,...) while((s32[]{:T(128)}, f32[2,4,64,64]{3,2,1,0:T(8,128)}, ...), condition=%wide.region_13.14_spmd, body=%wide.region_9.13_spmd.sunk | while | flops 204054592 | bytes 11731265 | solution.py:179
  265.6 2.5 constant_dynamic-slice_fusion.6
  271.4 1.5 fusion.266
  280.3 2.5 constant_dynamic-slice_fusion.6
  286.1 1.5 fusion.266
  297.7 15.5 %all_to_all.21 = f32[4,2,128,256]{3,2,1,0:T(8,128)S(1)} all-to-all(f32[4,2,128,256]{3,2,1,0:T(8,128)S(1)} %copy.268), channel_id=1, replica_groups=mesh['seq_0'=4,'seq_1'=8,'seq_2'=2,'head'=4] {'head'}, dimensions={0} | all-to-all | bytes 2097152 | tf_op jit(solution)/shard_map/all_to_all | solution.py:103
  314.3 10.5 %all_to_all.20 = bf16[4,2,128,256]{3,2,1,0:T(8,128)(2,1)S(1)} all-to-all(bf16[4,2,128,256]{3,2,1,0:T(8,128)(2,1)S(1)} %broadcast_in_dim.11), channel_id=1, replica_groups=mesh['seq_0'=4,'seq_1'=8,'seq_2'=2,'head'=4] {'head'}, dimensions={0} | all-to-all | bytes 1048576 | tf_op jit(solution)/shard_map/all_to_all | solution.py:76
  326.3 3.2 fusion.40
  329.6 13.3 %all_to_all.22 = f32[4,2,128,256]{3,2,1,0:T(8,128)S(1)} all-to-all(f32[4,2,128,256]{3,2,1,0:T(8,128)S(1)} %bitcast.689), channel_id=1, replica_groups=mesh['seq_0'=4,'seq_1'=8,'seq_2'=2,'head'=4] {'head'}, dimensions={0} | all-to-all | bytes 2097152 | tf_op jit(solution)/shard_map/all_to_all | solution.py:103
  (390 shorter events, 111.2 us)
Async XLA Ops:
  6.5 319.7 %copy-start = (bf16[1024,1024]{1,0:T(8,128)(2,1)S(1)}, bf16[1024,1024]{1,0:T(8,128)(2,1)}, u32[]{:S(2)}) copy-start(bf16[1024,1024]{1,0:T(8,128)(2,1)} %param.27) | copy-start | bytes 6291460
  8.4 7.9 %copy-start.75 = (f32[2,4,3,256]{3,1,2,0:T(4,128)S(1)}, f32[2,4,3,256]{3,1,2,0:T(4,128)}, u32[]{:S(2)}) copy-start(f32[2,4,3,256]{3,1,2,0:T(4,128)} %param.20) | copy-start | bytes 73732
  8.4 12.8 %copy-start.38 = (bf16[1024,256]{1,0:T(8,128)(2,1)S(1)}, bf16[1024,256]{1,0:T(8,128)(2,1)}, u32[]{:S(2)}) copy-start(bf16[1024,256]{1,0:T(8,128)(2,1)} %param.19) | copy-start | bytes 1572868
  8.4 14.1 %all-to-all-start = ((bf16[4,2,128,256]{3,2,1,0:T(8,128)(2,1)}), bf16[4,2,128,256]{3,2,1,0:T(8,128)(2,1)S(1)}, u32[]{:S(2)}, u32[]{:S(2)}) async-start(bf16[4,2,128,256]{3,2,1,0:T(8,128)(2,1)} %broadcast_in_dim.10), calls=%async_computation | async-start | bytes 1048576 | tf_op jit(solution)/shard_map/all_to_all | solution.py:76
  13.0 122.2 %all-gather.17.cloned.1.call-start = ((), (), s32[]{:S(2)}) async-start(), calls=%async_computation.5 | async-start | bytes 2359296 | tf_op jit(solution)/shard_map/all_gather | solution.py:26
  13.7 8.5 %copy-start.79 = (f32[4,64]{1,0:T(4,128)S(1)}, f32[4,64]{1,0:T(4,128)}, u32[]{:S(2)}) copy-start(f32[4,64]{1,0:T(4,128)} %param.21) | copy-start | bytes 3076
  22.8 11.6 %copy-start.39 = (bf16[1024,256]{0,1:T(8,128)(2,1)S(1)}, bf16[1024,256]{0,1:T(8,128)(2,1)}, u32[]{:S(2)}) copy-start(bf16[1024,256]{0,1:T(8,128)(2,1)} %copy.185) | copy-start | bytes 1572868
  22.8 11.6 %copy-start.80 = (f32[2,128]{1,0:T(2,128)S(1)}, f32[2,128]{1,0:T(2,128)}, u32[]{:S(2)}) copy-start(f32[2,128]{1,0:T(2,128)} %param.22) | copy-start | bytes 3076
  25.8 13.5 %collective-permute-start = (bf16[2,3,768]{2,1,0:T(4,128)(2,1)}, bf16[2,3,768]{2,1,0:T(4,128)(2,1)}, u32[]{:S(2)}, u32[]{:S(2)}) collective-permute-start(bf16[2,3,768]{2,1,0:T(4,128)(2,1)} %get-tuple-element.219), channel_id=1, source_target_pairs={{0,4},{4,8},{8,12},{12,16},{16,20},{20,24},{24,28},{28,32},{32,36}... | collective-permute-start | bytes 27656 | tf_op jit(solution)/shard_map/ppermute | solution.py:90
  27.8 11.6 %collective-permute-start.1 = (bf16[2,3,768]{2,1,0:T(4,128)(2,1)}, bf16[2,3,768]{2,1,0:T(4,128)(2,1)}, u32[]{:S(2)}, u32[]{:S(2)}) collective-permute-start(bf16[2,3,768]{2,1,0:T(4,128)(2,1)} %get-tuple-element.220), channel_id=1, source_target_pairs={{4,0},{8,4},{12,8},{16,12},{20,16},{24,20},{28,24},{32,28},{36,32}... | collective-permute-start | bytes 27656 | tf_op jit(solution)/shard_map/ppermute | solution.py:91
  42.6 4.0 %copy-start.57 = (f32[2,4,1,64]{3,2,1,0:T(1,128)S(1)}, f32[2,4,1,64]{3,2,1,0:T(1,128)}, u32[]{:S(2)}) copy-start(f32[2,4,1,64]{3,2,1,0:T(1,128)} %copy-done.56) | copy-start | bytes 6148
  52.8 99.8 %all-gather.15.cloned.1.call-start = ((), (), s32[]{:S(2)}) async-start(), calls=%async_computation.4 | async-start | bytes 2359296 | tf_op jit(solution)/shard_map/all_gather | solution.py:26
  60.3 117.6 %all-gather.19.cloned.1.call-start = ((), (), s32[]{:S(2)}) async-start(), calls=%async_computation.6 | async-start | bytes 2654208 | tf_op jit(solution)/shard_map/all_gather | solution.py:44
  71.3 7.2 %copy-start.65 = (f32[1,8,64]{2,1,0:T(8,128)}, f32[1,8,64]{2,1,0:T(8,128)S(1)}, u32[]{:S(2)}) copy-start(f32[1,8,64]{2,1,0:T(8,128)S(1)} %copy.297) | copy-start | bytes 6148
  74.1 154.7 %all-gather.21.cloned.1.call-start = ((), (), s32[]{:S(2)}) async-start(), calls=%async_computation.7 | async-start | bytes 1474560 | tf_op jit(solution)/shard_map/all_gather | solution.py:44
  77.4 44.1 %copy-start.19 = (f32[2,4,128,64]{2,3,1,0:T(8,128)S(1)}, f32[2,4,128,64]{2,3,1,0:T(8,128)}, u32[]{:S(2)}) copy-start(f32[2,4,128,64]{2,3,1,0:T(8,128)} %copy-done.18) | copy-start | bytes 786436
  129.5 4.5 %copy-start.37 = (f32[2,4,128,64]{2,3,1,0:T(8,128)S(1)}, f32[2,4,128,64]{2,3,1,0:T(8,128)}, u32[]{:S(2)}) copy-start(f32[2,4,128,64]{2,3,1,0:T(8,128)} %get-tuple-element.206) | copy-start | bytes 786436
  152.6 16.0 %copy-start.13 = (f32[4,4,64,64]{3,2,1,0:T(8,128)S(1)}, f32[4,4,64,64]{3,2,1,0:T(8,128)}, u32[]{:S(2)}) copy-start(f32[4,4,64,64]{3,2,1,0:T(8,128)} %copy-done.12) | copy-start | bytes 786436
  152.6 16.0 %copy-start.8 = (f32[8,2,4,64,64]{4,3,2,1,0:T(8,128)S(1)}, f32[8,2,4,64,64]{4,3,2,1,0:T(8,128)}, u32[]{:S(2)}) copy-start(f32[8,2,4,64,64]{4,3,2,1,0:T(8,128)} %all-gather.17.cloned.1.call-done) | copy-start | bytes 3145732
  152.6 16.1 %copy-start.17 = (f32[4,2,4,64,64]{4,3,2,1,0:T(8,128)S(1)}, f32[4,2,4,64,64]{4,3,2,1,0:T(8,128)}, u32[]{:S(2)}) copy-start(f32[4,2,4,64,64]{4,3,2,1,0:T(8,128)} %all_gather.67) | copy-start | bytes 1572868
  178.8 5.7 %copy-start.67 = (f32[1,8,64]{2,1,0:T(8,128)}, f32[1,8,64]{2,1,0:T(8,128)S(1)}, u32[]{:S(2)}) copy-start(f32[1,8,64]{2,1,0:T(8,128)S(1)} %copy.298) | copy-start | bytes 6148
  178.9 5.7 %copy-start.68 = (f32[1,8,64]{2,1,0:T(8,128)}, f32[1,8,64]{2,1,0:T(8,128)S(1)}, u32[]{:S(2)}) copy-start(f32[1,8,64]{2,1,0:T(8,128)S(1)} %copy.299) | copy-start | bytes 6148
  179.0 5.6 %copy-start.69 = (f32[1,8,64]{2,1,0:T(8,128)}, f32[1,8,64]{2,1,0:T(8,128)S(1)}, u32[]{:S(2)}) copy-start(f32[1,8,64]{2,1,0:T(8,128)S(1)} %copy.300) | copy-start | bytes 6148
  179.0 5.5 %copy-start.70 = (f32[1,8,64]{2,1,0:T(8,128)}, f32[1,8,64]{2,1,0:T(8,128)S(1)}, u32[]{:S(2)}) copy-start(f32[1,8,64]{2,1,0:T(8,128)S(1)} %copy.301) | copy-start | bytes 6148
  179.1 5.5 %copy-start.71 = (f32[1,8,64]{2,1,0:T(8,128)}, f32[1,8,64]{2,1,0:T(8,128)S(1)}, u32[]{:S(2)}) copy-start(f32[1,8,64]{2,1,0:T(8,128)S(1)} %copy.302) | copy-start | bytes 6148
  179.2 5.4 %copy-start.72 = (f32[1,8,64]{2,1,0:T(8,128)}, f32[1,8,64]{2,1,0:T(8,128)S(1)}, u32[]{:S(2)}) copy-start(f32[1,8,64]{2,1,0:T(8,128)S(1)} %copy.303) | copy-start | bytes 6148
  179.2 5.4 %copy-start.73 = (f32[1,8,64]{2,1,0:T(8,128)}, f32[1,8,64]{2,1,0:T(8,128)S(1)}, u32[]{:S(2)}) copy-start(f32[1,8,64]{2,1,0:T(8,128)S(1)} %copy.304) | copy-start | bytes 6148
  179.3 5.3 %copy-start.74 = (f32[1,8,64]{2,1,0:T(8,128)}, f32[1,8,64]{2,1,0:T(8,128)S(1)}, u32[]{:S(2)}) copy-start(f32[1,8,64]{2,1,0:T(8,128)S(1)} %copy.305) | copy-start | bytes 6148
  200.5 3.1 copy-start.14
  219.4 8.0 %copy-start.64 = (f32[1,8,64]{2,1,0:T(8,128)S(1)}, f32[1,8,64]{2,1,0:T(8,128)}, u32[]{:S(2)}) copy-start(f32[1,8,64]{2,1,0:T(8,128)} %copy.296) | copy-start | bytes 6148
  219.4 8.0 %copy-start.66 = (f32[1,8,64]{2,1,0:T(8,128)S(1)}, f32[1,8,64]{2,1,0:T(8,128)}, u32[]{:S(2)}) copy-start(f32[1,8,64]{2,1,0:T(8,128)} %copy-done.65) | copy-start | bytes 6148
  231.0 25.5 %copy-start.26 = (f32[1,512,64]{2,1,0:T(8,128)S(1)}, f32[1,512,64]{2,1,0:T(8,128)}, u32[]{:S(2)}) copy-start(f32[1,512,64]{2,1,0:T(8,128)} %copy.259) | copy-start | bytes 393220
  231.0 25.5 %copy-start.27 = (f32[1,512,64]{2,1,0:T(8,128)S(1)}, f32[1,512,64]{2,1,0:T(8,128)}, u32[]{:S(2)}) copy-start(f32[1,512,64]{2,1,0:T(8,128)} %copy.260) | copy-start | bytes 393220
  231.0 25.5 %copy-start.41 = (f32[1,8,64]{2,1,0:T(8,128)S(1)}, f32[1,8,64]{2,1,0:T(8,128)}, u32[]{:S(2)}) copy-start(f32[1,8,64]{2,1,0:T(8,128)} %copy-done.40) | copy-start | bytes 6148
  231.0 25.5 %copy-start.43 = (f32[1,8,64]{2,1,0:T(8,128)S(1)}, f32[1,8,64]{2,1,0:T(8,128)}, u32[]{:S(2)}) copy-start(f32[1,8,64]{2,1,0:T(8,128)} %copy-done.42) | copy-start | bytes 6148
  256.3 3.9 %copy-start.24 = (f32[1,512,64]{2,1,0:T(8,128)S(1)}, f32[1,512,64]{2,1,0:T(8,128)}, u32[]{:S(2)}) copy-start(f32[1,512,64]{2,1,0:T(8,128)} %copy.245) | copy-start | bytes 393220
  256.3 3.9 %copy-start.25 = (f32[1,512,64]{2,1,0:T(8,128)S(1)}, f32[1,512,64]{2,1,0:T(8,128)}, u32[]{:S(2)}) copy-start(f32[1,512,64]{2,1,0:T(8,128)} %copy.246) | copy-start | bytes 393220
  256.3 3.9 %copy-start.28 = (f32[1,512,64]{2,1,0:T(8,128)S(1)}, f32[1,512,64]{2,1,0:T(8,128)}, u32[]{:S(2)}) copy-start(f32[1,512,64]{2,1,0:T(8,128)} %copy.240) | copy-start | bytes 393220
  256.3 3.9 %copy-start.29 = (f32[1,512,64]{2,1,0:T(8,128)S(1)}, f32[1,512,64]{2,1,0:T(8,128)}, u32[]{:S(2)}) copy-start(f32[1,512,64]{2,1,0:T(8,128)} %copy.241) | copy-start | bytes 393220
  256.3 3.9 %copy-start.30 = (f32[1,512,64]{2,1,0:T(8,128)S(1)}, f32[1,512,64]{2,1,0:T(8,128)}, u32[]{:S(2)}) copy-start(f32[1,512,64]{2,1,0:T(8,128)} %copy.242) | copy-start | bytes 393220
  256.3 3.9 %copy-start.31 = (f32[1,512,64]{2,1,0:T(8,128)S(1)}, f32[1,512,64]{2,1,0:T(8,128)}, u32[]{:S(2)}) copy-start(f32[1,512,64]{2,1,0:T(8,128)} %copy.243) | copy-start | bytes 393220
  256.3 3.9 %copy-start.32 = (f32[1,512,64]{2,1,0:T(8,128)S(1)}, f32[1,512,64]{2,1,0:T(8,128)}, u32[]{:S(2)}) copy-start(f32[1,512,64]{2,1,0:T(8,128)} %copy.244) | copy-start | bytes 393220
  256.4 3.9 %copy-start.33 = (f32[1,512,64]{2,1,0:T(8,128)S(1)}, f32[1,512,64]{2,1,0:T(8,128)}, u32[]{:S(2)}) copy-start(f32[1,512,64]{2,1,0:T(8,128)} %copy.233) | copy-start | bytes 393220
  256.4 3.9 %copy-start.34 = (f32[1,512,64]{2,1,0:T(8,128)S(1)}, f32[1,512,64]{2,1,0:T(8,128)}, u32[]{:S(2)}) copy-start(f32[1,512,64]{2,1,0:T(8,128)} %copy.234) | copy-start | bytes 393220
  256.4 3.9 %copy-start.35 = (f32[1,512,64]{2,1,0:T(8,128)S(1)}, f32[1,512,64]{2,1,0:T(8,128)}, u32[]{:S(2)}) copy-start(f32[1,512,64]{2,1,0:T(8,128)} %copy.235) | copy-start | bytes 393220
  256.4 3.9 %copy-start.36 = (f32[1,512,64]{2,1,0:T(8,128)S(1)}, f32[1,512,64]{2,1,0:T(8,128)}, u32[]{:S(2)}) copy-start(f32[1,512,64]{2,1,0:T(8,128)} %copy.236) | copy-start | bytes 393220
  256.4 3.9 %copy-start.45 = (f32[1,8,64]{2,1,0:T(8,128)S(1)}, f32[1,8,64]{2,1,0:T(8,128)}, u32[]{:S(2)}) copy-start(f32[1,8,64]{2,1,0:T(8,128)} %copy-done.44) | copy-start | bytes 6148
  256.4 3.9 %copy-start.47 = (f32[1,8,64]{2,1,0:T(8,128)S(1)}, f32[1,8,64]{2,1,0:T(8,128)}, u32[]{:S(2)}) copy-start(f32[1,8,64]{2,1,0:T(8,128)} %copy-done.46) | copy-start | bytes 6148
  256.4 3.9 %copy-start.49 = (f32[1,8,64]{2,1,0:T(8,128)S(1)}, f32[1,8,64]{2,1,0:T(8,128)}, u32[]{:S(2)}) copy-start(f32[1,8,64]{2,1,0:T(8,128)} %copy-done.48) | copy-start | bytes 6148
  256.4 3.9 %copy-start.51 = (f32[1,8,64]{2,1,0:T(8,128)S(1)}, f32[1,8,64]{2,1,0:T(8,128)}, u32[]{:S(2)}) copy-start(f32[1,8,64]{2,1,0:T(8,128)} %copy-done.50) | copy-start | bytes 6148
  256.4 3.9 %copy-start.53 = (f32[1,8,64]{2,1,0:T(8,128)S(1)}, f32[1,8,64]{2,1,0:T(8,128)}, u32[]{:S(2)}) copy-start(f32[1,8,64]{2,1,0:T(8,128)} %copy-done.52) | copy-start | bytes 6148
  256.4 3.9 %copy-start.55 = (f32[1,8,64]{2,1,0:T(8,128)S(1)}, f32[1,8,64]{2,1,0:T(8,128)}, u32[]{:S(2)}) copy-start(f32[1,8,64]{2,1,0:T(8,128)} %copy-done.54) | copy-start | bytes 6148
  256.5 3.9 %copy-start.58 = (f32[1,8,64]{2,1,0:T(8,128)S(1)}, f32[1,8,64]{2,1,0:T(8,128)}, u32[]{:S(2)}) copy-start(f32[1,8,64]{2,1,0:T(8,128)} %get-tuple-element.235) | copy-start | bytes 6148
  256.5 3.9 %copy-start.59 = (f32[1,8,64]{2,1,0:T(8,128)S(1)}, f32[1,8,64]{2,1,0:T(8,128)}, u32[]{:S(2)}) copy-start(f32[1,8,64]{2,1,0:T(8,128)} %add_exponential_fusion) | copy-start | bytes 6148
  256.5 3.9 %copy-start.60 = (f32[1,8,64]{2,1,0:T(8,128)S(1)}, f32[1,8,64]{2,1,0:T(8,128)}, u32[]{:S(2)}) copy-start(f32[1,8,64]{2,1,0:T(8,128)} %exp.426) | copy-start | bytes 6148
  256.5 3.9 %copy-start.61 = (f32[1,8,64]{2,1,0:T(8,128)S(1)}, f32[1,8,64]{2,1,0:T(8,128)}, u32[]{:S(2)}) copy-start(f32[1,8,64]{2,1,0:T(8,128)} %exp.428) | copy-start | bytes 6148
  256.5 3.9 %copy-start.62 = (f32[1,8,64]{2,1,0:T(8,128)S(1)}, f32[1,8,64]{2,1,0:T(8,128)}, u32[]{:S(2)}) copy-start(f32[1,8,64]{2,1,0:T(8,128)} %exp.430) | copy-start | bytes 6148
  256.5 3.9 %copy-start.63 = (f32[1,8,64]{2,1,0:T(8,128)S(1)}, f32[1,8,64]{2,1,0:T(8,128)}, u32[]{:S(2)}) copy-start(f32[1,8,64]{2,1,0:T(8,128)} %exponential_multiply_fusion) | copy-start | bytes 6148
  273.3 3.3 copy-start.4
  288.0 3.3 copy-start.4
  292.7 3.5 %copy-start.76 = (f32[2,4,128]{2,1,0:T(4,128)S(1)}, f32[2,4,128]{2,1,0:T(4,128)}, u32[]{:S(2)}) copy-start(f32[2,4,128]{2,1,0:T(4,128)} %rsqrt.37) | copy-start | bytes 12292
  292.7 3.5 %copy-start.78 = (f32[4,64]{1,0:T(4,128)S(1)}, f32[4,64]{1,0:T(4,128)}, u32[]{:S(2)}) copy-start(f32[4,64]{1,0:T(4,128)} %param.23) | copy-start | bytes 3076
  292.7 4.6 %copy-start.21 = (bf16[1024,256]{1,0:T(8,128)(2,1)S(1)}, bf16[1024,256]{1,0:T(8,128)(2,1)}, u32[]{:S(2)}) copy-start(bf16[1024,256]{1,0:T(8,128)(2,1)} %copy.292) | copy-start | bytes 1572868
  313.3 11.9 %copy-start.77 = (f32[1024]{0:T(1024)S(1)}, f32[1024]{0:T(1024)}, u32[]{:S(2)}) copy-start(f32[1024]{0:T(1024)} %param.25) | copy-start | bytes 12292
  (35 other events, 56.8 us)
Sparse Core Ops, SparseCore 0:
  53.0 42.2 all-gather.16
  97.0 39.2 all-gather.14
  138.1 39.7 all-gather.18
  183.8 24.8 all-gather.20
where the time goes:
time: 353 us; the launch traced here: 350 us
  local copies, waits for them, and re-layouts  121 us (34%)
  blocking collectives  114 us (32%)
  other arithmetic  43.7 us (12%)
  matrix products  36.7 us (10%)
  between operations  14.4 us (4%)
  starting transfers between devices  13.2 us (4%)
  waiting for transfers between devices  6.41 us (2%)
    all_gather x7, blocking collectives, prefix_by_axis(): pieces = jax.tree.map(lambda part: lax.all_gather(part, axis), so_far)  72.9 us
    slice x34, local copies, waits for them, and re-layouts, entering(): so_far = combine(so_far, jax.tree.map(lambda part: part[k], pieces))  39.4 us
    all_to_all x2, blocking collectives, sent_and_summed(): lax.all_to_all(blocks, axis, split_axis=0, concat_axis=0, tiled=True)  28.8 us
    unnamed x156, local copies, waits for them, and re-layouts  11.3 us
    all_to_all x1, blocking collectives, copy_for_each(): return lax.all_to_all(copies, axis, split_axis=0, concat_axis=0, tiled=True)  10.5 us
    reshape x7, local copies, waits for them, and re-layouts, arrange(): shaped = array.reshape(batch_size, head_count, blocks, SPAN, array.shape[3])  9.78 us
    add x5, other arithmetic, compose(): factor * earlier[2] + latter[2]  9.66 us
    dynamic_slice x4, local copies, waits for them, and re-layouts, recurrence(): lax.scan(span_pass, state, (arrange(queries), arrange(keys_in), arrange(v...  7.55 us
  transfers between devices with their start and end apart: 7, of which 2 were waited for; matrix products, arithmetic and copies ran while one was open for 30% of the time, Pallas kernels for 0%

commit v1 on v0

v1 whole, which is shorter than its diff:
```python
import jax
import jax.numpy as jnp
from jax import lax
from jax.experimental import pallas as pl
from jax.experimental.pallas import tpu as pltpu
from jax.sharding import Mesh
from jax.sharding import PartitionSpec as P

CHIPS = ("x", "z")
SEQ = ("x", "z", "core")
EPSILON = 1e-06
BF16 = jnp.bfloat16
F32 = jnp.float32
HIGHEST = lax.Precision.HIGHEST
SPAN = 64
ROWS = 256
LANES = 256
SPANS = ROWS // SPAN


def nn(a, b, precision=None):
    return lax.dot_general(
        a, b, (((1,), (0,)), ((), ())), preferred_element_type=F32, precision=precision
    )


def nt(a, b):
    return lax.dot_general(a, b, (((1,), (1,)), ((), ())), preferred_element_type=F32)


def tn(a, b, precision=None):
    return lax.dot_general(
        a, b, (((0,), (0,)), ((), ())), preferred_element_type=F32, precision=precision
    )


def iota(shape, dim):
    return lax.broadcasted_iota(jnp.int32, shape, dim)


def in_first_head(rows):
    return iota((rows, 128), 1) < 64


def compact(blocks):
    first = in_first_head(64)
    left = jnp.where(first, blocks[0:64, 0:128], blocks[64:128, 0:128])
    right = jnp.where(first, blocks[128:192, 128:256], blocks[192:256, 128:256])
    return jnp.concatenate([left, right], axis=1)


def compact_rows(column):
    first = in_first_head(64)
    left = jnp.where(first, column[0:64], column[64:128])
    right = jnp.where(first, column[128:192], column[192:256])
    return jnp.concatenate([left, right], axis=1)


def minus_expm1(x):
    series = 1.0 + x * (1.0 / 7.0)
    for k in (6, 5, 4, 3, 2):
        series = 1.0 + x * (1.0 / k) * series
    return jnp.where(x > -0.3, -x * series, 1.0 - jnp.exp(x))


def as_column(row):
    picked = jnp.where(iota((128, 128), 0) == iota((128, 128), 1), row, 0.0)
    return jnp.sum(picked, axis=1, keepdims=True)


def split_kernel(tokens, extra, swap_out, a_out, b_out, mine_out):
    core = lax.axis_index("core")
    mine = tokens[core]
    other = tokens[1 - core]
    mine_out[...] = mine
    row = extra[pl.ds(1 - core, 1), :]
    high = row.astype(BF16).astype(F32)
    middle = (row - high).astype(BF16).astype(F32)
    low = row - high - middle
    line = iota((8, 256), 0)
    first = jnp.concatenate([high, middle], axis=1)
    second = jnp.concatenate([low, low], axis=1)
    packed = jnp.where(line == 0, first, jnp.where(line == 1, second, 0.0))
    swap_out[...] = jnp.concatenate([other.astype(F32), packed], axis=0).astype(BF16)
    wide_other = other.astype(F32)
    wide_mine = mine.astype(F32)
    a_out[...] = jnp.where(core == 1, wide_other[120:128], wide_other[0:8]).astype(BF16)
    b_out[...] = jnp.where(core == 1, wide_mine[120:128], wide_mine[0:8]).astype(BF16)


def front_kernel(
    part0, part1, part2, part3, gain, qkv_weight, gate_weight, taps, rate, extra, extra_other,
    qkv_out, cum_out, shrink_out, start_out, reach_out, sent_out, tokens_out,
    padded, decay,
):
    core = lax.axis_index("core")
    head = lax.axis_index("head")
    parts = (part0, part1, part2, part3)
    sources = [lax.rem(head + 4 - k, 4) for k in range(4)]
    own_rows = pl.multiple_of(core * 128, 128)
    other_rows = pl.multiple_of((1 - core) * 128, 128)
    square = jnp.zeros((ROWS + 16, 1), F32)
    for k in range(4):
        values = parts[k][...]
        tokens_out[sources[k], pl.ds(own_rows, 128), :] = values[0:128]
        tokens_out[sources[k], pl.ds(other_rows, 128), :] = values[128:256]
        wide = values.astype(F32)
        square = square + jnp.sum(wide * wide, axis=1, keepdims=True)
    scale = lax.rsqrt(square * (1.0 / 1024.0) + EPSILON)
    normed = [
        (parts[k][...].astype(F32) * scale * gain[pl.ds(sources[k], 1), :]).astype(BF16)
        for k in range(4)
    ]
    starts = [pl.multiple_of(source * 256, 256) for source in sources]
    own_pad = pl.multiple_of(8 + core * 128, 8)
    other_pad = pl.multiple_of(8 + (1 - core) * 128, 8)
    a_pad = pl.multiple_of(core * 264, 8)
    b_pad = pl.multiple_of((1 - core) * 264, 8)
    for i in range(3):
        total = nn(normed[0], qkv_weight[i, pl.ds(starts[0], 256), :])
        for k in range(1, 4):
            total = total + nn(normed[k], qkv_weight[i, pl.ds(starts[k], 256), :])
        total = total.astype(BF16).astype(F32)
        columns = slice(i * 256, (i + 1) * 256)
        padded[pl.ds(own_pad, 128), columns] = total[0:128]
        padded[pl.ds(other_pad, 128), columns] = total[128:256]
        padded[pl.ds(a_pad, 8), columns] = total[256:264]
        padded[pl.ds(b_pad, 8), columns] = total[264:272]
    gate = nn(normed[0], gate_weight[pl.ds(starts[0], 256), :])
    for k in range(1, 4):
        gate = gate + nn(normed[k], gate_weight[pl.ds(starts[k], 256), :])
    own_extra = as_column(extra[pl.ds(core, 1), :])
    sent = extra_other[...].astype(F32)
    other_extra = as_column(sent[0:1, 0:128] + sent[0:1, 128:256] + sent[1:2, 0:128])
    decays = -2.0 * rate[...] * jax.nn.sigmoid(gate[0:256])
    decay[pl.ds(own_rows, 128), :] = decays[0:128] - own_extra
    decay[pl.ds(other_rows, 128), :] = decays[128:256] - other_extra

    for i in range(3):
        columns = slice(i * 256, (i + 1) * 256)
        for direction in range(2):
            running = taps[direction, i, 0:1, :] * padded[8 : 8 + ROWS, columns]
            for j in range(1, 4):
                first = 8 + j if direction else 8 - j
                running = running + taps[direction, i, j : j + 1, :] * padded[
                    first : first + ROWS, columns
                ]
            qkv_out[direction, i] = (running * jax.nn.sigmoid(running)).astype(BF16)

    log_decay = decay[...]
    inflow = minus_expm1(log_decay)
    row, col = iota((ROWS, ROWS), 0), iota((ROWS, ROWS), 1)
    same = (row // SPAN) == (col // SPAN)
    earlier = (same & (col <= row)).astype(F32)
    later = (same & (col >= row)).astype(F32)
    spans = (iota((ROWS, 128 * SPANS), 0) // SPAN == iota((ROWS, 128 * SPANS), 1) // 128).astype(F32)
    span_totals = tn(log_decay, spans, HIGHEST)
    totals = [compact_rows(span_totals[:, n * 128 : (n + 1) * 128]) for n in range(SPANS)]
    factors = [jnp.exp(total) for total in totals]
    ends = []
    for direction in range(2):
        cumulative = nn(later if direction else earlier, log_decay, HIGHEST)
        cum_out[direction] = cumulative
        shrink_out[direction] = (jnp.exp(-cumulative) * inflow).astype(BF16)
        states = [jnp.zeros((SPAN, LANES), F32), jnp.zeros((SPAN, LANES), F32)]
        passed = jnp.zeros((SPAN, LANES), F32)
        for n in reversed(range(SPANS)) if direction else range(SPANS):
            rows = slice(n * SPAN, (n + 1) * SPAN)
            start_out[direction, n, 0] = states[0]
            start_out[direction, n, 1] = states[1]
            reach_out[direction, n] = jnp.exp(passed)
            local = cumulative[rows]
            last = local[0:1] if direction else local[SPAN - 1 : SPAN]
            remain = (jnp.exp(last - local) * inflow[rows]).astype(BF16)
            for which in range(2):
                added = compact(tn(remain, qkv_out[direction, 1 + which, rows, :]))
                states[which] = factors[n] * states[which] + added
            passed = passed + totals[n]
        ends.append(states)
    factor = jnp.exp(totals[0] + totals[1] + totals[2] + totals[3])
    high = factor.astype(BF16).astype(F32)
    lane = iota((SPAN, LANES), 1)
    factor_parts = jnp.where(lane % 64 < 32, high, factor - high)
    for which in range(2):
        for half in range(2):
            lanes = slice(half * 128, (half + 1) * 128)
            for block in range(8):
                rows = slice(block * 8, block * 8 + 8)
                sent_out[which * 16 + half * 8 + block] = jnp.concatenate(
                    [
                        ends[0][which][rows, lanes],
                        ends[1][which][rows, lanes],
                        factor_parts[rows, lanes],
                    ],
                    axis=0,
                ).astype(BF16)


def scan_kernel(pieces, states_out, wide):
    count = pieces.shape[0]
    first = iota((8, 128), 1) % 64 < 32
    factors, forward, backward = [], [], []
    for i in range(count):
        piece = pieces[i].astype(F32)
        both = piece[16:24]
        factors.append(both + jnp.where(first, pltpu.roll(both, 96, 1), pltpu.roll(both, 32, 1)))
        forward.append(piece[0:8])
        backward.append(piece[8:16])
    state = jnp.zeros((8, 128), F32)
    for i in range(count):
        wide[i, 0:8, :] = state
        state = factors[i] * state + forward[i]
    state = jnp.zeros((8, 128), F32)
    for i in reversed(range(count)):
        wide[i, 8:16, :] = state
        state = factors[i] * state + backward[i]
    states_out[...] = wide[...].astype(BF16)


def head_max(values):
    first = in_first_head(SPAN)
    halves = []
    for half in range(2):
        part = values[:, half * 128 : (half + 1) * 128]
        left = jnp.max(jnp.where(first, part, -jnp.inf), axis=1, keepdims=True)
        right = jnp.max(jnp.where(first, -jnp.inf, part), axis=1, keepdims=True)
        halves.append(jnp.where(first, left, right))
    return jnp.concatenate(halves, axis=1)


def attention_kernel(qkv, cumulative, shrink, start, reach, arrived, gain, out, entering):
    for m in range(32):
        which, half, block = m // 16, (m // 8) % 2, m % 8
        piece = arrived[m].astype(F32)
        for direction in range(2):
            entering[direction, which, block * 8 : block * 8 + 8, half * 128 : half * 128 + 128] = (
                piece[direction * 8 : direction * 8 + 8]
            )
    own = (iota((LANES, LANES), 0) // 64 == iota((LANES, LANES), 1) // 64).astype(BF16)
    position, other = iota((SPAN, LANES), 0), iota((SPAN, LANES), 1) % SPAN

    def expand(values):
        return jnp.concatenate([values] * 4, axis=0) * own

    for n in range(SPANS):
        rows = slice(n * SPAN, (n + 1) * SPAN)
        combined = jnp.zeros((SPAN, LANES), F32)
        for direction in range(2):
            seen = other >= position if direction else other <= position
            queries = qkv[direction, 0, rows, :]
            keys = expand(qkv[direction, 1, rows, :])
            values = expand(qkv[direction, 2, rows, :])
            lessen = expand(shrink[direction, rows, :])
            growth = jnp.exp(cumulative[direction, rows, :])
            reached = reach[direction, n]
            key_state = expand(
                (start[direction, n, 0] + reached * entering[direction, 0]).astype(BF16)
            )
            value_state = expand(
                (start[direction, n, 1] + reached * entering[direction, 1]).astype(BF16)
            )
            meeting = jnp.where(seen, nt(queries, keys), 0.0).astype(BF16)
            scores = growth * (nn(meeting, lessen) + nt(queries, key_state))
            powers = jnp.exp(scores - head_max(scores))
            attend = powers / nn(powers.astype(BF16), own)
            weighted = (attend * growth).astype(BF16)
            mixing = jnp.where(seen, nt(weighted, lessen), 0.0).astype(BF16)
            result = nn(mixing, values) + nn(weighted, value_state)
            mean = nn((result * result).astype(BF16), own) * (1.0 / 64.0)
            combined = combined + result * lax.rsqrt(mean + EPSILON) * gain[...]
        out[rows, :] = combined.astype(BF16)


def tail_kernel(
    part0, part1, part2, part3, weight0, weight1, weight2, weight3, tokens, gain, up, down,
    base_out, out1, out2, out3, residual, update,
):
    head = lax.axis_index("head")
    parts = (part0, part1, part2, part3)
    weights = (weight0, weight1, weight2, weight3)
    square = jnp.zeros((ROWS, 1), F32)
    for j in range(4):
        columns = slice(j * 256, (j + 1) * 256)
        total = nn(parts[0][...], weights[0][:, columns])
        for k in range(1, 4):
            total = total + nn(parts[k][...], weights[k][:, columns])
        value = (tokens[j].astype(F32) + total).astype(BF16).astype(F32)
        residual[j] = value
        square = square + jnp.sum(value * value, axis=1, keepdims=True)
    scale = lax.rsqrt(square * (1.0 / 1024.0) + EPSILON)
    entering = jnp.concatenate(
        [(residual[j] * scale * gain[j : j + 1, :]).astype(BF16) for j in range(4)], axis=1
    )
    hidden = jnp.concatenate(
        [
            jax.nn.gelu(nn(entering, up[:, j * 256 : (j + 1) * 256])).astype(BF16)
            for j in range(4)
        ],
        axis=1,
    )
    for j in range(4):
        update[j] = nn(hidden, down[:, j * 256 : (j + 1) * 256])
    base_out[...] = residual[head] + update[head]
    for k, out in ((1, out1), (2, out2), (3, out3)):
        out[...] = update[lax.rem(head + k, 4)].astype(BF16)


def finish_kernel(base, part1, part2, part3, kept_out, sent_out):
    core = lax.axis_index("core")

    def rows_of(which):
        rows = pl.ds(pl.multiple_of(which * 128, 128), 128)
        total = base[rows, :]
        for part in (part1, part2, part3):
            total = total + part[rows, :].astype(F32)
        return total.astype(BF16)

    kept_out[...] = rows_of(core)
    sent_out[...] = rows_of(1 - core)


def kernel(body, outs, scratch=(), flops=0):
    shapes = [jax.ShapeDtypeStruct(shape, dtype) for shape, dtype in outs]
    return pl.pallas_call(
        body,
        out_shape=shapes,
        scratch_shapes=[pltpu.VMEM(shape, dtype) for shape, dtype in scratch],
        compiler_params=pltpu.CompilerParams(vmem_limit_bytes=48 * 1024 * 1024),
        cost_estimate=pl.CostEstimate(flops=flops, bytes_accessed=1 << 20, transcendentals=0),
    )


def shifted(value, k):
    count = lax.axis_size("head")
    return lax.ppermute(value, "head", [(j, (j + k) % count) for j in range(count)])


def local(
    tokens,
    input_norm_gain,
    query_key_value_weight,
    forget_gate_weight,
    convolution_filter_taps,
    slot_forget_rate,
    extra_forget_log,
    head_norm_gain,
    output_projection_weight,
    feedforward_norm_gain,
    up_projection_weight,
    down_projection_weight,
):
    chips = lax.axis_size(CHIPS)
    swap_pairs = [(0, 1), (1, 0)]
    swap, edge_a, edge_b, mine = kernel(
        split_kernel,
        [((136, 256), BF16), ((8, 256), BF16), ((8, 256), BF16), ((128, 256), BF16)],
    )(tokens, extra_forget_log)
    ahead = [(2 * i - 1, 2 * i) for i in range(1, chips)]
    behind = [(2 * i + 2, 2 * i + 1) for i in range(chips - 1)]
    other = lax.ppermute(swap, "core", swap_pairs)
    halo_a = lax.ppermute(edge_a, SEQ, ahead + behind)
    halo_b = lax.ppermute(
        edge_b,
        SEQ,
        [(2 * i - 1, 2 * i + 1) for i in range(1, chips)]
        + [(2 * i + 2, 2 * i) for i in range(chips - 1)],
    )
    rows = jnp.concatenate([mine, other[:128], halo_a, halo_b], axis=0)
    parts = [rows] + [shifted(rows, k) for k in (1, 2, 3)]
    qkv, cumulative, shrink, start, reach, pieces, whole_tokens = kernel(
        front_kernel,
        [
            ((2, 3, ROWS, LANES), BF16),
            ((2, ROWS, LANES), F32),
            ((2, ROWS, LANES), BF16),
            ((2, SPANS, 2, SPAN, LANES), F32),
            ((2, SPANS, SPAN, LANES), F32),
            ((32, 24, 128), BF16),
            ((4, ROWS, 256), BF16),
        ],
        [((ROWS + 16, 768), F32), ((ROWS, LANES), F32)],
        10**9,
    )(
        *parts,
        input_norm_gain.reshape(4, 256),
        jnp.transpose(query_key_value_weight, (1, 0, 2)),
        forget_gate_weight,
        jnp.transpose(convolution_filter_taps, (0, 2, 1, 3)),
        slot_forget_rate.reshape(1, LANES),
        extra_forget_log,
        other[128:],
    )
    pieces, out_weight = lax.optimization_barrier((pieces, output_projection_weight))
    out_weights = [out_weight] + [shifted(out_weight, k) for k in (1, 2, 3)]
    held = lax.all_to_all(pieces, CHIPS, split_axis=0, concat_axis=0, tiled=True)
    (prefixes,) = kernel(
        scan_kernel, [((chips, 16, 128), BF16)], [((chips, 16, 128), F32)]
    )(held)
    arrived = lax.all_to_all(prefixes, CHIPS, split_axis=0, concat_axis=0, tiled=True)
    (attention,) = kernel(
        attention_kernel,
        [((ROWS, LANES), BF16)],
        [((2, 2, SPAN, LANES), F32)],
        10**9,
    )(
        qkv, cumulative, shrink, start, reach, arrived, head_norm_gain.reshape(1, LANES)
    )
    attended = [attention] + [shifted(attention, k) for k in (1, 2, 3)]
    base, out1, out2, out3 = kernel(
        tail_kernel,
        [((ROWS, 256), F32)] + [((ROWS, 256), BF16)] * 3,
        [((4, ROWS, 256), F32), ((4, ROWS, 256), F32)],
        2 * 10**9,
    )(
        *attended,
        *out_weights,
        whole_tokens,
        feedforward_norm_gain.reshape(4, 256),
        up_projection_weight,
        down_projection_weight,
    )
    kept, sent = kernel(
        finish_kernel, [((128, 256), BF16), ((128, 256), BF16)]
    )(base, shifted(out1, 1), shifted(out2, 2), shifted(out3, 3))
    returned = lax.ppermute(sent, "core", swap_pairs)
    first = lax.axis_index("core") == 0
    return jnp.stack([jnp.where(first, kept, returned), jnp.where(first, returned, kept)])


def solution(mesh):
    split = Mesh(
        mesh.devices.reshape(4, 8, 2, mesh.shape["head"]), ("x", "z", "core", "head")
    )
    placed = (
        P(None, SEQ, "head"),
        P(),
        P(None, None, "head"),
        P(None, "head"),
        P(None, None, None, "head"),
        P("head", None),
        P(None, SEQ),
        P("head", None),
        P("head", None),
        P(),
        P(None, "head"),
        P("head", None),
    )
    return jax.shard_map(
        local, mesh=split, in_specs=placed, out_specs=P(None, SEQ, "head"), check_vma=False
    )
```

time: 353 us -> 112 us (0.32)
  the two profiles are of different devices: /device:TPU:2 before, /device:TPU:1 now
where the time goes in v1:
time: 112 us; the launch traced here: 111 us
  starting transfers between devices  49.3 us (44%)
  waiting for transfers between devices  26.8 us (24%)
  local copies, waits for them, and re-layouts  17 us (15%)
  Pallas kernels  16.9 us (15%)
    ppermute x12, starting transfers between devices, shifted(): lax.ppermute(value, 'head', [(j, (j + k) % count) for j in range(count)])  17.2 us
    unnamed x42, local copies, waits for them, and re-layouts  15.5 us
    all_to_all x1, starting transfers between devices, local(): lax.all_to_all(pieces, CHIPS, split_axis=0, concat_axis=0, tiled=True)  11.7 us
    ppermute x12, waiting for transfers between devices, shifted(): lax.ppermute(value, 'head', [(j, (j + k) % count) for j in range(count)])  10.6 us
    all_to_all x1, waiting for transfers between devices, local(): lax.all_to_all(prefixes, CHIPS, split_axis=0, concat_axis=0, tiled=True)  8.88 us
    ppermute x1, starting transfers between devices, local(): returned = lax.ppermute(sent, 'core', swap_pairs)  6.15 us
    pallas_call x1, Pallas kernels, local(): kernel(front_kernel, [((2, 3, ROWS, LANES), BF16), ((2, ROWS, LANES), F32...  5.94 us
    all_to_all x1, waiting for transfers between devices, local(): lax.all_to_all(pieces, CHIPS, split_axis=0, concat_axis=0, tiled=True)  5.72 us
  transfers between devices with their start and end apart: 18, of which 11 were waited for; matrix products, arithmetic and copies ran while one was open for 1% of the time, Pallas kernels for 6%

profile of v1, /device:TPU:1, one launch (start us, length us, event | category | flops | bytes accessed | tf_op | source)
XLA Modules:
  0.0 110.8 jit_solution(2334105971824050522)
XLA Ops:
  0.0 0.9 copy-done
  0.9 0.7 copy-done.1
  1.6 3.3 %collective-permute-start = (bf16[136,256]{1,0:T(8,128)(2,1)S(1)}, bf16[136,256]{1,0:T(8,128)(2,1)S(1)}, u32[]{:S(2)}, u32[]{:S(2)}) collective-permute-start(bf16[136,256]{1,0:T(8,128)(2,1)S(1)} %get-tuple-element.25), channel_id=1, source_target_pairs={{0,4},{4,0},{1,5},{5,1},{2,6},{6,2},{3,7},{7,3},{8,12},{12,8},{9,1... | collective-permute-start | bytes 208904 | tf_op jit(solution)/shard_map/ppermute | solution.py:360
  4.9 1.9 %collective-permute-start.1 = (bf16[8,256]{1,0:T(8,128)(2,1)S(1)}, bf16[8,256]{1,0:T(8,128)(2,1)S(1)}, u32[]{:S(2)}, u32[]{:S(2)}) collective-permute-start(bf16[8,256]{1,0:T(8,128)(2,1)S(1)} %get-tuple-element.26), channel_id=1, source_target_pairs={{4,8},{12,16},{20,24},{28,32},{36,40},{44,48},{52,56},{60,64},{68,... | collective-permute-start | bytes 12296 | tf_op jit(solution)/shard_map/ppermute | solution.py:361
  6.8 3.4 %collective-permute-start.2 = (bf16[8,256]{1,0:T(8,128)(2,1)S(1)}, bf16[8,256]{1,0:T(8,128)(2,1)S(1)}, u32[]{:S(2)}, u32[]{:S(2)}) collective-permute-start(bf16[8,256]{1,0:T(8,128)(2,1)S(1)} %get-tuple-element.27), channel_id=1, source_target_pairs={{4,12},{12,20},{20,28},{28,36},{36,44},{44,52},{52,60},{60,68},{68... | collective-permute-start | bytes 12296 | tf_op jit(solution)/shard_map/ppermute | solution.py:362
  10.2 0.0 collective-permute-done
  10.2 0.0 collective-permute-done.1
  10.2 0.7 collective-permute-done.2
  10.9 1.4 %collective-permute-start.3 = (bf16[272,256]{1,0:T(8,128)(2,1)S(1)}, bf16[272,256]{1,0:T(8,128)(2,1)S(1)}, u32[]{:S(2)}, u32[]{:S(2)}) collective-permute-start(bf16[272,256]{1,0:T(8,128)(2,1)S(1)} %pad_maximum_fusion.part0), channel_id=1, source_target_pairs={{0,1},{1,2},{2,3},{3,0},{4,5},{5,6},{6,7},{7,4},{8,9},{9,10},{10,1... | collective-permute-start | bytes 417800 | tf_op jit(solution)/shard_map/ppermute | solution.py:335
  12.3 2.6 %collective-permute-start.4 = (bf16[272,256]{1,0:T(8,128)(2,1)S(1)}, bf16[272,256]{1,0:T(8,128)(2,1)S(1)}, u32[]{:S(2)}, u32[]{:S(2)}) collective-permute-start(bf16[272,256]{1,0:T(8,128)(2,1)S(1)} %pad_maximum_fusion.part0), channel_id=1, source_target_pairs={{0,2},{1,3},{2,0},{3,1},{4,6},{5,7},{6,4},{7,5},{8,10},{9,11},{10,... | collective-permute-start | bytes 417800 | tf_op jit(solution)/shard_map/ppermute | solution.py:335
  14.9 1.1 collective-permute-start.5
  16.0 0.7 reshape.12.gain
  16.7 0.8 reshape.13.rate
  17.5 0.0 collective-permute-done.3.part1
  17.5 4.4 %collective-permute-done.4.part2 = bf16[272,256]{1,0:T(8,128)(2,1)S(1)} collective-permute-done((bf16[272,256]{1,0:T(8,128)(2,1)S(1)}, bf16[272,256]{1,0:T(8,128)(2,1)S(1)}, u32[]{:S(2)}, u32[]{:S(2)}) %collective-permute-start.4) | collective-permute-done | bytes 139296 | tf_op jit(solution)/shard_map/ppermute | solution.py:335
  21.9 0.0 collective-permute-done.5.part3
  21.9 0.7 copy-done.2
  22.6 1.0 copy-done.4
  23.6 0.7 copy-done.6
  24.4 5.9 %shard_map.119 = (bf16[2,3,256,256]{3,2,1,0:T(8,128)(2,1)S(1)}, f32[2,256,256]{2,1,0:T(8,128)S(1)}, bf16[2,256,256]{2,1,0:T(8,128)(2,1)S(1)}, f32[2,4,2,64,256]{...) custom-call(bf16[272,256]{1,0:T(8,128)(2,1)S(1)} %pad_maximum_fusion, ...), custom_call_target="tpu_custom_call" | custom-call | flops 1000000000 | bytes 1048576 | tf_op jit(solution)/shard_map/pallas_call | solution.py:370
  30.3 0.8 copy-done.7
  31.1 1.0 copy-done.9
  32.1 0.9 copy-done.11
  33.0 0.8 copy-done.13
  33.8 0.8 copy-done.15
  34.6 0.7 copy-done.17
  35.3 11.7 %all-to-all-start = ((bf16[32,24,128]{2,1,0:T(8,128)(2,1)}), bf16[32,24,128]{2,1,0:T(8,128)(2,1)S(1)}, u32[]{:S(2)}, u32[]{:S(2)}) async-start(bf16[32,24,128]{2,1,0:T(8,128)(2,1)} %get-tuple-element.34), calls=%async_computation | async-start | bytes 393216 | tf_op jit(solution)/shard_map/all_to_all | solution.py:395
  47.0 0.0 copy-done.5
  47.0 0.0 copy-start.3
  47.1 2.2 %collective-permute-start.10 = (bf16[256,1024]{1,0:T(8,128)(2,1)S(1)}, bf16[256,1024]{1,0:T(8,128)(2,1)S(1)}, u32[]{:S(2)}, u32[]{:S(2)}) collective-permute-start(bf16[256,1024]{1,0:T(8,128)(2,1)S(1)} %copy-done.5), channel_id=1, source_target_pairs={{0,2},{1,3},{2,0},{3,1},{4,6},{5,7},{6,4},{7,5},{8,10},{9,11},{10,... | collective-permute-start | bytes 1572872 | tf_op jit(solution)/shard_map/ppermute | solution.py:335
  49.2 0.9 collective-permute-start.11
  50.2 0.5 collective-permute-start.9
  50.7 5.7 %all-to-all-done.pieces = bf16[32,24,128]{2,1,0:T(8,128)(2,1)S(1)} async-done(((bf16[32,24,128]{2,1,0:T(8,128)(2,1)}), bf16[32,24,128]{2,1,0:T(8,128)(2,1)S(1)}, u32[]{:S(2)}, u32[]{:S(2)}) %all-to-all-start) | async-done | bytes 196640 | tf_op jit(solution)/shard_map/all_to_all | solution.py:395
  56.4 0.8 shard_map.120
  57.2 5.6 %all-to-all-start.1 = ((bf16[32,16,128]{2,1,0:T(8,128)(2,1)}), bf16[32,16,128]{2,1,0:T(8,128)(2,1)S(1)}, u32[]{:S(2)}, u32[]{:S(2)}) async-start(bf16[32,16,128]{2,1,0:T(8,128)(2,1)} %shard_map.120), calls=%async_computation.1 | async-start | bytes 262144 | tf_op jit(solution)/shard_map/all_to_all | solution.py:399
  62.9 0.1 reshape.14.gain
  63.0 8.9 %all-to-all-done.1.arrived = bf16[32,16,128]{2,1,0:T(8,128)(2,1)S(1)} async-done(((bf16[32,16,128]{2,1,0:T(8,128)(2,1)}), bf16[32,16,128]{2,1,0:T(8,128)(2,1)S(1)}, u32[]{:S(2)}, u32[]{:S(2)}) %all-to-all-start.1) | async-done | bytes 131104 | tf_op jit(solution)/shard_map/all_to_all | solution.py:399
  71.8 1.2 %copy-done.10 = f32[2,4,2,64,256]{4,3,2,1,0:T(8,128)S(1)} copy-done((f32[2,4,2,64,256]{4,3,2,1,0:T(8,128)S(1)}, f32[2,4,2,64,256]{4,3,2,1,0:T(8,128)}, u32[]{:S(2)}) %copy-start.10) | copy-done | bytes 1048600
  73.1 1.1 %copy-done.12 = bf16[2,3,256,256]{3,2,1,0:T(8,128)(2,1)S(1)} copy-done((bf16[2,3,256,256]{3,2,1,0:T(8,128)(2,1)S(1)}, bf16[2,3,256,256]{3,2,1,0:T(8,128)(2,1)}, u32[]{:S(2)}) %copy-start.12) | copy-done | bytes 786456
  74.2 1.0 copy-done.14
  75.3 1.0 copy-done.16
  76.3 0.9 copy-done.18
  77.2 5.7 %shard_map.121.part0 = bf16[256,256]{1,0:T(8,128)(2,1)S(1)} custom-call(bf16[2,3,256,256]{3,2,1,0:T(8,128)(2,1)S(1)} %copy-done.12, f32[2,256,256]{2,1,0:T(8,128)S(1)} %copy-done.14, bf16[2,256,256]{2,1,0:T(8,128)(2,1)S(1)} %copy-done.18, f32[2,4,2,64,256]{4,3,2,1,0:T(8,128)S(1)} %copy-done.10, f32[2,4,64,256]{3,2,1,0:T(8,128)S(1)} %copy-done.16, ...), custom_call_target="tpu_custom_call" | custom-call | flops 1000000000 | bytes 1048576 | tf_op jit(solution)/shard_map/pallas_call | solution.py:400
  82.9 0.7 collective-permute-start.6
  83.6 2.4 %collective-permute-start.7 = (bf16[256,256]{1,0:T(8,128)(2,1)S(1)}, bf16[256,256]{1,0:T(8,128)(2,1)}, u32[]{:S(2)}, u32[]{:S(2)}) collective-permute-start(bf16[256,256]{1,0:T(8,128)(2,1)S(1)} %shard_map.121.part0), channel_id=1, source_target_pairs={{0,2},{1,3},{2,0},{3,1},{4,6},{5,7},{6,4},{7,5},{8,10},{9,11},{10,... | collective-permute-start | bytes 393224 | tf_op jit(solution)/shard_map/ppermute | solution.py:335
  86.1 0.0 collective-permute-done.10.weight2
  86.1 1.1 collective-permute-start.8
  87.2 0.0 collective-permute-done.11.weight3
  87.2 0.0 collective-permute-done.9.weight1
  87.2 0.8 collective-permute-done.6.part1
  88.0 1.9 %collective-permute-done.7.part2 = bf16[256,256]{1,0:T(8,128)(2,1)} collective-permute-done((bf16[256,256]{1,0:T(8,128)(2,1)S(1)}, bf16[256,256]{1,0:T(8,128)(2,1)}, u32[]{:S(2)}, u32[]{:S(2)}) %collective-permute-start.7) | collective-permute-done | bytes 131104 | tf_op jit(solution)/shard_map/ppermute | solution.py:335
  89.9 0.4 collective-permute-done.8.part3
  90.3 1.0 copy-done.8
  91.3 4.4 %shard_map.122 = (f32[256,256]{1,0:T(8,128)S(1)}, bf16[256,256]{1,0:T(8,128)(2,1)S(1)}, bf16[256,256]{1,0:T(8,128)(2,1)S(1)}, bf16[256,256]{1,0:T(8,128)(2,1)S(1)}) custom-call(bf16[256,256]{1,0:T(8,128)(2,1)S(1)} %shard_map.121.part0, bf16[256,256]{1,0:T(8,128)(2,1)S(1)} %collective-permute-done.6.part1, bf16[256,256]{1,0:T(8,128)(2,1)} %collective-permute-done.7.part2, ...), custom_call_target="tpu_custom_call" | custom-call | flops 2000000000 | bytes 1048576 | tf_op jit(solution)/shard_map/pallas_call | solution.py:409
  95.7 1.4 %collective-permute-start.12 = (bf16[256,256]{1,0:T(8,128)(2,1)S(1)}, bf16[256,256]{1,0:T(8,128)(2,1)S(1)}, u32[]{:S(2)}, u32[]{:S(2)}) collective-permute-start(bf16[256,256]{1,0:T(8,128)(2,1)S(1)} %get-tuple-element.38), channel_id=1, source_target_pairs={{0,1},{1,2},{2,3},{3,0},{4,5},{5,6},{6,7},{7,4},{8,9},{9,10},{10,1... | collective-permute-start | bytes 393224 | tf_op jit(solution)/shard_map/ppermute | solution.py:335
  97.1 2.1 %collective-permute-start.13 = (bf16[256,256]{1,0:T(8,128)(2,1)S(1)}, bf16[256,256]{1,0:T(8,128)(2,1)S(1)}, u32[]{:S(2)}, u32[]{:S(2)}) collective-permute-start(bf16[256,256]{1,0:T(8,128)(2,1)S(1)} %get-tuple-element.39), channel_id=1, source_target_pairs={{0,2},{1,3},{2,0},{3,1},{4,6},{5,7},{6,4},{7,5},{8,10},{9,11},{10,... | collective-permute-start | bytes 393224 | tf_op jit(solution)/shard_map/ppermute | solution.py:335
  99.2 0.8 collective-permute-start.14
  100.0 0.8 collective-permute-done.12.part1
  100.8 2.1 %collective-permute-done.13.part2 = bf16[256,256]{1,0:T(8,128)(2,1)S(1)} collective-permute-done((bf16[256,256]{1,0:T(8,128)(2,1)S(1)}, bf16[256,256]{1,0:T(8,128)(2,1)S(1)}, u32[]{:S(2)}, u32[]{:S(2)}) %collective-permute-start.13) | collective-permute-done | bytes 131104 | tf_op jit(solution)/shard_map/ppermute | solution.py:335
  102.9 0.1 collective-permute-done.14.part3
  103.0 0.1 shard_map.123
  103.1 6.2 %collective-permute-start.15 = (bf16[128,256]{1,0:T(8,128)(2,1)S(1)}, bf16[128,256]{1,0:T(8,128)(2,1)S(1)}, u32[]{:S(2)}, u32[]{:S(2)}) collective-permute-start(bf16[128,256]{1,0:T(8,128)(2,1)S(1)} %get-tuple-element.42), channel_id=1, source_target_pairs={{0,4},{4,0},{1,5},{5,1},{2,6},{6,2},{3,7},{7,3},{8,12},{12,8},{9,1... | collective-permute-start | bytes 196616 | tf_op jit(solution)/shard_map/ppermute | solution.py:425
  109.2 0.9 collective-permute-done.15
  110.1 0.7 pad_maximum_fusion.1
  (29 shorter events, 0.1 us)
Async XLA Ops:
  0.0 0.9 copy-start
  0.9 0.7 copy-start.1
  1.6 8.6 %collective-permute-start = (bf16[136,256]{1,0:T(8,128)(2,1)S(1)}, bf16[136,256]{1,0:T(8,128)(2,1)S(1)}, u32[]{:S(2)}, u32[]{:S(2)}) collective-permute-start(bf16[136,256]{1,0:T(8,128)(2,1)S(1)} %get-tuple-element.25), channel_id=1, source_target_pairs={{0,4},{4,0},{1,5},{5,1},{2,6},{6,2},{3,7},{7,3},{8,12},{12,8},{9,1... | collective-permute-start | bytes 208904 | tf_op jit(solution)/shard_map/ppermute | solution.py:360
  4.9 5.3 %collective-permute-start.1 = (bf16[8,256]{1,0:T(8,128)(2,1)S(1)}, bf16[8,256]{1,0:T(8,128)(2,1)S(1)}, u32[]{:S(2)}, u32[]{:S(2)}) collective-permute-start(bf16[8,256]{1,0:T(8,128)(2,1)S(1)} %get-tuple-element.26), channel_id=1, source_target_pairs={{4,8},{12,16},{20,24},{28,32},{36,40},{44,48},{52,56},{60,64},{68,... | collective-permute-start | bytes 12296 | tf_op jit(solution)/shard_map/ppermute | solution.py:361
  6.8 4.1 %collective-permute-start.2 = (bf16[8,256]{1,0:T(8,128)(2,1)S(1)}, bf16[8,256]{1,0:T(8,128)(2,1)S(1)}, u32[]{:S(2)}, u32[]{:S(2)}) collective-permute-start(bf16[8,256]{1,0:T(8,128)(2,1)S(1)} %get-tuple-element.27), channel_id=1, source_target_pairs={{4,12},{12,20},{20,28},{28,36},{36,44},{44,52},{52,60},{60,68},{68... | collective-permute-start | bytes 12296 | tf_op jit(solution)/shard_map/ppermute | solution.py:362
  10.9 6.5 %collective-permute-start.3 = (bf16[272,256]{1,0:T(8,128)(2,1)S(1)}, bf16[272,256]{1,0:T(8,128)(2,1)S(1)}, u32[]{:S(2)}, u32[]{:S(2)}) collective-permute-start(bf16[272,256]{1,0:T(8,128)(2,1)S(1)} %pad_maximum_fusion.part0), channel_id=1, source_target_pairs={{0,1},{1,2},{2,3},{3,0},{4,5},{5,6},{6,7},{7,4},{8,9},{9,10},{10,1... | collective-permute-start | bytes 417800 | tf_op jit(solution)/shard_map/ppermute | solution.py:335
  12.3 9.6 %collective-permute-start.4 = (bf16[272,256]{1,0:T(8,128)(2,1)S(1)}, bf16[272,256]{1,0:T(8,128)(2,1)S(1)}, u32[]{:S(2)}, u32[]{:S(2)}) collective-permute-start(bf16[272,256]{1,0:T(8,128)(2,1)S(1)} %pad_maximum_fusion.part0), channel_id=1, source_target_pairs={{0,2},{1,3},{2,0},{3,1},{4,6},{5,7},{6,4},{7,5},{8,10},{9,11},{10,... | collective-permute-start | bytes 417800 | tf_op jit(solution)/shard_map/ppermute | solution.py:335
  14.9 7.0 %collective-permute-start.5 = (bf16[272,256]{1,0:T(8,128)(2,1)S(1)}, bf16[272,256]{1,0:T(8,128)(2,1)S(1)}, u32[]{:S(2)}, u32[]{:S(2)}) collective-permute-start(bf16[272,256]{1,0:T(8,128)(2,1)S(1)} %pad_maximum_fusion.part0), channel_id=1, source_target_pairs={{0,3},{1,0},{2,1},{3,2},{4,7},{5,4},{6,5},{7,6},{8,11},{9,8},{10,9... | collective-permute-start | bytes 417800 | tf_op jit(solution)/shard_map/ppermute | solution.py:335
  21.9 0.7 copy-start.2
  22.6 1.0 copy-start.4
  23.6 0.7 copy-start.6
  24.4 22.7 %copy-start.5 = (bf16[256,1024]{1,0:T(8,128)(2,1)S(1)}, bf16[256,1024]{1,0:T(8,128)(2,1)}, u32[]{:S(2)}) copy-start(bf16[256,1024]{1,0:T(8,128)(2,1)} %weight0) | copy-start | bytes 1572868
  24.4 38.5 %copy-start.20 = (f32[4,64]{1,0:T(4,128)S(1)}, f32[4,64]{1,0:T(4,128)}, u32[]{:S(2)}) copy-start(f32[4,64]{1,0:T(4,128)} %param.19) | copy-start | bytes 3076
  30.3 0.8 copy-start.7
  31.1 1.0 copy-start.9
  32.1 0.9 copy-start.11
  33.0 0.8 copy-start.13
  33.8 0.8 copy-start.15
  34.6 0.7 copy-start.17
  35.3 51.9 %copy-start.19 = (f32[1024]{0:T(1024)S(1)}, f32[1024]{0:T(1024)}, u32[]{:S(2)}) copy-start(f32[1024]{0:T(1024)} %param.21) | copy-start | bytes 12292
  35.3 21.1 %all-to-all-start = ((bf16[32,24,128]{2,1,0:T(8,128)(2,1)}), bf16[32,24,128]{2,1,0:T(8,128)(2,1)S(1)}, u32[]{:S(2)}, u32[]{:S(2)}) async-start(bf16[32,24,128]{2,1,0:T(8,128)(2,1)} %get-tuple-element.34), calls=%async_computation | async-start | bytes 393216 | tf_op jit(solution)/shard_map/all_to_all | solution.py:395
  47.0 43.2 %copy-start.3 = (bf16[1024,1024]{1,0:T(8,128)(2,1)S(1)}, bf16[1024,1024]{1,0:T(8,128)(2,1)}, u32[]{:S(2)}) copy-start(bf16[1024,1024]{1,0:T(8,128)(2,1)} %up.1) | copy-start | bytes 6291460
  47.1 39.0 %collective-permute-start.10 = (bf16[256,1024]{1,0:T(8,128)(2,1)S(1)}, bf16[256,1024]{1,0:T(8,128)(2,1)S(1)}, u32[]{:S(2)}, u32[]{:S(2)}) collective-permute-start(bf16[256,1024]{1,0:T(8,128)(2,1)S(1)} %copy-done.5), channel_id=1, source_target_pairs={{0,2},{1,3},{2,0},{3,1},{4,6},{5,7},{6,4},{7,5},{8,10},{9,11},{10,... | collective-permute-start | bytes 1572872 | tf_op jit(solution)/shard_map/ppermute | solution.py:335
  49.2 37.9 %collective-permute-start.11 = (bf16[256,1024]{1,0:T(8,128)(2,1)S(1)}, bf16[256,1024]{1,0:T(8,128)(2,1)}, u32[]{:S(2)}, u32[]{:S(2)}) collective-permute-start(bf16[256,1024]{1,0:T(8,128)(2,1)S(1)} %copy-done.5), channel_id=1, source_target_pairs={{0,3},{1,0},{2,1},{3,2},{4,7},{5,4},{6,5},{7,6},{8,11},{9,8},{10,9... | collective-permute-start | bytes 1572872 | tf_op jit(solution)/shard_map/ppermute | solution.py:335
  50.2 37.0 %collective-permute-start.9 = (bf16[256,1024]{1,0:T(8,128)(2,1)S(1)}, bf16[256,1024]{1,0:T(8,128)(2,1)}, u32[]{:S(2)}, u32[]{:S(2)}) collective-permute-start(bf16[256,1024]{1,0:T(8,128)(2,1)S(1)} %copy-done.5), channel_id=1, source_target_pairs={{0,1},{1,2},{2,3},{3,0},{4,5},{5,6},{6,7},{7,4},{8,9},{9,10},{10,1... | collective-permute-start | bytes 1572872 | tf_op jit(solution)/shard_map/ppermute | solution.py:335
  57.2 14.6 %all-to-all-start.1 = ((bf16[32,16,128]{2,1,0:T(8,128)(2,1)}), bf16[32,16,128]{2,1,0:T(8,128)(2,1)S(1)}, u32[]{:S(2)}, u32[]{:S(2)}) async-start(bf16[32,16,128]{2,1,0:T(8,128)(2,1)} %shard_map.120), calls=%async_computation.1 | async-start | bytes 262144 | tf_op jit(solution)/shard_map/all_to_all | solution.py:399
  71.8 1.2 %copy-start.10 = (f32[2,4,2,64,256]{4,3,2,1,0:T(8,128)S(1)}, f32[2,4,2,64,256]{4,3,2,1,0:T(8,128)}, u32[]{:S(2)}) copy-start(f32[2,4,2,64,256]{4,3,2,1,0:T(8,128)} %copy-done.9) | copy-start | bytes 3145732
  73.1 1.1 %copy-start.12 = (bf16[2,3,256,256]{3,2,1,0:T(8,128)(2,1)S(1)}, bf16[2,3,256,256]{3,2,1,0:T(8,128)(2,1)}, u32[]{:S(2)}) copy-start(bf16[2,3,256,256]{3,2,1,0:T(8,128)(2,1)} %copy-done.11) | copy-start | bytes 2359300
  74.2 1.0 copy-start.14
  75.2 1.0 copy-start.16
  76.3 0.9 copy-start.18
  82.9 5.1 %collective-permute-start.6 = (bf16[256,256]{1,0:T(8,128)(2,1)S(1)}, bf16[256,256]{1,0:T(8,128)(2,1)S(1)}, u32[]{:S(2)}, u32[]{:S(2)}) collective-permute-start(bf16[256,256]{1,0:T(8,128)(2,1)S(1)} %shard_map.121.part0), channel_id=1, source_target_pairs={{0,1},{1,2},{2,3},{3,0},{4,5},{5,6},{6,7},{7,4},{8,9},{9,10},{10,1... | collective-permute-start | bytes 393224 | tf_op jit(solution)/shard_map/ppermute | solution.py:335
  83.6 6.3 %collective-permute-start.7 = (bf16[256,256]{1,0:T(8,128)(2,1)S(1)}, bf16[256,256]{1,0:T(8,128)(2,1)}, u32[]{:S(2)}, u32[]{:S(2)}) collective-permute-start(bf16[256,256]{1,0:T(8,128)(2,1)S(1)} %shard_map.121.part0), channel_id=1, source_target_pairs={{0,2},{1,3},{2,0},{3,1},{4,6},{5,7},{6,4},{7,5},{8,10},{9,11},{10,... | collective-permute-start | bytes 393224 | tf_op jit(solution)/shard_map/ppermute | solution.py:335
  86.1 4.2 %collective-permute-start.8 = (bf16[256,256]{1,0:T(8,128)(2,1)S(1)}, bf16[256,256]{1,0:T(8,128)(2,1)}, u32[]{:S(2)}, u32[]{:S(2)}) collective-permute-start(bf16[256,256]{1,0:T(8,128)(2,1)S(1)} %shard_map.121.part0), channel_id=1, source_target_pairs={{0,3},{1,0},{2,1},{3,2},{4,7},{5,4},{6,5},{7,6},{8,11},{9,8},{10,9... | collective-permute-start | bytes 393224 | tf_op jit(solution)/shard_map/ppermute | solution.py:335
  90.3 1.0 copy-start.8
  95.7 5.1 %collective-permute-start.12 = (bf16[256,256]{1,0:T(8,128)(2,1)S(1)}, bf16[256,256]{1,0:T(8,128)(2,1)S(1)}, u32[]{:S(2)}, u32[]{:S(2)}) collective-permute-start(bf16[256,256]{1,0:T(8,128)(2,1)S(1)} %get-tuple-element.38), channel_id=1, source_target_pairs={{0,1},{1,2},{2,3},{3,0},{4,5},{5,6},{6,7},{7,4},{8,9},{9,10},{10,1... | collective-permute-start | bytes 393224 | tf_op jit(solution)/shard_map/ppermute | solution.py:335
  97.1 5.9 %collective-permute-start.13 = (bf16[256,256]{1,0:T(8,128)(2,1)S(1)}, bf16[256,256]{1,0:T(8,128)(2,1)S(1)}, u32[]{:S(2)}, u32[]{:S(2)}) collective-permute-start(bf16[256,256]{1,0:T(8,128)(2,1)S(1)} %get-tuple-element.39), channel_id=1, source_target_pairs={{0,2},{1,3},{2,0},{3,1},{4,6},{5,7},{6,4},{7,5},{8,10},{9,11},{10,... | collective-permute-start | bytes 393224 | tf_op jit(solution)/shard_map/ppermute | solution.py:335
  99.2 3.8 %collective-permute-start.14 = (bf16[256,256]{1,0:T(8,128)(2,1)S(1)}, bf16[256,256]{1,0:T(8,128)(2,1)S(1)}, u32[]{:S(2)}, u32[]{:S(2)}) collective-permute-start(bf16[256,256]{1,0:T(8,128)(2,1)S(1)} %get-tuple-element.40), channel_id=1, source_target_pairs={{0,3},{1,0},{2,1},{3,2},{4,7},{5,4},{6,5},{7,6},{8,11},{9,8},{10,9... | collective-permute-start | bytes 393224 | tf_op jit(solution)/shard_map/ppermute | solution.py:335
  103.1 7.1 %collective-permute-start.15 = (bf16[128,256]{1,0:T(8,128)(2,1)S(1)}, bf16[128,256]{1,0:T(8,128)(2,1)S(1)}, u32[]{:S(2)}, u32[]{:S(2)}) collective-permute-start(bf16[128,256]{1,0:T(8,128)(2,1)S(1)} %get-tuple-element.42), channel_id=1, source_target_pairs={{0,4},{4,0},{1,5},{5,1},{2,6},{6,2},{3,7},{7,3},{8,12},{12,8},{9,1... | collective-permute-start | bytes 196616 | tf_op jit(solution)/shard_map/ppermute | solution.py:425

commit v2 on v1

--- a/solution.py
+++ b/solution.py
@@ -68,8 +68,40 @@
     return jnp.sum(picked, axis=1, keepdims=True)
 
 
-def split_kernel(tokens, extra, swap_out, a_out, b_out, mine_out):
+def begin(pairs, semaphores):
+    copies = [
+        pltpu.make_async_copy(source, target, semaphores.at[k])
+        for k, (source, target) in enumerate(pairs)
+    ]
+    for copy in copies:
+        copy.start()
+    return copies
+
+
+def finish(copies):
+    for copy in copies:
+        copy.wait()
+
+
+def in_lanes(heads):
+    return jnp.concatenate([heads[h : h + 1, :] for h in range(4)], axis=1)
+
+
+def gain_of(gain, source):
+    return jnp.concatenate(
+        [gain[pl.ds(2 * source, 1), :], gain[pl.ds(2 * source + 1, 1), :]], axis=1
+    )
+
+
+def warm_kernel(qkv_weight, gate_weight, qkv_out, gate_out, semaphores):
+    finish(begin([(qkv_weight, qkv_out), (gate_weight, gate_out)], semaphores))
+
+
+def split_kernel(
+    tokens_in, extra_in, swap_out, a_out, b_out, mine_out, tokens, extra, semaphores
+):
     core = lax.axis_index("core")
+    finish(begin([(tokens_in, tokens), (extra_in, extra)], semaphores))
     mine = tokens[core]
     other = tokens[1 - core]
     mine_out[...] = mine
@@ -90,8 +122,8 @@
 
 def front_kernel(
     part0, part1, part2, part3, gain, qkv_weight, gate_weight, taps, rate, extra, extra_other,
-    qkv_out, cum_out, shrink_out, start_out, reach_out, sent_out, tokens_out,
-    padded, decay,
+    sent_out, query_out, kv_out, cum_out, shrink_out, start_out, reach_out, tokens_out,
+    padded, decay, query, kv, cum, shrink, start, reach, tokens, semaphores,
 ):
     core = lax.axis_index("core")
     head = lax.axis_index("head")
@@ -102,13 +134,14 @@
     square = jnp.zeros((ROWS + 16, 1), F32)
     for k in range(4):
         values = parts[k][...]
-        tokens_out[sources[k], pl.ds(own_rows, 128), :] = values[0:128]
-        tokens_out[sources[k], pl.ds(other_rows, 128), :] = values[128:256]
+        tokens[sources[k], pl.ds(own_rows, 128), :] = values[0:128]
+        tokens[sources[k], pl.ds(other_rows, 128), :] = values[128:256]
         wide = values.astype(F32)
         square = square + jnp.sum(wide * wide, axis=1, keepdims=True)
+    going = begin([(tokens, tokens_out)], semaphores.at[pl.ds(0, 1)])
     scale = lax.rsqrt(square * (1.0 / 1024.0) + EPSILON)
     normed = [
-        (parts[k][...].astype(F32) * scale * gain[pl.ds(sources[k], 1), :]).astype(BF16)
+        (parts[k][...].astype(F32) * scale * gain_of(gain, sources[k])).astype(BF16)
         for k in range(4)
     ]
     starts = [pl.multiple_of(source * 256, 256) for source in sources]
@@ -126,26 +159,23 @@
         padded[pl.ds(other_pad, 128), columns] = total[128:256]
         padded[pl.ds(a_pad, 8), columns] = total[256:264]
         padded[pl.ds(b_pad, 8), columns] = total[264:272]
+    query[...] = padded[:, 0:256].astype(BF16)
+    going += begin([(query, query_out)], semaphores.at[pl.ds(1, 1)])
     gate = nn(normed[0], gate_weight[pl.ds(starts[0], 256), :])
     for k in range(1, 4):
         gate = gate + nn(normed[k], gate_weight[pl.ds(starts[k], 256), :])
     own_extra = as_column(extra[pl.ds(core, 1), :])
     sent = extra_other[...].astype(F32)
     other_extra = as_column(sent[0:1, 0:128] + sent[0:1, 128:256] + sent[1:2, 0:128])
-    decays = -2.0 * rate[...] * jax.nn.sigmoid(gate[0:256])
+    decays = -2.0 * in_lanes(rate[...]) * jax.nn.sigmoid(gate[0:256])
     decay[pl.ds(own_rows, 128), :] = decays[0:128] - own_extra
     decay[pl.ds(other_rows, 128), :] = decays[128:256] - other_extra
 
-    for i in range(3):
+    for i in (1, 2):
         columns = slice(i * 256, (i + 1) * 256)
         for direction in range(2):
-            running = taps[direction, i, 0:1, :] * padded[8 : 8 + ROWS, columns]
-            for j in range(1, 4):
-                first = 8 + j if direction else 8 - j
-                running = running + taps[direction, i, j : j + 1, :] * padded[
-                    first : first + ROWS, columns
-                ]
-            qkv_out[direction, i] = (running * jax.nn.sigmoid(running)).astype(BF16)
+            kv[direction, i - 1] = convolved(padded, taps, direction, i, columns)
+    going += begin([(kv, kv_out)], semaphores.at[pl.ds(2, 1)])
 
     log_decay = decay[...]
     inflow = minus_expm1(log_decay)
@@ -154,29 +184,32 @@
     earlier = (same & (col <= row)).astype(F32)
     later = (same & (col >= row)).astype(F32)
     spans = (iota((ROWS, 128 * SPANS), 0) // SPAN == iota((ROWS, 128 * SPANS), 1) // 128).astype(F32)
+    for direction in range(2):
+        cum[direction] = nn(later if direction else earlier, log_decay, HIGHEST)
+        shrink[direction] = (jnp.exp(-cum[direction]) * inflow).astype(BF16)
+    going += begin([(cum, cum_out), (shrink, shrink_out)], semaphores.at[pl.ds(3, 2)])
     span_totals = tn(log_decay, spans, HIGHEST)
     totals = [compact_rows(span_totals[:, n * 128 : (n + 1) * 128]) for n in range(SPANS)]
     factors = [jnp.exp(total) for total in totals]
     ends = []
     for direction in range(2):
-        cumulative = nn(later if direction else earlier, log_decay, HIGHEST)
-        cum_out[direction] = cumulative
-        shrink_out[direction] = (jnp.exp(-cumulative) * inflow).astype(BF16)
+        cumulative = cum[direction]
         states = [jnp.zeros((SPAN, LANES), F32), jnp.zeros((SPAN, LANES), F32)]
         passed = jnp.zeros((SPAN, LANES), F32)
         for n in reversed(range(SPANS)) if direction else range(SPANS):
             rows = slice(n * SPAN, (n + 1) * SPAN)
-            start_out[direction, n, 0] = states[0]
-            start_out[direction, n, 1] = states[1]
-            reach_out[direction, n] = jnp.exp(passed)
+            start[direction, n, 0] = states[0].astype(BF16)
+            start[direction, n, 1] = states[1].astype(BF16)
+            reach[direction, n] = jnp.exp(passed)
             local = cumulative[rows]
             last = local[0:1] if direction else local[SPAN - 1 : SPAN]
             remain = (jnp.exp(last - local) * inflow[rows]).astype(BF16)
             for which in range(2):
-                added = compact(tn(remain, qkv_out[direction, 1 + which, rows, :]))
+                added = compact(tn(remain, kv[direction, which, rows, :]))
                 states[which] = factors[n] * states[which] + added
             passed = passed + totals[n]
         ends.append(states)
+    going += begin([(start, start_out), (reach, reach_out)], semaphores.at[pl.ds(5, 2)])
     factor = jnp.exp(totals[0] + totals[1] + totals[2] + totals[3])
     high = factor.astype(BF16).astype(F32)
     lane = iota((SPAN, LANES), 1)
@@ -194,6 +227,66 @@
                     ],
                     axis=0,
                 ).astype(BF16)
+    finish(going)
+
+
+def convolved(padded, taps, direction, i, columns):
+    running = taps[direction, i, 0:1, :] * padded[8 : 8 + ROWS, columns]
+    for j in range(1, 4):
+        first = 8 + j if direction else 8 - j
+        running = running + taps[direction, i, j : j + 1, :] * padded[first : first + ROWS, columns]
+    return (running * jax.nn.sigmoid(running)).astype(BF16)
+
+
+def own_head():
+    return (iota((LANES, LANES), 0) // 64 == iota((LANES, LANES), 1) // 64).astype(BF16)
+
+
+def expand(values, own):
+    return jnp.concatenate([values] * 4, axis=0) * own
+
+
+def seen_by(direction):
+    position, other = iota((SPAN, LANES), 0), iota((SPAN, LANES), 1) % SPAN
+    return other >= position if direction else other <= position
+
+
+def meeting_kernel(
+    query_in, kv_in, cum_in, shrink_in, start_in, taps,
+    queries_out, scores_out, growth_out,
+    query, keys, cum, shrink, start, padded, queries, scores, growth, semaphores,
+):
+    coming = begin(
+        [
+            (query_in, query),
+            (kv_in.at[:, 0], keys),
+            (cum_in, cum),
+            (shrink_in, shrink),
+            (start_in.at[:, :, 0], start),
+        ],
+        semaphores.at[pl.ds(0, 5)],
+    )
+    coming[0].wait()
+    padded[...] = query[...].astype(F32)
+    for direction in range(2):
+        queries[direction] = convolved(padded, taps, direction, 0, slice(0, 256))
+    going = begin([(queries, queries_out)], semaphores.at[pl.ds(5, 1)])
+    finish(coming[1:])
+    own = own_head()
+    growth[...] = jnp.exp(cum[...])
+    going += begin([(growth, growth_out)], semaphores.at[pl.ds(6, 1)])
+    for n in range(SPANS):
+        rows = slice(n * SPAN, (n + 1) * SPAN)
+        for direction in range(2):
+            asked = queries[direction, rows, :]
+            meeting = nt(asked, expand(keys[direction, rows, :], own))
+            meeting = jnp.where(seen_by(direction), meeting, 0.0).astype(BF16)
+            scores[direction, rows, :] = growth[direction, rows, :] * (
+                nn(meeting, expand(shrink[direction, rows, :], own))
+                + nt(asked, expand(start[direction, n], own))
+            )
+    going += begin([(scores, scores_out)], semaphores.at[pl.ds(7, 1)])
+    finish(going)
 
 
 def scan_kernel(pieces, states_out, wide):
@@ -228,7 +321,28 @@
     return jnp.concatenate(halves, axis=1)
 
 
-def attention_kernel(qkv, cumulative, shrink, start, reach, arrived, gain, out, entering):
+def attention_kernel(
+    queries_in, kv_in, shrink_in, start_in, reach_in, scores_in, growth_in, arrived, gain,
+    out,
+    queries, values, shrink, start, reach, scores, growth, entering, semaphores,
+):
+    coming = []
+    for n in range(SPANS):
+        rows = pl.ds(n * SPAN, SPAN)
+        coming.append(
+            begin(
+                [
+                    (reach_in.at[:, n], reach.at[:, n]),
+                    (queries_in.at[:, rows, :], queries.at[:, rows, :]),
+                    (growth_in.at[:, rows, :], growth.at[:, rows, :]),
+                    (scores_in.at[:, rows, :], scores.at[:, rows, :]),
+                    (shrink_in.at[:, rows, :], shrink.at[:, rows, :]),
+                    (start_in.at[:, n, 1], start.at[:, n]),
+                    (kv_in.at[:, 1, rows, :], values.at[:, rows, :]),
+                ],
+                semaphores.at[pl.ds(7 * n, 7)],
+            )
+        )
     for m in range(32):
         which, half, block = m // 16, (m // 8) % 2, m % 8
         piece = arrived[m].astype(F32)
@@ -236,46 +350,38 @@
             entering[direction, which, block * 8 : block * 8 + 8, half * 128 : half * 128 + 128] = (
                 piece[direction * 8 : direction * 8 + 8]
             )
-    own = (iota((LANES, LANES), 0) // 64 == iota((LANES, LANES), 1) // 64).astype(BF16)
-    position, other = iota((SPAN, LANES), 0), iota((SPAN, LANES), 1) % SPAN
-
-    def expand(values):
-        return jnp.concatenate([values] * 4, axis=0) * own
-
+    own = own_head()
+    gains = in_lanes(gain[...])
     for n in range(SPANS):
+        finish(coming[n])
         rows = slice(n * SPAN, (n + 1) * SPAN)
         combined = jnp.zeros((SPAN, LANES), F32)
         for direction in range(2):
-            seen = other >= position if direction else other <= position
-            queries = qkv[direction, 0, rows, :]
-            keys = expand(qkv[direction, 1, rows, :])
-            values = expand(qkv[direction, 2, rows, :])
-            lessen = expand(shrink[direction, rows, :])
-            growth = jnp.exp(cumulative[direction, rows, :])
+            lessen = expand(shrink[direction, rows, :], own)
             reached = reach[direction, n]
-            key_state = expand(
-                (start[direction, n, 0] + reached * entering[direction, 0]).astype(BF16)
+            grown = growth[direction, rows, :]
+            key_state = expand((reached * entering[direction, 0]).astype(BF16), own)
+            value_state = expand(
+                (start[direction, n].astype(F32) + reached * entering[direction, 1]).astype(BF16),
+                own,
             )
-            value_state = expand(
-                (start[direction, n, 1] + reached * entering[direction, 1]).astype(BF16)
-            )
-            meeting = jnp.where(seen, nt(queries, keys), 0.0).astype(BF16)
-            scores = growth * (nn(meeting, lessen) + nt(queries, key_state))
-            powers = jnp.exp(scores - head_max(scores))
+            total = scores[direction, rows, :] + grown * nt(queries[direction, rows, :], key_state)
+            powers = jnp.exp(total - head_max(total))
             attend = powers / nn(powers.astype(BF16), own)
-            weighted = (attend * growth).astype(BF16)
-            mixing = jnp.where(seen, nt(weighted, lessen), 0.0).astype(BF16)
-            result = nn(mixing, values) + nn(weighted, value_state)
+            weighted = (attend * grown).astype(BF16)
+            mixing = jnp.where(seen_by(direction), nt(weighted, lessen), 0.0).astype(BF16)
+            result = nn(mixing, expand(values[direction, rows, :], own)) + nn(weighted, value_state)
             mean = nn((result * result).astype(BF16), own) * (1.0 / 64.0)
-            combined = combined + result * lax.rsqrt(mean + EPSILON) * gain[...]
+            combined = combined + result * lax.rsqrt(mean + EPSILON) * gains
         out[rows, :] = combined.astype(BF16)
 
 
 def tail_kernel(
-    part0, part1, part2, part3, weight0, weight1, weight2, weight3, tokens, gain, up, down,
-    base_out, out1, out2, out3, residual, update,
+    part0, part1, part2, part3, weight0, weight1, weight2, weight3, tokens_in, gain, up, down_in,
+    base_out, out1, out2, out3, residual, update, tokens, down, semaphores,
 ):
     head = lax.axis_index("head")
+    coming = begin([(tokens_in, tokens), (down_in, down)], semaphores)
     parts = (part0, part1, part2, part3)
     weights = (weight0, weight1, weight2, weight3)
     square = jnp.zeros((ROWS, 1), F32)
@@ -284,12 +390,14 @@
         total = nn(parts[0][...], weights[0][:, columns])
         for k in range(1, 4):
             total = total + nn(parts[k][...], weights[k][:, columns])
+        if j == 0:
+            coming[0].wait()
         value = (tokens[j].astype(F32) + total).astype(BF16).astype(F32)
         residual[j] = value
         square = square + jnp.sum(value * value, axis=1, keepdims=True)
     scale = lax.rsqrt(square * (1.0 / 1024.0) + EPSILON)
     entering = jnp.concatenate(
-        [(residual[j] * scale * gain[j : j + 1, :]).astype(BF16) for j in range(4)], axis=1
+        [(residual[j] * scale * gain_of(gain, j)).astype(BF16) for j in range(4)], axis=1
     )
     hidden = jnp.concatenate(
         [
@@ -298,6 +406,7 @@
         ],
         axis=1,
     )
+    coming[1].wait()
     for j in range(4):
         update[j] = nn(hidden, down[:, j * 256 : (j + 1) * 256])
     base_out[...] = residual[head] + update[head]
@@ -319,15 +428,36 @@
     sent_out[...] = rows_of(1 - core)
 
 
-def kernel(body, outs, scratch=(), flops=0):
-    shapes = [jax.ShapeDtypeStruct(shape, dtype) for shape, dtype in outs]
-    return pl.pallas_call(
+def kernel(body, ins, outs, scratch=(), copies=0, flops=0):
+    spaces = {"h": pltpu.HBM, "v": pltpu.VMEM}
+    places = [pl.BlockSpec(memory_space=spaces[place]) for place in ins]
+    shapes = [
+        pltpu.HBM(out[0], out[1]) if out[2] == "h" else jax.ShapeDtypeStruct(out[0], out[1])
+        for out in outs
+    ]
+    out_places = [pl.BlockSpec(memory_space=spaces[out[2]]) for out in outs]
+    buffers = [pltpu.VMEM(shape, dtype) for shape, dtype in scratch]
+    if copies:
+        buffers.append(pltpu.SemaphoreType.DMA((copies,)))
+    call = pl.pallas_call(
         body,
+        in_specs=places,
+        out_specs=out_places,
         out_shape=shapes,
-        scratch_shapes=[pltpu.VMEM(shape, dtype) for shape, dtype in scratch],
-        compiler_params=pltpu.CompilerParams(vmem_limit_bytes=48 * 1024 * 1024),
+        scratch_shapes=buffers,
+        compiler_params=pltpu.CompilerParams(vmem_limit_bytes=32 * 1024 * 1024),
         cost_estimate=pl.CostEstimate(flops=flops, bytes_accessed=1 << 20, transcendentals=0),
     )
+
+    def placed(*arrays):
+        return call(
+            *[
+                pltpu.with_memory_space_constraint(array, pltpu.HBM) if place == "h" else array
+                for array, place in zip(arrays, ins)
+            ]
+        )
+
+    return placed
 
 
 def shifted(value, k):
@@ -353,7 +483,15 @@
     swap_pairs = [(0, 1), (1, 0)]
     swap, edge_a, edge_b, mine = kernel(
         split_kernel,
-        [((136, 256), BF16), ((8, 256), BF16), ((8, 256), BF16), ((128, 256), BF16)],
+        "hh",
+        [
+            ((136, 256), BF16, "v"),
+            ((8, 256), BF16, "v"),
+            ((8, 256), BF16, "v"),
+            ((128, 256), BF16, "v"),
+        ],
+        [((2, 128, 256), BF16), ((2, 128), F32)],
+        copies=2,
     )(tokens, extra_forget_log)
     ahead = [(2 * i - 1, 2 * i) for i in range(1, chips)]
     behind = [(2 * i + 2, 2 * i + 1) for i in range(chips - 1)]
@@ -366,61 +504,123 @@
         + [(2 * i + 2, 2 * i) for i in range(chips - 1)],
     )
     rows = jnp.concatenate([mine, other[:128], halo_a, halo_b], axis=0)
+    qkv_weight = jnp.transpose(query_key_value_weight, (1, 0, 2))
+    rows, qkv_weight, gate_weight = lax.optimization_barrier(
+        (rows, qkv_weight, forget_gate_weight)
+    )
     parts = [rows] + [shifted(rows, k) for k in (1, 2, 3)]
-    qkv, cumulative, shrink, start, reach, pieces, whole_tokens = kernel(
+    qkv_weight, gate_weight = kernel(
+        warm_kernel,
+        "hh",
+        [((3, 1024, 256), BF16, "v"), ((1024, 256), BF16, "v")],
+        copies=2,
+        flops=10**9,
+    )(qkv_weight, gate_weight)
+    taps = jnp.transpose(convolution_filter_taps, (0, 2, 1, 3))
+    halves = (2, ROWS, LANES)
+    starts = (2, SPANS, 2, SPAN, LANES)
+    reaches = (2, SPANS, SPAN, LANES)
+    pieces, query, kv, cum, shrink, start, reach, whole_tokens = kernel(
         front_kernel,
-        [
-            ((2, 3, ROWS, LANES), BF16),
-            ((2, ROWS, LANES), F32),
-            ((2, ROWS, LANES), BF16),
-            ((2, SPANS, 2, SPAN, LANES), F32),
-            ((2, SPANS, SPAN, LANES), F32),
-            ((32, 24, 128), BF16),
+        "v" * 11,
+        [
+            ((32, 24, 128), BF16, "v"),
+            ((ROWS + 16, 256), BF16, "h"),
+            ((2, 2, ROWS, LANES), BF16, "h"),
+            (halves, F32, "h"),
+            (halves, BF16, "h"),
+            (starts, BF16, "h"),
+            (reaches, F32, "h"),
+            ((4, ROWS, 256), BF16, "h"),
+        ],
+        [
+            ((ROWS + 16, 768), F32),
+            ((ROWS, LANES), F32),
+            ((ROWS + 16, 256), BF16),
+            ((2, 2, ROWS, LANES), BF16),
+            (halves, F32),
+            (halves, BF16),
+            (starts, BF16),
+            (reaches, F32),
             ((4, ROWS, 256), BF16),
         ],
-        [((ROWS + 16, 768), F32), ((ROWS, LANES), F32)],
-        10**9,
+        copies=7,
+        flops=10**9,
     )(
         *parts,
-        input_norm_gain.reshape(4, 256),
-        jnp.transpose(query_key_value_weight, (1, 0, 2)),
-        forget_gate_weight,
-        jnp.transpose(convolution_filter_taps, (0, 2, 1, 3)),
-        slot_forget_rate.reshape(1, LANES),
+        input_norm_gain.reshape(8, 128),
+        qkv_weight,
+        gate_weight,
+        taps,
+        slot_forget_rate,
         extra_forget_log,
         other[128:],
     )
     pieces, out_weight = lax.optimization_barrier((pieces, output_projection_weight))
     out_weights = [out_weight] + [shifted(out_weight, k) for k in (1, 2, 3)]
     held = lax.all_to_all(pieces, CHIPS, split_axis=0, concat_axis=0, tiled=True)
+    queries, scores, growth = kernel(
+        meeting_kernel,
+        "hhhhhv",
+        [(halves, BF16, "h"), (halves, F32, "h"), (halves, F32, "h")],
+        [
+            ((ROWS + 16, 256), BF16),
+            (halves, BF16),
+            (halves, F32),
+            (halves, BF16),
+            (reaches, BF16),
+            ((ROWS + 16, 256), F32),
+            (halves, BF16),
+            (halves, F32),
+            (halves, F32),
+        ],
+        copies=8,
+        flops=10**9,
+    )(query, kv, cum, shrink, start, taps)
     (prefixes,) = kernel(
-        scan_kernel, [((chips, 16, 128), BF16)], [((chips, 16, 128), F32)]
+        scan_kernel, "v", [((chips, 16, 128), BF16, "v")], [((chips, 16, 128), F32)]
     )(held)
     arrived = lax.all_to_all(prefixes, CHIPS, split_axis=0, concat_axis=0, tiled=True)
     (attention,) = kernel(
         attention_kernel,
-        [((ROWS, LANES), BF16)],
-        [((2, 2, SPAN, LANES), F32)],
-        10**9,
-    )(
-        qkv, cumulative, shrink, start, reach, arrived, head_norm_gain.reshape(1, LANES)
-    )
+        "hhhhhhhvv",
+        [((ROWS, LANES), BF16, "v")],
+        [
+            (halves, BF16),
+            (halves, BF16),
+            (halves, BF16),
+            (reaches, BF16),
+            (reaches, F32),
+            (halves, F32),
+            (halves, F32),
+            ((2, 2, SPAN, LANES), F32),
+        ],
+        copies=28,
+        flops=10**9,
+    )(queries, kv, shrink, start, reach, scores, growth, arrived, head_norm_gain)
     attended = [attention] + [shifted(attention, k) for k in (1, 2, 3)]
     base, out1, out2, out3 = kernel(
         tail_kernel,
-        [((ROWS, 256), F32)] + [((ROWS, 256), BF16)] * 3,
-        [((4, ROWS, 256), F32), ((4, ROWS, 256), F32)],
-        2 * 10**9,
+        "v" * 8 + "hvvh",
+        [((ROWS, 256), F32, "v")] + [((ROWS, 256), BF16, "v")] * 3,
+        [
+            ((4, ROWS, 256), F32),
+            ((4, ROWS, 256), F32),
+            ((4, ROWS, 256), BF16),
+            ((1024, 1024), BF16),
+        ],
+        copies=2,
+        flops=2 * 10**9,
     )(
         *attended,
         *out_weights,
         whole_tokens,
-        feedforward_norm_gain.reshape(4, 256),
+        feedforward_norm_gain.reshape(8, 128),
         up_projection_weight,
         down_projection_weight,
     )
     kept, sent = kernel(
-        finish_kernel, [((128, 256), BF16), ((128, 256), BF16)]
+        finish_kernel, "vvvv", [((128, 256), BF16, "v"), ((128, 256), BF16, "v")]
     )(base, shifted(out1, 1), shifted(out2, 2), shifted(out3, 3))
     returned = lax.ppermute(sent, "core", swap_pairs)
     first = lax.axis_index("core") == 0

time: 112 us -> 96.8 us (0.86)
  local copies, waits for them, and re-layouts: 17 us -> 0.06 us
  Pallas kernels: 16.9 us -> 23 us
  waiting for transfers between devices: 26.8 us -> 23.3 us
    unnamed x42 -> x16, local copies, waits for them, and re-layouts: 15.5 us -> 0.05 us
    pallas_call x6 -> x8, Pallas kernels: 16.9 us -> 23 us  [placed(): call(*[pltpu.with_memory_space_constraint(array, pltpu.HBM) if place == '...]
    all_to_all x1, waiting for transfers between devices: 8.88 us -> 5.57 us  [local(): lax.all_to_all(prefixes, CHIPS, split_axis=0, concat_axis=0, tiled=True)]
    reshape x4 -> x0, local copies, waits for them, and re-layouts: 1.54 us -> none  [the longest x1 0.76 us: local(): slot_forget_rate.reshape(1, LANES)]
  transfers between devices with their start and end apart: 18 -> 18, of which waited for: 11 -> 11; matrix products, arithmetic and copies ran while one was open for 1% -> 0% of each run, Pallas kernels for 6% -> 13%
where the time goes in v2:
time: 96.8 us; the launch traced here: 96.4 us
  starting transfers between devices  49.2 us (51%)
  waiting for transfers between devices  23.3 us (24%)
  Pallas kernels  23 us (24%)
    pallas_call x8, Pallas kernels, placed(): call(*[pltpu.with_memory_space_constraint(array, pltpu.HBM) if place == '...  23 us
    ppermute x12, starting transfers between devices, shifted(): lax.ppermute(value, 'head', [(j, (j + k) % count) for j in range(count)])  17.2 us
    all_to_all x1, starting transfers between devices, local(): lax.all_to_all(pieces, CHIPS, split_axis=0, concat_axis=0, tiled=True)  11.6 us
    ppermute x12, waiting for transfers between devices, shifted(): lax.ppermute(value, 'head', [(j, (j + k) % count) for j in range(count)])  10.4 us
    ppermute x1, starting transfers between devices, local(): returned = lax.ppermute(sent, 'core', swap_pairs)  6.14 us
    all_to_all x1, waiting for transfers between devices, local(): lax.all_to_all(pieces, CHIPS, split_axis=0, concat_axis=0, tiled=True)  5.73 us
    all_to_all x1, starting transfers between devices, local(): lax.all_to_all(prefixes, CHIPS, split_axis=0, concat_axis=0, tiled=True)  5.64 us
    all_to_all x1, waiting for transfers between devices, local(): lax.all_to_all(prefixes, CHIPS, split_axis=0, concat_axis=0, tiled=True)  5.57 us
  transfers between devices with their start and end apart: 18, of which 11 were waited for; matrix products, arithmetic and copies ran while one was open for 0% of the time, Pallas kernels for 13%

profile of v2, /device:TPU:1, one launch (start us, length us, event | category | flops | bytes accessed | tf_op | source)
XLA Modules:
  0.0 96.4 jit_solution(7148969586174274370)
XLA Ops:
  0.0 0.9 shard_map.118
  0.9 0.0 copy-start
  1.0 0.0 copy-start.3
  1.0 0.0 copy-start.4
  1.0 0.0 copy-start.6
  1.0 3.3 %collective-permute-start = (bf16[136,256]{1,0:T(8,128)(2,1)S(1)}, bf16[136,256]{1,0:T(8,128)(2,1)S(1)}, u32[]{:S(2)}, u32[]{:S(2)}) collective-permute-start(bf16[136,256]{1,0:T(8,128)(2,1)S(1)} %get-tuple-element.34), channel_id=1, source_target_pairs={{0,4},{4,0},{1,5},{5,1},{2,6},{6,2},{3,7},{7,3},{8,12},{12,8},{9,1... | collective-permute-start | bytes 208904 | tf_op jit(solution)/shard_map/ppermute | solution.py:498
  4.3 1.9 %collective-permute-start.1 = (bf16[8,256]{1,0:T(8,128)(2,1)S(1)}, bf16[8,256]{1,0:T(8,128)(2,1)S(1)}, u32[]{:S(2)}, u32[]{:S(2)}) collective-permute-start(bf16[8,256]{1,0:T(8,128)(2,1)S(1)} %get-tuple-element.35), channel_id=1, source_target_pairs={{4,8},{12,16},{20,24},{28,32},{36,40},{44,48},{52,56},{60,64},{68,... | collective-permute-start | bytes 12296 | tf_op jit(solution)/shard_map/ppermute | solution.py:499
  6.2 3.4 %collective-permute-start.2 = (bf16[8,256]{1,0:T(8,128)(2,1)S(1)}, bf16[8,256]{1,0:T(8,128)(2,1)S(1)}, u32[]{:S(2)}, u32[]{:S(2)}) collective-permute-start(bf16[8,256]{1,0:T(8,128)(2,1)S(1)} %get-tuple-element.36), channel_id=1, source_target_pairs={{4,12},{12,20},{20,28},{28,36},{36,44},{44,52},{52,60},{60,68},{68... | collective-permute-start | bytes 12296 | tf_op jit(solution)/shard_map/ppermute | solution.py:500
  9.6 0.0 collective-permute-done
  9.6 0.0 collective-permute-done.1
  9.6 0.7 collective-permute-done.2
  10.3 1.4 %collective-permute-start.3 = (bf16[272,256]{1,0:T(8,128)(2,1)S(1)}, bf16[272,256]{1,0:T(8,128)(2,1)S(1)}, u32[]{:S(2)}, u32[]{:S(2)}) collective-permute-start(bf16[272,256]{1,0:T(8,128)(2,1)S(1)} %pad_maximum_fusion.part0), channel_id=1, source_target_pairs={{0,1},{1,2},{2,3},{3,0},{4,5},{5,6},{6,7},{7,4},{8,9},{9,10},{10,1... | collective-permute-start | bytes 417800 | tf_op jit(solution)/shard_map/ppermute | solution.py:465
  11.7 2.6 %collective-permute-start.4 = (bf16[272,256]{1,0:T(8,128)(2,1)S(1)}, bf16[272,256]{1,0:T(8,128)(2,1)S(1)}, u32[]{:S(2)}, u32[]{:S(2)}) collective-permute-start(bf16[272,256]{1,0:T(8,128)(2,1)S(1)} %pad_maximum_fusion.part0), channel_id=1, source_target_pairs={{0,2},{1,3},{2,0},{3,1},{4,6},{5,7},{6,4},{7,5},{8,10},{9,11},{10,... | collective-permute-start | bytes 417800 | tf_op jit(solution)/shard_map/ppermute | solution.py:465
  14.3 1.1 %collective-permute-start.5 = (bf16[272,256]{1,0:T(8,128)(2,1)S(1)}, bf16[272,256]{1,0:T(8,128)(2,1)S(1)}, u32[]{:S(2)}, u32[]{:S(2)}) collective-permute-start(bf16[272,256]{1,0:T(8,128)(2,1)S(1)} %pad_maximum_fusion.part0), channel_id=1, source_target_pairs={{0,3},{1,0},{2,1},{3,2},{4,7},{5,4},{6,5},{7,6},{8,11},{9,8},{10,9... | collective-permute-start | bytes 417800 | tf_op jit(solution)/shard_map/ppermute | solution.py:465
  15.4 1.5 %shard_map.119 = (bf16[3,1024,256]{2,1,0:T(8,128)(2,1)S(1)}, bf16[1024,256]{1,0:T(8,128)(2,1)S(1)}) custom-call(bf16[3,1024,256]{2,1,0:T(8,128)(2,1)} %bitcast.12, bf16[1024,256]{1,0:T(8,128)(2,1)} %gate_weight), custom_call_target="tpu_custom_call" | custom-call | flops 1000000000 | bytes 1048576 | tf_op jit(solution)/shard_map/pallas_call | solution.py:453
  16.9 0.0 copy-start.2
  16.9 0.0 collective-permute-done.3.part1
  17.0 4.3 %collective-permute-done.4.part2 = bf16[272,256]{1,0:T(8,128)(2,1)S(1)} collective-permute-done((bf16[272,256]{1,0:T(8,128)(2,1)S(1)}, bf16[272,256]{1,0:T(8,128)(2,1)S(1)}, u32[]{:S(2)}, u32[]{:S(2)}) %collective-permute-start.4) | collective-permute-done | bytes 139296 | tf_op jit(solution)/shard_map/ppermute | solution.py:465
  21.3 0.0 collective-permute-done.5.part3
  21.3 0.0 copy-done
  21.3 0.0 copy-done.3
  21.3 0.0 copy-done.4
  21.3 0.0 copy-done.6
  21.3 4.8 %shard_map.120 = (bf16[32,24,128]{2,1,0:T(8,128)(2,1)}, bf16[272,256]{1,0:T(8,128)(2,1)}, bf16[2,2,256,256]{3,2,1,0:T(8,128)(2,1)}, f32[2,256,256]{2,1,0:T(8,128...) custom-call(bf16[272,256]{1,0:T(8,128)(2,1)S(1)} %pad_maximum_fusion, ...), custom_call_target="tpu_custom_call" | custom-call | flops 1000000000 | bytes 1048576 | tf_op jit(solution)/shard_map/pallas_call | solution.py:453
  26.1 11.6 %all-to-all-start = ((bf16[32,24,128]{2,1,0:T(8,128)(2,1)}), bf16[32,24,128]{2,1,0:T(8,128)(2,1)S(1)}, u32[]{:S(2)}, u32[]{:S(2)}) async-start(bf16[32,24,128]{2,1,0:T(8,128)(2,1)} %get-tuple-element.52), calls=%async_computation | async-start | bytes 393216 | tf_op jit(solution)/shard_map/all_to_all | solution.py:561
  37.8 0.0 copy-done.2
  37.8 0.0 copy-start.7
  37.8 2.2 %collective-permute-start.10 = (bf16[256,1024]{1,0:T(8,128)(2,1)S(1)}, bf16[256,1024]{1,0:T(8,128)(2,1)S(1)}, u32[]{:S(2)}, u32[]{:S(2)}) collective-permute-start(bf16[256,1024]{1,0:T(8,128)(2,1)S(1)} %copy-done.2), channel_id=1, source_target_pairs={{0,2},{1,3},{2,0},{3,1},{4,6},{5,7},{6,4},{7,5},{8,10},{9,11},{10,... | collective-permute-start | bytes 1572872 | tf_op jit(solution)/shard_map/ppermute | solution.py:465
  40.0 0.9 collective-permute-start.11
  40.9 0.5 collective-permute-start.9
  41.4 5.7 %all-to-all-done.pieces = bf16[32,24,128]{2,1,0:T(8,128)(2,1)S(1)} async-done(((bf16[32,24,128]{2,1,0:T(8,128)(2,1)}), bf16[32,24,128]{2,1,0:T(8,128)(2,1)S(1)}, u32[]{:S(2)}, u32[]{:S(2)}) %all-to-all-start) | async-done | bytes 196640 | tf_op jit(solution)/shard_map/all_to_all | solution.py:561
  47.1 0.8 shard_map.122
  47.9 5.6 %all-to-all-start.1 = ((bf16[32,16,128]{2,1,0:T(8,128)(2,1)}), bf16[32,16,128]{2,1,0:T(8,128)(2,1)S(1)}, u32[]{:S(2)}, u32[]{:S(2)}) async-start(bf16[32,16,128]{2,1,0:T(8,128)(2,1)} %shard_map.122), calls=%async_computation.1 | async-start | bytes 262144 | tf_op jit(solution)/shard_map/all_to_all | solution.py:583
  53.6 3.4 %shard_map.121 = (bf16[2,256,256]{2,1,0:T(8,128)(2,1)}, f32[2,256,256]{2,1,0:T(8,128)}, f32[2,256,256]{2,1,0:T(8,128)}) custom-call(bf16[272,256]{1,0:T(8,128)(2,1)} %get-tuple-element.42.query_in, bf16[2,2,256,256]{3,2,1,0:T(8,128)(2,1)} %get-tuple-element.43.kv_in, f32[2,256,256]{2,1,0:T(8,128)} %get-tuple-element.44.cum_in, ...), custom_call_target="tpu_custom_call" | custom-call | flops 1000000000 | bytes 1048576 | tf_op jit(solution)/shard_map/pallas_call | solution.py:453
  57.0 0.0 copy-start.1
  57.0 0.0 copy-start.5
  57.0 5.6 %all-to-all-done.1.arrived = bf16[32,16,128]{2,1,0:T(8,128)(2,1)S(1)} async-done(((bf16[32,16,128]{2,1,0:T(8,128)(2,1)}), bf16[32,16,128]{2,1,0:T(8,128)(2,1)S(1)}, u32[]{:S(2)}, u32[]{:S(2)}) %all-to-all-start.1) | async-done | bytes 131104 | tf_op jit(solution)/shard_map/all_to_all | solution.py:583
  62.6 0.0 copy-done.7
  62.6 6.7 %shard_map.123.part0 = bf16[256,256]{1,0:T(8,128)(2,1)S(1)} custom-call(bf16[2,256,256]{2,1,0:T(8,128)(2,1)} %get-tuple-element.47.queries_in, bf16[2,2,256,256]{3,2,1,0:T(8,128)(2,1)} %get-tuple-element.43.kv_in, bf16[2,256,256]{2,1,0:T(8,128)(2,1)} %get-tuple-element.45.shrink_in, bf16[2,4,2,64,256]{4,3,2,1,0:T(8,128)(2,1)} %get-tuple-element.46.start_in, ...), custom_call_target="tpu_custom_call" | custom-call | flops 1000000000 | bytes 1048576 | tf_op jit(solution)/shard_map/pallas_call | solution.py:453
  69.3 0.7 collective-permute-start.6
  70.0 2.4 %collective-permute-start.7 = (bf16[256,256]{1,0:T(8,128)(2,1)S(1)}, bf16[256,256]{1,0:T(8,128)(2,1)S(1)}, u32[]{:S(2)}, u32[]{:S(2)}) collective-permute-start(bf16[256,256]{1,0:T(8,128)(2,1)S(1)} %shard_map.123.part0), channel_id=1, source_target_pairs={{0,2},{1,3},{2,0},{3,1},{4,6},{5,7},{6,4},{7,5},{8,10},{9,11},{10,... | collective-permute-start | bytes 393224 | tf_op jit(solution)/shard_map/ppermute | solution.py:465
  72.4 0.0 collective-permute-done.10.weight2
  72.4 1.1 %collective-permute-start.8 = (bf16[256,256]{1,0:T(8,128)(2,1)S(1)}, bf16[256,256]{1,0:T(8,128)(2,1)S(1)}, u32[]{:S(2)}, u32[]{:S(2)}) collective-permute-start(bf16[256,256]{1,0:T(8,128)(2,1)S(1)} %shard_map.123.part0), channel_id=1, source_target_pairs={{0,3},{1,0},{2,1},{3,2},{4,7},{5,4},{6,5},{7,6},{8,11},{9,8},{10,9... | collective-permute-start | bytes 393224 | tf_op jit(solution)/shard_map/ppermute | solution.py:465
  73.5 0.0 collective-permute-done.11.weight3
  73.5 0.0 collective-permute-done.9.weight1
  73.5 0.9 collective-permute-done.6.part1
  74.4 1.8 %collective-permute-done.7.part2 = bf16[256,256]{1,0:T(8,128)(2,1)S(1)} collective-permute-done((bf16[256,256]{1,0:T(8,128)(2,1)S(1)}, bf16[256,256]{1,0:T(8,128)(2,1)S(1)}, u32[]{:S(2)}, u32[]{:S(2)}) %collective-permute-start.7) | collective-permute-done | bytes 131104 | tf_op jit(solution)/shard_map/ppermute | solution.py:465
  76.2 0.5 collective-permute-done.8.part3
  76.6 0.0 copy-done.1
  76.6 0.0 copy-done.5
  76.6 4.8 %shard_map.124 = (f32[256,256]{1,0:T(8,128)S(1)}, bf16[256,256]{1,0:T(8,128)(2,1)S(1)}, bf16[256,256]{1,0:T(8,128)(2,1)S(1)}, bf16[256,256]{1,0:T(8,128)(2,1)S(1)}) custom-call(bf16[256,256]{1,0:T(8,128)(2,1)S(1)} %shard_map.123.part0, bf16[256,256]{1,0:T(8,128)(2,1)S(1)} %collective-permute-done.6.part1, bf16[256,256]{1,0:T(8,128)(2,1)S(1)} %collective-permute-done.7.part2, ...), custom_call_target="tpu_custom_call" | custom-call | flops 2000000000 | bytes 1048576 | tf_op jit(solution)/shard_map/pallas_call | solution.py:453
  81.4 1.4 %collective-permute-start.12 = (bf16[256,256]{1,0:T(8,128)(2,1)S(1)}, bf16[256,256]{1,0:T(8,128)(2,1)S(1)}, u32[]{:S(2)}, u32[]{:S(2)}) collective-permute-start(bf16[256,256]{1,0:T(8,128)(2,1)S(1)} %get-tuple-element.56), channel_id=1, source_target_pairs={{0,1},{1,2},{2,3},{3,0},{4,5},{5,6},{6,7},{7,4},{8,9},{9,10},{10,1... | collective-permute-start | bytes 393224 | tf_op jit(solution)/shard_map/ppermute | solution.py:465
  82.8 2.0 %collective-permute-start.13 = (bf16[256,256]{1,0:T(8,128)(2,1)S(1)}, bf16[256,256]{1,0:T(8,128)(2,1)S(1)}, u32[]{:S(2)}, u32[]{:S(2)}) collective-permute-start(bf16[256,256]{1,0:T(8,128)(2,1)S(1)} %get-tuple-element.57), channel_id=1, source_target_pairs={{0,2},{1,3},{2,0},{3,1},{4,6},{5,7},{6,4},{7,5},{8,10},{9,11},{10,... | collective-permute-start | bytes 393224 | tf_op jit(solution)/shard_map/ppermute | solution.py:465
  84.8 0.9 collective-permute-start.14
  85.7 0.8 collective-permute-done.12.part1
  86.5 2.0 %collective-permute-done.13.part2 = bf16[256,256]{1,0:T(8,128)(2,1)S(1)} collective-permute-done((bf16[256,256]{1,0:T(8,128)(2,1)S(1)}, bf16[256,256]{1,0:T(8,128)(2,1)S(1)}, u32[]{:S(2)}, u32[]{:S(2)}) %collective-permute-start.13) | collective-permute-done | bytes 131104 | tf_op jit(solution)/shard_map/ppermute | solution.py:465
  88.5 0.1 collective-permute-done.14.part3
  88.6 0.1 shard_map.125
  88.7 6.1 %collective-permute-start.15 = (bf16[128,256]{1,0:T(8,128)(2,1)S(1)}, bf16[128,256]{1,0:T(8,128)(2,1)S(1)}, u32[]{:S(2)}, u32[]{:S(2)}) collective-permute-start(bf16[128,256]{1,0:T(8,128)(2,1)S(1)} %get-tuple-element.60), channel_id=1, source_target_pairs={{0,4},{4,0},{1,5},{5,1},{2,6},{6,2},{3,7},{7,3},{8,12},{12,8},{9,1... | collective-permute-start | bytes 196616 | tf_op jit(solution)/shard_map/ppermute | solution.py:625
  94.8 0.9 collective-permute-done.15
  95.7 0.7 pad_maximum_fusion.1
  (4 shorter events, 0.0 us)
Async XLA Ops:
  0.9 20.3 %copy-start = (f32[2,128]{1,0:T(2,128)S(1)}, f32[2,128]{1,0:T(2,128)}, u32[]{:S(2)}) copy-start(f32[2,128]{1,0:T(2,128)} %extra.1) | copy-start | bytes 3076
  1.0 20.3 %copy-start.3 = (f32[2,4,3,256]{3,1,2,0:T(4,128)S(1)}, f32[2,4,3,256]{3,1,2,0:T(4,128)}, u32[]{:S(2)}) copy-start(f32[2,4,3,256]{3,1,2,0:T(4,128)} %param.16) | copy-start | bytes 73732
  1.0 20.3 %copy-start.4 = (f32[1024]{0:T(1024)S(1)}, f32[1024]{0:T(1024)}, u32[]{:S(2)}) copy-start(f32[1024]{0:T(1024)} %param.13) | copy-start | bytes 12292
  1.0 20.3 %copy-start.6 = (f32[4,64]{1,0:T(4,128)S(1)}, f32[4,64]{1,0:T(4,128)}, u32[]{:S(2)}) copy-start(f32[4,64]{1,0:T(4,128)} %rate.1) | copy-start | bytes 3076
  1.0 8.6 %collective-permute-start = (bf16[136,256]{1,0:T(8,128)(2,1)S(1)}, bf16[136,256]{1,0:T(8,128)(2,1)S(1)}, u32[]{:S(2)}, u32[]{:S(2)}) collective-permute-start(bf16[136,256]{1,0:T(8,128)(2,1)S(1)} %get-tuple-element.34), channel_id=1, source_target_pairs={{0,4},{4,0},{1,5},{5,1},{2,6},{6,2},{3,7},{7,3},{8,12},{12,8},{9,1... | collective-permute-start | bytes 208904 | tf_op jit(solution)/shard_map/ppermute | solution.py:498
  4.3 5.3 %collective-permute-start.1 = (bf16[8,256]{1,0:T(8,128)(2,1)S(1)}, bf16[8,256]{1,0:T(8,128)(2,1)S(1)}, u32[]{:S(2)}, u32[]{:S(2)}) collective-permute-start(bf16[8,256]{1,0:T(8,128)(2,1)S(1)} %get-tuple-element.35), channel_id=1, source_target_pairs={{4,8},{12,16},{20,24},{28,32},{36,40},{44,48},{52,56},{60,64},{68,... | collective-permute-start | bytes 12296 | tf_op jit(solution)/shard_map/ppermute | solution.py:499
  6.2 4.1 %collective-permute-start.2 = (bf16[8,256]{1,0:T(8,128)(2,1)S(1)}, bf16[8,256]{1,0:T(8,128)(2,1)S(1)}, u32[]{:S(2)}, u32[]{:S(2)}) collective-permute-start(bf16[8,256]{1,0:T(8,128)(2,1)S(1)} %get-tuple-element.36), channel_id=1, source_target_pairs={{4,12},{12,20},{20,28},{28,36},{36,44},{44,52},{52,60},{60,68},{68... | collective-permute-start | bytes 12296 | tf_op jit(solution)/shard_map/ppermute | solution.py:500
  10.3 6.6 %collective-permute-start.3 = (bf16[272,256]{1,0:T(8,128)(2,1)S(1)}, bf16[272,256]{1,0:T(8,128)(2,1)S(1)}, u32[]{:S(2)}, u32[]{:S(2)}) collective-permute-start(bf16[272,256]{1,0:T(8,128)(2,1)S(1)} %pad_maximum_fusion.part0), channel_id=1, source_target_pairs={{0,1},{1,2},{2,3},{3,0},{4,5},{5,6},{6,7},{7,4},{8,9},{9,10},{10,1... | collective-permute-start | bytes 417800 | tf_op jit(solution)/shard_map/ppermute | solution.py:465
  11.7 9.6 %collective-permute-start.4 = (bf16[272,256]{1,0:T(8,128)(2,1)S(1)}, bf16[272,256]{1,0:T(8,128)(2,1)S(1)}, u32[]{:S(2)}, u32[]{:S(2)}) collective-permute-start(bf16[272,256]{1,0:T(8,128)(2,1)S(1)} %pad_maximum_fusion.part0), channel_id=1, source_target_pairs={{0,2},{1,3},{2,0},{3,1},{4,6},{5,7},{6,4},{7,5},{8,10},{9,11},{10,... | collective-permute-start | bytes 417800 | tf_op jit(solution)/shard_map/ppermute | solution.py:465
  14.3 7.0 %collective-permute-start.5 = (bf16[272,256]{1,0:T(8,128)(2,1)S(1)}, bf16[272,256]{1,0:T(8,128)(2,1)S(1)}, u32[]{:S(2)}, u32[]{:S(2)}) collective-permute-start(bf16[272,256]{1,0:T(8,128)(2,1)S(1)} %pad_maximum_fusion.part0), channel_id=1, source_target_pairs={{0,3},{1,0},{2,1},{3,2},{4,7},{5,4},{6,5},{7,6},{8,11},{9,8},{10,9... | collective-permute-start | bytes 417800 | tf_op jit(solution)/shard_map/ppermute | solution.py:465
  16.9 20.8 %copy-start.2 = (bf16[256,1024]{1,0:T(8,128)(2,1)S(1)}, bf16[256,1024]{1,0:T(8,128)(2,1)}, u32[]{:S(2)}) copy-start(bf16[256,1024]{1,0:T(8,128)(2,1)} %weight0) | copy-start | bytes 1572868
  26.1 21.0 %all-to-all-start = ((bf16[32,24,128]{2,1,0:T(8,128)(2,1)}), bf16[32,24,128]{2,1,0:T(8,128)(2,1)S(1)}, u32[]{:S(2)}, u32[]{:S(2)}) async-start(bf16[32,24,128]{2,1,0:T(8,128)(2,1)} %get-tuple-element.52), calls=%async_computation | async-start | bytes 393216 | tf_op jit(solution)/shard_map/all_to_all | solution.py:561
  37.8 24.8 %copy-start.7 = (f32[4,64]{1,0:T(4,128)S(1)}, f32[4,64]{1,0:T(4,128)}, u32[]{:S(2)}) copy-start(f32[4,64]{1,0:T(4,128)} %gain.1) | copy-start | bytes 3076
  37.8 34.6 %collective-permute-start.10 = (bf16[256,1024]{1,0:T(8,128)(2,1)S(1)}, bf16[256,1024]{1,0:T(8,128)(2,1)S(1)}, u32[]{:S(2)}, u32[]{:S(2)}) collective-permute-start(bf16[256,1024]{1,0:T(8,128)(2,1)S(1)} %copy-done.2), channel_id=1, source_target_pairs={{0,2},{1,3},{2,0},{3,1},{4,6},{5,7},{6,4},{7,5},{8,10},{9,11},{10,... | collective-permute-start | bytes 1572872 | tf_op jit(solution)/shard_map/ppermute | solution.py:465
  40.0 33.5 %collective-permute-start.11 = (bf16[256,1024]{1,0:T(8,128)(2,1)S(1)}, bf16[256,1024]{1,0:T(8,128)(2,1)}, u32[]{:S(2)}, u32[]{:S(2)}) collective-permute-start(bf16[256,1024]{1,0:T(8,128)(2,1)S(1)} %copy-done.2), channel_id=1, source_target_pairs={{0,3},{1,0},{2,1},{3,2},{4,7},{5,4},{6,5},{7,6},{8,11},{9,8},{10,9... | collective-permute-start | bytes 1572872 | tf_op jit(solution)/shard_map/ppermute | solution.py:465
  40.9 32.6 %collective-permute-start.9 = (bf16[256,1024]{1,0:T(8,128)(2,1)S(1)}, bf16[256,1024]{1,0:T(8,128)(2,1)}, u32[]{:S(2)}, u32[]{:S(2)}) collective-permute-start(bf16[256,1024]{1,0:T(8,128)(2,1)S(1)} %copy-done.2), channel_id=1, source_target_pairs={{0,1},{1,2},{2,3},{3,0},{4,5},{5,6},{6,7},{7,4},{8,9},{9,10},{10,1... | collective-permute-start | bytes 1572872 | tf_op jit(solution)/shard_map/ppermute | solution.py:465
  47.9 14.6 %all-to-all-start.1 = ((bf16[32,16,128]{2,1,0:T(8,128)(2,1)}), bf16[32,16,128]{2,1,0:T(8,128)(2,1)S(1)}, u32[]{:S(2)}, u32[]{:S(2)}) async-start(bf16[32,16,128]{2,1,0:T(8,128)(2,1)} %shard_map.122), calls=%async_computation.1 | async-start | bytes 262144 | tf_op jit(solution)/shard_map/all_to_all | solution.py:583
  57.0 19.7 %copy-start.1 = (bf16[1024,1024]{1,0:T(8,128)(2,1)S(1)}, bf16[1024,1024]{1,0:T(8,128)(2,1)}, u32[]{:S(2)}) copy-start(bf16[1024,1024]{1,0:T(8,128)(2,1)} %up.1) | copy-start | bytes 6291460
  57.0 19.7 %copy-start.5 = (f32[1024]{0:T(1024)S(1)}, f32[1024]{0:T(1024)}, u32[]{:S(2)}) copy-start(f32[1024]{0:T(1024)} %param.21) | copy-start | bytes 12292
  69.3 5.1 %collective-permute-start.6 = (bf16[256,256]{1,0:T(8,128)(2,1)S(1)}, bf16[256,256]{1,0:T(8,128)(2,1)S(1)}, u32[]{:S(2)}, u32[]{:S(2)}) collective-permute-start(bf16[256,256]{1,0:T(8,128)(2,1)S(1)} %shard_map.123.part0), channel_id=1, source_target_pairs={{0,1},{1,2},{2,3},{3,0},{4,5},{5,6},{6,7},{7,4},{8,9},{9,10},{10,1... | collective-permute-start | bytes 393224 | tf_op jit(solution)/shard_map/ppermute | solution.py:465
  70.0 6.2 %collective-permute-start.7 = (bf16[256,256]{1,0:T(8,128)(2,1)S(1)}, bf16[256,256]{1,0:T(8,128)(2,1)S(1)}, u32[]{:S(2)}, u32[]{:S(2)}) collective-permute-start(bf16[256,256]{1,0:T(8,128)(2,1)S(1)} %shard_map.123.part0), channel_id=1, source_target_pairs={{0,2},{1,3},{2,0},{3,1},{4,6},{5,7},{6,4},{7,5},{8,10},{9,11},{10,... | collective-permute-start | bytes 393224 | tf_op jit(solution)/shard_map/ppermute | solution.py:465
  72.4 4.2 %collective-permute-start.8 = (bf16[256,256]{1,0:T(8,128)(2,1)S(1)}, bf16[256,256]{1,0:T(8,128)(2,1)S(1)}, u32[]{:S(2)}, u32[]{:S(2)}) collective-permute-start(bf16[256,256]{1,0:T(8,128)(2,1)S(1)} %shard_map.123.part0), channel_id=1, source_target_pairs={{0,3},{1,0},{2,1},{3,2},{4,7},{5,4},{6,5},{7,6},{8,11},{9,8},{10,9... | collective-permute-start | bytes 393224 | tf_op jit(solution)/shard_map/ppermute | solution.py:465
  81.4 5.1 %collective-permute-start.12 = (bf16[256,256]{1,0:T(8,128)(2,1)S(1)}, bf16[256,256]{1,0:T(8,128)(2,1)S(1)}, u32[]{:S(2)}, u32[]{:S(2)}) collective-permute-start(bf16[256,256]{1,0:T(8,128)(2,1)S(1)} %get-tuple-element.56), channel_id=1, source_target_pairs={{0,1},{1,2},{2,3},{3,0},{4,5},{5,6},{6,7},{7,4},{8,9},{9,10},{10,1... | collective-permute-start | bytes 393224 | tf_op jit(solution)/shard_map/ppermute | solution.py:465
  82.8 5.8 %collective-permute-start.13 = (bf16[256,256]{1,0:T(8,128)(2,1)S(1)}, bf16[256,256]{1,0:T(8,128)(2,1)S(1)}, u32[]{:S(2)}, u32[]{:S(2)}) collective-permute-start(bf16[256,256]{1,0:T(8,128)(2,1)S(1)} %get-tuple-element.57), channel_id=1, source_target_pairs={{0,2},{1,3},{2,0},{3,1},{4,6},{5,7},{6,4},{7,5},{8,10},{9,11},{10,... | collective-permute-start | bytes 393224 | tf_op jit(solution)/shard_map/ppermute | solution.py:465
  84.8 3.8 %collective-permute-start.14 = (bf16[256,256]{1,0:T(8,128)(2,1)S(1)}, bf16[256,256]{1,0:T(8,128)(2,1)S(1)}, u32[]{:S(2)}, u32[]{:S(2)}) collective-permute-start(bf16[256,256]{1,0:T(8,128)(2,1)S(1)} %get-tuple-element.58), channel_id=1, source_target_pairs={{0,3},{1,0},{2,1},{3,2},{4,7},{5,4},{6,5},{7,6},{8,11},{9,8},{10,9... | collective-permute-start | bytes 393224 | tf_op jit(solution)/shard_map/ppermute | solution.py:465
  88.7 7.0 %collective-permute-start.15 = (bf16[128,256]{1,0:T(8,128)(2,1)S(1)}, bf16[128,256]{1,0:T(8,128)(2,1)S(1)}, u32[]{:S(2)}, u32[]{:S(2)}) collective-permute-start(bf16[128,256]{1,0:T(8,128)(2,1)S(1)} %get-tuple-element.60), channel_id=1, source_target_pairs={{0,4},{4,0},{1,5},{5,1},{2,6},{6,2},{3,7},{7,3},{8,12},{12,8},{9,1... | collective-permute-start | bytes 196616 | tf_op jit(solution)/shard_map/ppermute | solution.py:625

commit v3 on v2

--- a/solution.py
+++ b/solution.py
@@ -1,3 +1,5 @@
+import functools
+
 import jax
 import jax.numpy as jnp
 from jax import lax
@@ -5,6 +7,7 @@
 from jax.experimental.pallas import tpu as pltpu
 from jax.sharding import Mesh
 from jax.sharding import PartitionSpec as P
+
 
 CHIPS = ("x", "z")
 SEQ = ("x", "z", "core")
@@ -97,14 +100,13 @@
     finish(begin([(qkv_weight, qkv_out), (gate_weight, gate_out)], semaphores))
 
 
-def split_kernel(
-    tokens_in, extra_in, swap_out, a_out, b_out, mine_out, tokens, extra, semaphores
-):
+def edge_kernel(tokens_in, extra_in, edge_out, swap_out, mine_out, tokens, extra, semaphores):
     core = lax.axis_index("core")
     finish(begin([(tokens_in, tokens), (extra_in, extra)], semaphores))
-    mine = tokens[core]
-    other = tokens[1 - core]
-    mine_out[...] = mine
+    mine_out[...] = tokens[core]
+    for which in range(2):
+        wide = tokens[which].astype(F32)
+        edge_out[which] = jnp.where(core == 1, wide[120:128], wide[0:8]).astype(BF16)
     row = extra[pl.ds(1 - core, 1), :]
     high = row.astype(BF16).astype(F32)
     middle = (row - high).astype(BF16).astype(F32)
@@ -113,17 +115,21 @@
     first = jnp.concatenate([high, middle], axis=1)
     second = jnp.concatenate([low, low], axis=1)
     packed = jnp.where(line == 0, first, jnp.where(line == 1, second, 0.0))
-    swap_out[...] = jnp.concatenate([other.astype(F32), packed], axis=0).astype(BF16)
-    wide_other = other.astype(F32)
-    wide_mine = mine.astype(F32)
-    a_out[...] = jnp.where(core == 1, wide_other[120:128], wide_other[0:8]).astype(BF16)
-    b_out[...] = jnp.where(core == 1, wide_mine[120:128], wide_mine[0:8]).astype(BF16)
+    swap_out[0:128] = tokens[1 - core]
+    swap_out[128:136] = packed.astype(BF16)
+
+
+def swap_kernel(local_part, edges, swap_out, kept_out):
+    core = lax.axis_index("core")
+    swap_out[0:136] = local_part[...]
+    swap_out[136:144] = edges[1 - core]
+    kept_out[...] = edges[core]
 
 
 def front_kernel(
     part0, part1, part2, part3, gain, qkv_weight, gate_weight, taps, rate, extra, extra_other,
-    sent_out, query_out, kv_out, cum_out, shrink_out, start_out, reach_out, tokens_out,
-    padded, decay, query, kv, cum, shrink, start, reach, tokens, semaphores,
+    sent_out, query_out, kv_out, cum_out, shrink_out, start_out, reach_out, kept_out, passed_out,
+    padded, decay, query, kv, cum, shrink, start, reach, kept, passed_on, semaphores,
 ):
     core = lax.axis_index("core")
     head = lax.axis_index("head")
@@ -134,11 +140,11 @@
     square = jnp.zeros((ROWS + 16, 1), F32)
     for k in range(4):
         values = parts[k][...]
-        tokens[sources[k], pl.ds(own_rows, 128), :] = values[0:128]
-        tokens[sources[k], pl.ds(other_rows, 128), :] = values[128:256]
+        kept[sources[k]] = values[0:128]
+        passed_on[sources[k]] = values[128:256]
         wide = values.astype(F32)
         square = square + jnp.sum(wide * wide, axis=1, keepdims=True)
-    going = begin([(tokens, tokens_out)], semaphores.at[pl.ds(0, 1)])
+    going = begin([(kept, kept_out), (passed_on, passed_out)], semaphores.at[pl.ds(0, 2)])
     scale = lax.rsqrt(square * (1.0 / 1024.0) + EPSILON)
     normed = [
         (parts[k][...].astype(F32) * scale * gain_of(gain, sources[k])).astype(BF16)
@@ -160,7 +166,7 @@
         padded[pl.ds(a_pad, 8), columns] = total[256:264]
         padded[pl.ds(b_pad, 8), columns] = total[264:272]
     query[...] = padded[:, 0:256].astype(BF16)
-    going += begin([(query, query_out)], semaphores.at[pl.ds(1, 1)])
+    going += begin([(query, query_out)], semaphores.at[pl.ds(2, 1)])
     gate = nn(normed[0], gate_weight[pl.ds(starts[0], 256), :])
     for k in range(1, 4):
         gate = gate + nn(normed[k], gate_weight[pl.ds(starts[k], 256), :])
@@ -175,7 +181,7 @@
         columns = slice(i * 256, (i + 1) * 256)
         for direction in range(2):
             kv[direction, i - 1] = convolved(padded, taps, direction, i, columns)
-    going += begin([(kv, kv_out)], semaphores.at[pl.ds(2, 1)])
+    going += begin([(kv, kv_out)], semaphores.at[pl.ds(3, 1)])
 
     log_decay = decay[...]
     inflow = minus_expm1(log_decay)
@@ -187,7 +193,7 @@
     for direction in range(2):
         cum[direction] = nn(later if direction else earlier, log_decay, HIGHEST)
         shrink[direction] = (jnp.exp(-cum[direction]) * inflow).astype(BF16)
-    going += begin([(cum, cum_out), (shrink, shrink_out)], semaphores.at[pl.ds(3, 2)])
+    going += begin([(cum, cum_out), (shrink, shrink_out)], semaphores.at[pl.ds(4, 2)])
     span_totals = tn(log_decay, spans, HIGHEST)
     totals = [compact_rows(span_totals[:, n * 128 : (n + 1) * 128]) for n in range(SPANS)]
     factors = [jnp.exp(total) for total in totals]
@@ -209,7 +215,7 @@
                 states[which] = factors[n] * states[which] + added
             passed = passed + totals[n]
         ends.append(states)
-    going += begin([(start, start_out), (reach, reach_out)], semaphores.at[pl.ds(5, 2)])
+    going += begin([(start, start_out), (reach, reach_out)], semaphores.at[pl.ds(6, 2)])
     factor = jnp.exp(totals[0] + totals[1] + totals[2] + totals[3])
     high = factor.astype(BF16).astype(F32)
     lane = iota((SPAN, LANES), 1)
@@ -311,7 +317,7 @@
 
 
 def head_max(values):
-    first = in_first_head(SPAN)
+    first = in_first_head(values.shape[0])
     halves = []
     for half in range(2):
         part = values[:, half * 128 : (half + 1) * 128]
@@ -322,27 +328,28 @@
 
 
 def attention_kernel(
+    own_half,
     queries_in, kv_in, shrink_in, start_in, reach_in, scores_in, growth_in, arrived, gain,
     out,
-    queries, values, shrink, start, reach, scores, growth, entering, semaphores,
+    queries, values, shrink, start, reach, scores, growth, weighted, mixing, result, entering,
+    semaphores,
 ):
-    coming = []
-    for n in range(SPANS):
-        rows = pl.ds(n * SPAN, SPAN)
-        coming.append(
-            begin(
-                [
-                    (reach_in.at[:, n], reach.at[:, n]),
-                    (queries_in.at[:, rows, :], queries.at[:, rows, :]),
-                    (growth_in.at[:, rows, :], growth.at[:, rows, :]),
-                    (scores_in.at[:, rows, :], scores.at[:, rows, :]),
-                    (shrink_in.at[:, rows, :], shrink.at[:, rows, :]),
-                    (start_in.at[:, n, 1], start.at[:, n]),
-                    (kv_in.at[:, 1, rows, :], values.at[:, rows, :]),
-                ],
-                semaphores.at[pl.ds(7 * n, 7)],
-            )
-        )
+    core = lax.axis_index("core")
+    half_index = core if own_half else 1 - core
+    rows = pl.ds(pl.multiple_of(half_index * 128, 128), 128)
+    spans = pl.ds(half_index * 2, 2)
+    coming = begin(
+        [
+            (reach_in.at[:, spans], reach),
+            (queries_in.at[:, rows, :], queries),
+            (growth_in.at[:, rows, :], growth),
+            (scores_in.at[:, rows, :], scores),
+            (shrink_in.at[:, rows, :], shrink),
+            (start_in.at[:, spans, 1], start),
+            (kv_in.at[:, 1, rows, :], values),
+        ],
+        semaphores,
+    )
     for m in range(32):
         which, half, block = m // 16, (m // 8) % 2, m % 8
         piece = arrived[m].astype(F32)
@@ -352,36 +359,48 @@
             )
     own = own_head()
     gains = in_lanes(gain[...])
-    for n in range(SPANS):
-        finish(coming[n])
-        rows = slice(n * SPAN, (n + 1) * SPAN)
-        combined = jnp.zeros((SPAN, LANES), F32)
-        for direction in range(2):
-            lessen = expand(shrink[direction, rows, :], own)
-            reached = reach[direction, n]
-            grown = growth[direction, rows, :]
-            key_state = expand((reached * entering[direction, 0]).astype(BF16), own)
-            value_state = expand(
-                (start[direction, n].astype(F32) + reached * entering[direction, 1]).astype(BF16),
-                own,
-            )
-            total = scores[direction, rows, :] + grown * nt(queries[direction, rows, :], key_state)
-            powers = jnp.exp(total - head_max(total))
-            attend = powers / nn(powers.astype(BF16), own)
-            weighted = (attend * grown).astype(BF16)
-            mixing = jnp.where(seen_by(direction), nt(weighted, lessen), 0.0).astype(BF16)
-            result = nn(mixing, expand(values[direction, rows, :], own)) + nn(weighted, value_state)
-            mean = nn((result * result).astype(BF16), own) * (1.0 / 64.0)
-            combined = combined + result * lax.rsqrt(mean + EPSILON) * gains
-        out[rows, :] = combined.astype(BF16)
+    units = [(direction, n) for direction in range(2) for n in range(2)]
+    finish(coming[:4])
+    for direction, n in units:
+        span = slice(n * SPAN, (n + 1) * SPAN)
+        key_state = expand((reach[direction, n] * entering[direction, 0]).astype(BF16), own)
+        scores[direction, span, :] = scores[direction, span, :] + growth[
+            direction, span, :
+        ] * nt(queries[direction, span, :], key_state)
+    for direction in range(2):
+        total = scores[direction]
+        powers = jnp.exp(total - head_max(total))
+        attend = powers / nn(powers.astype(BF16), own)
+        weighted[direction] = (attend * growth[direction]).astype(BF16)
+    finish(coming[4:])
+    for direction, n in units:
+        span = slice(n * SPAN, (n + 1) * SPAN)
+        lessen = expand(shrink[direction, span, :], own)
+        mixed = jnp.where(seen_by(direction), nt(weighted[direction, span, :], lessen), 0.0)
+        mixing[direction, span, :] = mixed.astype(BF16)
+    for direction, n in units:
+        span = slice(n * SPAN, (n + 1) * SPAN)
+        state = start[direction, n].astype(F32) + reach[direction, n] * entering[direction, 1]
+        result[direction, span, :] = nn(
+            mixing[direction, span, :], expand(values[direction, span, :], own)
+        ) + nn(weighted[direction, span, :], expand(state.astype(BF16), own))
+    combined = jnp.zeros((128, LANES), F32)
+    for direction in range(2):
+        found = result[direction]
+        mean = nn((found * found).astype(BF16), own) * (1.0 / 64.0)
+        combined = combined + found * lax.rsqrt(mean + EPSILON) * gains
+    out[...] = combined.astype(BF16)
 
 
 def tail_kernel(
-    part0, part1, part2, part3, weight0, weight1, weight2, weight3, tokens_in, gain, up, down_in,
+    part0, part1, part2, part3, weight0, weight1, weight2, weight3, kept_in, passed_in, gain, up, down_in,
     base_out, out1, out2, out3, residual, update, tokens, down, semaphores,
 ):
     head = lax.axis_index("head")
-    coming = begin([(tokens_in, tokens), (down_in, down)], semaphores)
+    coming = begin(
+        [(kept_in, tokens.at[:, 0:128]), (passed_in, tokens.at[:, 128:256]), (down_in, down)],
+        semaphores,
+    )
     parts = (part0, part1, part2, part3)
     weights = (weight0, weight1, weight2, weight3)
     square = jnp.zeros((ROWS, 1), F32)
@@ -391,7 +410,7 @@
         for k in range(1, 4):
             total = total + nn(parts[k][...], weights[k][:, columns])
         if j == 0:
-            coming[0].wait()
+            finish(coming[:2])
         value = (tokens[j].astype(F32) + total).astype(BF16).astype(F32)
         residual[j] = value
         square = square + jnp.sum(value * value, axis=1, keepdims=True)
@@ -406,7 +425,7 @@
         ],
         axis=1,
     )
-    coming[1].wait()
+    coming[2].wait()
     for j in range(4):
         update[j] = nn(hidden, down[:, j * 256 : (j + 1) * 256])
     base_out[...] = residual[head] + update[head]
@@ -414,18 +433,14 @@
         out[...] = update[lax.rem(head + k, 4)].astype(BF16)
 
 
-def finish_kernel(base, part1, part2, part3, kept_out, sent_out):
+def finish_kernel(base, part1, part2, part3, out):
     core = lax.axis_index("core")
-
-    def rows_of(which):
-        rows = pl.ds(pl.multiple_of(which * 128, 128), 128)
-        total = base[rows, :]
-        for part in (part1, part2, part3):
-            total = total + part[rows, :].astype(F32)
-        return total.astype(BF16)
-
-    kept_out[...] = rows_of(core)
-    sent_out[...] = rows_of(1 - core)
+    total = base[...]
+    for part in (part1, part2, part3):
+        total = total + part[...].astype(F32)
+    total = total.astype(BF16)
+    out[core] = total[0:128]
+    out[1 - core] = total[128:256]
 
 
 def kernel(body, ins, outs, scratch=(), copies=0, flops=0):
@@ -481,29 +496,21 @@
 ):
     chips = lax.axis_size(CHIPS)
     swap_pairs = [(0, 1), (1, 0)]
-    swap, edge_a, edge_b, mine = kernel(
-        split_kernel,
+    edges, swap, mine = kernel(
+        edge_kernel,
         "hh",
-        [
-            ((136, 256), BF16, "v"),
-            ((8, 256), BF16, "v"),
-            ((8, 256), BF16, "v"),
-            ((128, 256), BF16, "v"),
-        ],
+        [((2, 8, 256), BF16, "v"), ((136, 256), BF16, "v"), ((128, 256), BF16, "v")],
         [((2, 128, 256), BF16), ((2, 128), F32)],
         copies=2,
     )(tokens, extra_forget_log)
     ahead = [(2 * i - 1, 2 * i) for i in range(1, chips)]
     behind = [(2 * i + 2, 2 * i + 1) for i in range(chips - 1)]
+    edges = lax.ppermute(edges, SEQ, ahead + behind)
+    swap, kept_edge = kernel(
+        swap_kernel, "vv", [((144, 256), BF16, "v"), ((8, 256), BF16, "v")]
+    )(swap, edges)
     other = lax.ppermute(swap, "core", swap_pairs)
-    halo_a = lax.ppermute(edge_a, SEQ, ahead + behind)
-    halo_b = lax.ppermute(
-        edge_b,
-        SEQ,
-        [(2 * i - 1, 2 * i + 1) for i in range(1, chips)]
-        + [(2 * i + 2, 2 * i) for i in range(chips - 1)],
-    )
-    rows = jnp.concatenate([mine, other[:128], halo_a, halo_b], axis=0)
+    rows = jnp.concatenate([mine, other[:128], kept_edge, other[136:]], axis=0)
     qkv_weight = jnp.transpose(query_key_value_weight, (1, 0, 2))
     rows, qkv_weight, gate_weight = lax.optimization_barrier(
         (rows, qkv_weight, forget_gate_weight)
@@ -520,7 +527,7 @@
     halves = (2, ROWS, LANES)
     starts = (2, SPANS, 2, SPAN, LANES)
     reaches = (2, SPANS, SPAN, LANES)
-    pieces, query, kv, cum, shrink, start, reach, whole_tokens = kernel(
+    pieces, query, kv, cum, shrink, start, reach, kept, passed = kernel(
         front_kernel,
         "v" * 11,
         [
@@ -531,7 +538,8 @@
             (halves, BF16, "h"),
             (starts, BF16, "h"),
             (reaches, F32, "h"),
-            ((4, ROWS, 256), BF16, "h"),
+            ((4, 128, 256), BF16, "h"),
+            ((4, 128, 256), BF16, "h"),
         ],
         [
             ((ROWS + 16, 768), F32),
@@ -542,9 +550,10 @@
             (halves, BF16),
             (starts, BF16),
             (reaches, F32),
-            ((4, ROWS, 256), BF16),
+            ((4, 128, 256), BF16),
+            ((4, 128, 256), BF16),
         ],
-        copies=7,
+        copies=8,
         flops=10**9,
     )(
         *parts,
@@ -554,12 +563,17 @@
         taps,
         slot_forget_rate,
         extra_forget_log,
-        other[128:],
-    )
-    pieces, out_weight = lax.optimization_barrier((pieces, output_projection_weight))
-    out_weights = [out_weight] + [shifted(out_weight, k) for k in (1, 2, 3)]
+        other[128:136],
+    )
+    pieces, out_weight, passed = lax.optimization_barrier(
+        (pieces, output_projection_weight, passed)
+    )
     held = lax.all_to_all(pieces, CHIPS, split_axis=0, concat_axis=0, tiled=True)
-    queries, scores, growth = kernel(
+    out_weights = [out_weight]
+    for k in (1, 2, 3):
+        out_weights.append(shifted(out_weight, k))
+    passed = lax.ppermute(passed, "core", swap_pairs)
+    meeting = kernel(
         meeting_kernel,
         "hhhhhv",
         [(halves, BF16, "h"), (halves, F32, "h"), (halves, F32, "h")],
@@ -576,32 +590,45 @@
         ],
         copies=8,
         flops=10**9,
-    )(query, kv, cum, shrink, start, taps)
+    )
+    queries, scores, growth = meeting(query, kv, cum, shrink, start, taps)
     (prefixes,) = kernel(
         scan_kernel, "v", [((chips, 16, 128), BF16, "v")], [((chips, 16, 128), F32)]
     )(held)
     arrived = lax.all_to_all(prefixes, CHIPS, split_axis=0, concat_axis=0, tiled=True)
-    (attention,) = kernel(
-        attention_kernel,
-        "hhhhhhhvv",
-        [((ROWS, LANES), BF16, "v")],
-        [
-            (halves, BF16),
-            (halves, BF16),
-            (halves, BF16),
-            (reaches, BF16),
-            (reaches, F32),
-            (halves, F32),
-            (halves, F32),
-            ((2, 2, SPAN, LANES), F32),
-        ],
-        copies=28,
-        flops=10**9,
-    )(queries, kv, shrink, start, reach, scores, growth, arrived, head_norm_gain)
+    half = (2, 128, LANES)
+    reached = (2, 2, SPAN, LANES)
+    attention = []
+    for own_half in (False, True):
+        attend = kernel(
+            functools.partial(attention_kernel, own_half),
+            "hhhhhhhvv",
+            [((128, LANES), BF16, "v")],
+            [
+                (half, BF16),
+                (half, BF16),
+                (half, BF16),
+                (reached, BF16),
+                (reached, F32),
+                (half, F32),
+                (half, F32),
+                (half, BF16),
+                (half, BF16),
+                (half, F32),
+                ((2, 2, SPAN, LANES), F32),
+            ],
+            copies=7,
+            flops=10**9,
+        )
+        attention += attend(
+            queries, kv, shrink, start, reach, scores, growth, arrived, head_norm_gain
+        )
+    swapped = lax.ppermute(attention[0], "core", swap_pairs)
+    attention = jnp.concatenate([attention[1], swapped], axis=0)
     attended = [attention] + [shifted(attention, k) for k in (1, 2, 3)]
     base, out1, out2, out3 = kernel(
         tail_kernel,
-        "v" * 8 + "hvvh",
+        "v" * 8 + "hhvvh",
         [((ROWS, 256), F32, "v")] + [((ROWS, 256), BF16, "v")] * 3,
         [
             ((4, ROWS, 256), F32),
@@ -609,22 +636,21 @@
             ((4, ROWS, 256), BF16),
             ((1024, 1024), BF16),
         ],
-        copies=2,
+        copies=3,
         flops=2 * 10**9,
     )(
         *attended,
         *out_weights,
-        whole_tokens,
+        kept,
+        passed,
         feedforward_norm_gain.reshape(8, 128),
         up_projection_weight,
         down_projection_weight,
     )
-    kept, sent = kernel(
-        finish_kernel, "vvvv", [((128, 256), BF16, "v"), ((128, 256), BF16, "v")]
-    )(base, shifted(out1, 1), shifted(out2, 2), shifted(out3, 3))
-    returned = lax.ppermute(sent, "core", swap_pairs)
-    first = lax.axis_index("core") == 0
-    return jnp.stack([jnp.where(first, kept, returned), jnp.where(first, returned, kept)])
+    (out,) = kernel(finish_kernel, "vvvv", [((2, 128, 256), BF16, "v")])(
+        base, shifted(out1, 1), shifted(out2, 2), shifted(out3, 3)
+    )
+    return out
 
 
 def solution(mesh):
@@ -645,6 +671,7 @@
         P(None, "head"),
         P("head", None),
     )
+
     return jax.shard_map(
         local, mesh=split, in_specs=placed, out_specs=P(None, SEQ, "head"), check_vma=False
     )

time: 96.8 us -> 96.6 us (level)
  blocking collectives: 0 us -> 21.1 us
  starting transfers between devices: 49.2 us -> 33.4 us
  Pallas kernels: 23 us -> 20 us
  waiting for transfers between devices: 23.3 us -> 21.5 us
    all_to_all x0 -> x1, blocking collectives: none -> 21.1 us  [local(): lax.all_to_all(pieces, CHIPS, split_axis=0, concat_axis=0, tiled=True)]
    all_to_all x1 -> x0, starting transfers between devices: 11.6 us -> none  [local(): lax.all_to_all(pieces, CHIPS, split_axis=0, concat_axis=0, tiled=True)]
    ppermute x12, waiting for transfers between devices: 10.4 us -> 19 us  [shifted(): lax.ppermute(value, 'head', [(j, (j + k) % count) for j in range(count)])]
    all_to_all x1 -> x0, waiting for transfers between devices: 5.73 us -> none  [local(): lax.all_to_all(pieces, CHIPS, split_axis=0, concat_axis=0, tiled=True)]
    all_to_all x1, waiting for transfers between devices: 5.57 us -> 0.01 us  [local(): lax.all_to_all(prefixes, CHIPS, split_axis=0, concat_axis=0, tiled=True)]
    ppermute x1, starting transfers between devices: 3.29 us -> 0.09 us  [local(): other = lax.ppermute(swap, 'core', swap_pairs)]
    pallas_call x8 -> x10, Pallas kernels: 23 us -> 20 us  [placed(): call(*[pltpu.with_memory_space_constraint(array, pltpu.HBM) if place == '...]
    ppermute x1, waiting for transfers between devices: 0.01 us -> 1.25 us  [local(): other = lax.ppermute(swap, 'core', swap_pairs)]
  transfers between devices with their start and end apart: 18 -> 17, of which waited for: 11 -> 8; matrix products, arithmetic and copies ran while one was open for 0% -> 0% of each run, Pallas kernels for 13% -> 10%
where the time goes in v3:
time: 96.6 us; the launch traced here: 96.3 us
  starting transfers between devices  33.4 us (35%)
  waiting for transfers between devices  21.5 us (22%)
  blocking collectives  21.1 us (22%)
  Pallas kernels  20 us (21%)
    all_to_all x1, blocking collectives, local(): lax.all_to_all(pieces, CHIPS, split_axis=0, concat_axis=0, tiled=True)  21.1 us
    pallas_call x10, Pallas kernels, placed(): call(*[pltpu.with_memory_space_constraint(array, pltpu.HBM) if place == '...  20 us
    ppermute x12, waiting for transfers between devices, shifted(): lax.ppermute(value, 'head', [(j, (j + k) % count) for j in range(count)])  19 us
    ppermute x12, starting transfers between devices, shifted(): lax.ppermute(value, 'head', [(j, (j + k) % count) for j in range(count)])  17.6 us
    ppermute x1, starting transfers between devices, local(): edges = lax.ppermute(edges, SEQ, ahead + behind)  4.92 us
    all_to_all x1, starting transfers between devices, local(): lax.all_to_all(prefixes, CHIPS, split_axis=0, concat_axis=0, tiled=True)  4.61 us
    ppermute x1, starting transfers between devices, local(): passed = lax.ppermute(passed, 'core', swap_pairs)  3.42 us
    ppermute x1, starting transfers between devices, local(): swapped = lax.ppermute(attention[0], 'core', swap_pairs)  2.69 us
  transfers between devices with their start and end apart: 17, of which 8 were waited for; matrix products, arithmetic and copies ran while one was open for 0% of the time, Pallas kernels for 10%

profile of v3, /device:TPU:1, one launch (start us, length us, event | category | flops | bytes accessed | tf_op | source)
XLA Modules:
  0.0 96.3 jit_solution(12005137513958451523)
XLA Ops:
  0.0 0.9 shard_map.118
  0.9 4.9 %collective-permute-start = (bf16[2,8,256]{2,1,0:T(8,128)(2,1)S(1)}, bf16[2,8,256]{2,1,0:T(8,128)(2,1)S(1)}, u32[]{:S(2)}, u32[]{:S(2)}) collective-permute-start(bf16[2,8,256]{2,1,0:T(8,128)(2,1)S(1)} %get-tuple-element.36), channel_id=1, source_target_pairs={{4,8},{12,16},{20,24},{28,32},{36,40},{44,48},{52,56},{60,64},{68,... | collective-permute-start | bytes 24584 | tf_op jit(solution)/shard_map/ppermute | solution.py:508
  5.9 1.3 %collective-permute-done.edges = bf16[2,8,256]{2,1,0:T(8,128)(2,1)S(1)} collective-permute-done((bf16[2,8,256]{2,1,0:T(8,128)(2,1)S(1)}, bf16[2,8,256]{2,1,0:T(8,128)(2,1)S(1)}, u32[]{:S(2)}, u32[]{:S(2)}) %collective-permute-start) | collective-permute-done | bytes 8224 | tf_op jit(solution)/shard_map/ppermute | solution.py:508
  7.2 0.0 copy-start
  7.2 0.0 copy-start.3
  7.2 0.0 copy-start.4
  7.2 0.0 copy-start.6
  7.2 0.1 collective-permute-start.1
  7.3 1.3 %collective-permute-done.1 = bf16[144,256]{1,0:T(8,128)(2,1)S(1)} collective-permute-done((bf16[144,256]{1,0:T(8,128)(2,1)S(1)}, bf16[144,256]{1,0:T(8,128)(2,1)S(1)}, u32[]{:S(2)}, u32[]{:S(2)}) %collective-permute-start.1) | collective-permute-done | bytes 73760 | tf_op jit(solution)/shard_map/ppermute | solution.py:512
  8.6 1.4 %collective-permute-start.2 = (bf16[272,256]{1,0:T(8,128)(2,1)S(1)}, bf16[272,256]{1,0:T(8,128)(2,1)S(1)}, u32[]{:S(2)}, u32[]{:S(2)}) collective-permute-start(bf16[272,256]{1,0:T(8,128)(2,1)S(1)} %pad_maximum_fusion.part0), channel_id=1, source_target_pairs={{0,1},{1,2},{2,3},{3,0},{4,5},{5,6},{6,7},{7,4},{8,9},{9,10},{10,1... | collective-permute-start | bytes 417800 | tf_op jit(solution)/shard_map/ppermute | solution.py:480
  10.0 2.6 %collective-permute-start.3 = (bf16[272,256]{1,0:T(8,128)(2,1)S(1)}, bf16[272,256]{1,0:T(8,128)(2,1)S(1)}, u32[]{:S(2)}, u32[]{:S(2)}) collective-permute-start(bf16[272,256]{1,0:T(8,128)(2,1)S(1)} %pad_maximum_fusion.part0), channel_id=1, source_target_pairs={{0,2},{1,3},{2,0},{3,1},{4,6},{5,7},{6,4},{7,5},{8,10},{9,11},{10,... | collective-permute-start | bytes 417800 | tf_op jit(solution)/shard_map/ppermute | solution.py:480
  12.6 1.1 %collective-permute-start.4 = (bf16[272,256]{1,0:T(8,128)(2,1)S(1)}, bf16[272,256]{1,0:T(8,128)(2,1)S(1)}, u32[]{:S(2)}, u32[]{:S(2)}) collective-permute-start(bf16[272,256]{1,0:T(8,128)(2,1)S(1)} %pad_maximum_fusion.part0), channel_id=1, source_target_pairs={{0,3},{1,0},{2,1},{3,2},{4,7},{5,4},{6,5},{7,6},{8,11},{9,8},{10,9... | collective-permute-start | bytes 417800 | tf_op jit(solution)/shard_map/ppermute | solution.py:480
  13.7 1.5 %shard_map.120 = (bf16[3,1024,256]{2,1,0:T(8,128)(2,1)S(1)}, bf16[1024,256]{1,0:T(8,128)(2,1)S(1)}) custom-call(bf16[3,1024,256]{2,1,0:T(8,128)(2,1)} %bitcast.8, bf16[1024,256]{1,0:T(8,128)(2,1)} %gate_weight), custom_call_target="tpu_custom_call" | custom-call | flops 1000000000 | bytes 1048576 | tf_op jit(solution)/shard_map/pallas_call | solution.py:468
  15.2 0.0 collective-permute-done.2.part1
  15.2 4.0 %collective-permute-done.3.part2 = bf16[272,256]{1,0:T(8,128)(2,1)S(1)} collective-permute-done((bf16[272,256]{1,0:T(8,128)(2,1)S(1)}, bf16[272,256]{1,0:T(8,128)(2,1)S(1)}, u32[]{:S(2)}, u32[]{:S(2)}) %collective-permute-start.3) | collective-permute-done | bytes 139296 | tf_op jit(solution)/shard_map/ppermute | solution.py:480
  19.2 0.0 collective-permute-done.4.part3
  19.2 0.0 copy-done
  19.2 0.0 copy-done.3
  19.2 0.0 copy-done.4
  19.2 0.0 copy-done.6
  19.2 0.0 copy-start.2
  19.3 4.1 %shard_map.121 = (bf16[32,24,128]{2,1,0:T(8,128)(2,1)S(1)}, bf16[272,256]{1,0:T(8,128)(2,1)}, bf16[2,2,256,256]{3,2,1,0:T(8,128)(2,1)}, f32[2,256,256]{2,1,0:T(8...) custom-call(bf16[272,256]{1,0:T(8,128)(2,1)S(1)} %pad_maximum_fusion, ...), custom_call_target="tpu_custom_call" | custom-call | flops 1000000000 | bytes 1048576 | tf_op jit(solution)/shard_map/pallas_call | solution.py:468
  23.4 21.1 %all_to_all.10.pieces = bf16[32,24,128]{2,1,0:T(8,128)(2,1)S(1)} all-to-all(bf16[32,24,128]{2,1,0:T(8,128)(2,1)S(1)} %get-tuple-element.55), channel_id=1, replica_groups=mesh['x'=4,'z'=8,'core'=2,'head'=4] {'x','z'}, dimensions={0} | all-to-all | bytes 393216 | tf_op jit(solution)/shard_map/all_to_all | solution.py:571
  44.4 0.0 copy-start.7
  44.4 0.8 shard_map.123
  45.2 4.6 %all-to-all-start.1 = ((bf16[32,16,128]{2,1,0:T(8,128)(2,1)}), bf16[32,16,128]{2,1,0:T(8,128)(2,1)S(1)}, u32[]{:S(2)}, u32[]{:S(2)}) async-start(bf16[32,16,128]{2,1,0:T(8,128)(2,1)} %shard_map.123), calls=%async_computation.1 | async-start | bytes 262144 | tf_op jit(solution)/shard_map/all_to_all | solution.py:598
  49.8 0.0 copy-done.2
  49.9 1.8 %collective-permute-start.10 = (bf16[256,1024]{1,0:T(8,128)(2,1)S(1)}, bf16[256,1024]{1,0:T(8,128)(2,1)S(1)}, u32[]{:S(2)}, u32[]{:S(2)}) collective-permute-start(bf16[256,1024]{1,0:T(8,128)(2,1)S(1)} %copy-done.2), channel_id=1, source_target_pairs={{0,2},{1,3},{2,0},{3,1},{4,6},{5,7},{6,4},{7,5},{8,10},{9,11},{10,... | collective-permute-start | bytes 1572872 | tf_op jit(solution)/shard_map/ppermute | solution.py:480
  51.6 1.7 %collective-permute-start.11 = (bf16[256,1024]{1,0:T(8,128)(2,1)S(1)}, bf16[256,1024]{1,0:T(8,128)(2,1)S(1)}, u32[]{:S(2)}, u32[]{:S(2)}) collective-permute-start(bf16[256,1024]{1,0:T(8,128)(2,1)S(1)} %copy-done.2), channel_id=1, source_target_pairs={{0,3},{1,0},{2,1},{3,2},{4,7},{5,4},{6,5},{7,6},{8,11},{9,8},{10,9... | collective-permute-start | bytes 1572872 | tf_op jit(solution)/shard_map/ppermute | solution.py:480
  53.4 0.0 collective-permute-start.9
  53.4 3.4 %collective-permute-start.12 = (bf16[4,128,256]{2,1,0:T(8,128)(2,1)}, bf16[4,128,256]{2,1,0:T(8,128)(2,1)S(1)}, u32[]{:S(2)}, u32[]{:S(2)}) collective-permute-start(bf16[4,128,256]{2,1,0:T(8,128)(2,1)} %get-tuple-element.58), channel_id=1, source_target_pairs={{0,4},{4,0},{1,5},{5,1},{2,6},{6,2},{3,7},{7,3},{8,12},{12,8},{9,1... | collective-permute-start | bytes 786440 | tf_op jit(solution)/shard_map/ppermute | solution.py:575
  56.8 3.4 %shard_map.122 = (bf16[2,256,256]{2,1,0:T(8,128)(2,1)}, f32[2,256,256]{2,1,0:T(8,128)}, f32[2,256,256]{2,1,0:T(8,128)}) custom-call(bf16[272,256]{1,0:T(8,128)(2,1)} %get-tuple-element.44.query_in, bf16[2,2,256,256]{3,2,1,0:T(8,128)(2,1)} %get-tuple-element.45.kv_in, f32[2,256,256]{2,1,0:T(8,128)} %get-tuple-element.46.cum_in, ...), custom_call_target="tpu_custom_call" | custom-call | flops 1000000000 | bytes 1048576 | tf_op jit(solution)/shard_map/pallas_call | solution.py:468
  60.2 0.0 all-to-all-done.1.arrived
  60.2 0.0 copy-done.7
  60.2 2.4 %shard_map.125 = bf16[128,256]{1,0:T(8,128)(2,1)S(1)} custom-call(bf16[2,256,256]{2,1,0:T(8,128)(2,1)} %get-tuple-element.49.queries_in, bf16[2,2,256,256]{3,2,1,0:T(8,128)(2,1)} %get-tuple-element.45.kv_in, bf16[2,256,256]{2,1,0:T(8,128)(2,1)} %get-tuple-element.47.shrink_in, bf16[2,4,2,64,256]{4,3,2,1,0:T(8,128)(2,1)} %get-tuple-element.48.start_in, ...), custom_call_target="tpu_custom_call" | custom-call | flops 1000000000 | bytes 1048576 | tf_op jit(solution)/shard_map/pallas_call | solution.py:468
  62.7 0.0 copy-start.1
  62.7 0.0 copy-start.5
  62.7 2.7 %collective-permute-start.5 = (bf16[128,256]{1,0:T(8,128)(2,1)S(1)}, bf16[128,256]{1,0:T(8,128)(2,1)S(1)}, u32[]{:S(2)}, u32[]{:S(2)}) collective-permute-start(bf16[128,256]{1,0:T(8,128)(2,1)S(1)} %shard_map.125), channel_id=1, source_target_pairs={{0,4},{4,0},{1,5},{5,1},{2,6},{6,2},{3,7},{7,3},{8,12},{12,8},{9,1... | collective-permute-start | bytes 196616 | tf_op jit(solution)/shard_map/ppermute | solution.py:626
  65.4 2.4 %shard_map.124 = bf16[128,256]{1,0:T(8,128)(2,1)S(1)} custom-call(bf16[2,256,256]{2,1,0:T(8,128)(2,1)} %get-tuple-element.49.queries_in, bf16[2,2,256,256]{3,2,1,0:T(8,128)(2,1)} %get-tuple-element.45.kv_in, bf16[2,256,256]{2,1,0:T(8,128)(2,1)} %get-tuple-element.47.shrink_in, bf16[2,4,2,64,256]{4,3,2,1,0:T(8,128)(2,1)} %get-tuple-element.48.start_in, ...), custom_call_target="tpu_custom_call" | custom-call | flops 1000000000 | bytes 1048576 | tf_op jit(solution)/shard_map/pallas_call | solution.py:468
  67.8 0.0 collective-permute-done.5
  67.8 1.1 %collective-permute-start.6 = (bf16[256,256]{1,0:T(8,128)(2,1)S(1)}, bf16[256,256]{1,0:T(8,128)(2,1)S(1)}, u32[]{:S(2)}, u32[]{:S(2)}) collective-permute-start(bf16[256,256]{1,0:T(8,128)(2,1)S(1)} %pad_maximum_fusion.1.part0), channel_id=1, source_target_pairs={{0,1},{1,2},{2,3},{3,0},{4,5},{5,6},{6,7},{7,4},{8,9},{9,10},{10,1... | collective-permute-start | bytes 393224 | tf_op jit(solution)/shard_map/ppermute | solution.py:480
  68.9 0.0 collective-permute-done.12.passed_in
  68.9 0.0 copy-start.8
  68.9 2.3 %collective-permute-start.7 = (bf16[256,256]{1,0:T(8,128)(2,1)S(1)}, bf16[256,256]{1,0:T(8,128)(2,1)S(1)}, u32[]{:S(2)}, u32[]{:S(2)}) collective-permute-start(bf16[256,256]{1,0:T(8,128)(2,1)S(1)} %pad_maximum_fusion.1.part0), channel_id=1, source_target_pairs={{0,2},{1,3},{2,0},{3,1},{4,6},{5,7},{6,4},{7,5},{8,10},{9,11},{10,... | collective-permute-start | bytes 393224 | tf_op jit(solution)/shard_map/ppermute | solution.py:480
  71.2 0.0 collective-permute-done.10.weight2
  71.2 0.9 collective-permute-start.8
  72.1 4.9 %collective-permute-done.11.weight3 = bf16[256,1024]{1,0:T(8,128)(2,1)S(1)} collective-permute-done((bf16[256,1024]{1,0:T(8,128)(2,1)S(1)}, bf16[256,1024]{1,0:T(8,128)(2,1)S(1)}, u32[]{:S(2)}, u32[]{:S(2)}) %collective-permute-start.11) | collective-permute-done | bytes 524320 | tf_op jit(solution)/shard_map/ppermute | solution.py:480
  77.0 0.0 collective-permute-done.9.weight1
  77.0 3.8 %collective-permute-done.6.part1 = bf16[256,256]{1,0:T(8,128)(2,1)S(1)} collective-permute-done((bf16[256,256]{1,0:T(8,128)(2,1)S(1)}, bf16[256,256]{1,0:T(8,128)(2,1)S(1)}, u32[]{:S(2)}, u32[]{:S(2)}) %collective-permute-start.6) | collective-permute-done | bytes 131104 | tf_op jit(solution)/shard_map/ppermute | solution.py:480
  80.7 0.0 collective-permute-done.7.part2
  80.7 0.4 collective-permute-done.8.part3
  81.2 0.0 copy-done.8
  81.2 0.0 copy-done.1
  81.2 0.0 copy-done.5
  81.2 3.6 %shard_map.126 = (f32[256,256]{1,0:T(8,128)S(1)}, bf16[256,256]{1,0:T(8,128)(2,1)S(1)}, bf16[256,256]{1,0:T(8,128)(2,1)S(1)}, bf16[256,256]{1,0:T(8,128)(2,1)S(1)}) custom-call(bf16[256,256]{1,0:T(8,128)(2,1)S(1)} %pad_maximum_fusion.1.part0, bf16[256,256]{1,0:T(8,128)(2,1)S(1)} %collective-permute-done.6.part1, ...), custom_call_target="tpu_custom_call" | custom-call | flops 2000000000 | bytes 1048576 | tf_op jit(solution)/shard_map/pallas_call | solution.py:468
  84.8 2.1 %collective-permute-start.13 = (bf16[256,256]{1,0:T(8,128)(2,1)S(1)}, bf16[256,256]{1,0:T(8,128)(2,1)S(1)}, u32[]{:S(2)}, u32[]{:S(2)}) collective-permute-start(bf16[256,256]{1,0:T(8,128)(2,1)S(1)} %get-tuple-element.60), channel_id=1, source_target_pairs={{0,1},{1,2},{2,3},{3,0},{4,5},{5,6},{6,7},{7,4},{8,9},{9,10},{10,1... | collective-permute-start | bytes 393224 | tf_op jit(solution)/shard_map/ppermute | solution.py:480
  86.9 2.7 %collective-permute-start.14 = (bf16[256,256]{1,0:T(8,128)(2,1)S(1)}, bf16[256,256]{1,0:T(8,128)(2,1)S(1)}, u32[]{:S(2)}, u32[]{:S(2)}) collective-permute-start(bf16[256,256]{1,0:T(8,128)(2,1)S(1)} %get-tuple-element.61), channel_id=1, source_target_pairs={{0,2},{1,3},{2,0},{3,1},{4,6},{5,7},{6,4},{7,5},{8,10},{9,11},{10,... | collective-permute-start | bytes 393224 | tf_op jit(solution)/shard_map/ppermute | solution.py:480
  89.6 0.0 collective-permute-start.15
  89.6 1.6 %collective-permute-done.13.part1 = bf16[256,256]{1,0:T(8,128)(2,1)S(1)} collective-permute-done((bf16[256,256]{1,0:T(8,128)(2,1)S(1)}, bf16[256,256]{1,0:T(8,128)(2,1)S(1)}, u32[]{:S(2)}, u32[]{:S(2)}) %collective-permute-start.13) | collective-permute-done | bytes 131104 | tf_op jit(solution)/shard_map/ppermute | solution.py:480
  91.2 4.3 %collective-permute-done.14.part2 = bf16[256,256]{1,0:T(8,128)(2,1)S(1)} collective-permute-done((bf16[256,256]{1,0:T(8,128)(2,1)S(1)}, bf16[256,256]{1,0:T(8,128)(2,1)S(1)}, u32[]{:S(2)}, u32[]{:S(2)}) %collective-permute-start.14) | collective-permute-done | bytes 131104 | tf_op jit(solution)/shard_map/ppermute | solution.py:480
  95.5 0.0 collective-permute-done.15.part3
  95.5 0.7 shard_map.127
  (5 shorter events, 0.0 us)
Async XLA Ops:
  0.9 6.3 %collective-permute-start = (bf16[2,8,256]{2,1,0:T(8,128)(2,1)S(1)}, bf16[2,8,256]{2,1,0:T(8,128)(2,1)S(1)}, u32[]{:S(2)}, u32[]{:S(2)}) collective-permute-start(bf16[2,8,256]{2,1,0:T(8,128)(2,1)S(1)} %get-tuple-element.36), channel_id=1, source_target_pairs={{4,8},{12,16},{20,24},{28,32},{36,40},{44,48},{52,56},{60,64},{68,... | collective-permute-start | bytes 24584 | tf_op jit(solution)/shard_map/ppermute | solution.py:508
  7.2 12.0 %copy-start = (f32[2,128]{1,0:T(2,128)S(1)}, f32[2,128]{1,0:T(2,128)}, u32[]{:S(2)}) copy-start(f32[2,128]{1,0:T(2,128)} %extra.1) | copy-start | bytes 3076
  7.2 12.0 %copy-start.3 = (f32[2,4,3,256]{3,1,2,0:T(4,128)S(1)}, f32[2,4,3,256]{3,1,2,0:T(4,128)}, u32[]{:S(2)}) copy-start(f32[2,4,3,256]{3,1,2,0:T(4,128)} %param.16) | copy-start | bytes 73732
  7.2 12.0 %copy-start.4 = (f32[1024]{0:T(1024)S(1)}, f32[1024]{0:T(1024)}, u32[]{:S(2)}) copy-start(f32[1024]{0:T(1024)} %param.13) | copy-start | bytes 12292
  7.2 12.0 %copy-start.6 = (f32[4,64]{1,0:T(4,128)S(1)}, f32[4,64]{1,0:T(4,128)}, u32[]{:S(2)}) copy-start(f32[4,64]{1,0:T(4,128)} %rate.1) | copy-start | bytes 3076
  7.2 1.4 %collective-permute-start.1 = (bf16[144,256]{1,0:T(8,128)(2,1)S(1)}, bf16[144,256]{1,0:T(8,128)(2,1)S(1)}, u32[]{:S(2)}, u32[]{:S(2)}) collective-permute-start(bf16[144,256]{1,0:T(8,128)(2,1)S(1)} %get-tuple-element.37), channel_id=1, source_target_pairs={{0,4},{4,0},{1,5},{5,1},{2,6},{6,2},{3,7},{7,3},{8,12},{12,8},{9,1... | collective-permute-start | bytes 221192 | tf_op jit(solution)/shard_map/ppermute | solution.py:512
  8.6 6.6 %collective-permute-start.2 = (bf16[272,256]{1,0:T(8,128)(2,1)S(1)}, bf16[272,256]{1,0:T(8,128)(2,1)S(1)}, u32[]{:S(2)}, u32[]{:S(2)}) collective-permute-start(bf16[272,256]{1,0:T(8,128)(2,1)S(1)} %pad_maximum_fusion.part0), channel_id=1, source_target_pairs={{0,1},{1,2},{2,3},{3,0},{4,5},{5,6},{6,7},{7,4},{8,9},{9,10},{10,1... | collective-permute-start | bytes 417800 | tf_op jit(solution)/shard_map/ppermute | solution.py:480
  10.0 9.2 %collective-permute-start.3 = (bf16[272,256]{1,0:T(8,128)(2,1)S(1)}, bf16[272,256]{1,0:T(8,128)(2,1)S(1)}, u32[]{:S(2)}, u32[]{:S(2)}) collective-permute-start(bf16[272,256]{1,0:T(8,128)(2,1)S(1)} %pad_maximum_fusion.part0), channel_id=1, source_target_pairs={{0,2},{1,3},{2,0},{3,1},{4,6},{5,7},{6,4},{7,5},{8,10},{9,11},{10,... | collective-permute-start | bytes 417800 | tf_op jit(solution)/shard_map/ppermute | solution.py:480
  12.6 6.6 %collective-permute-start.4 = (bf16[272,256]{1,0:T(8,128)(2,1)S(1)}, bf16[272,256]{1,0:T(8,128)(2,1)S(1)}, u32[]{:S(2)}, u32[]{:S(2)}) collective-permute-start(bf16[272,256]{1,0:T(8,128)(2,1)S(1)} %pad_maximum_fusion.part0), channel_id=1, source_target_pairs={{0,3},{1,0},{2,1},{3,2},{4,7},{5,4},{6,5},{7,6},{8,11},{9,8},{10,9... | collective-permute-start | bytes 417800 | tf_op jit(solution)/shard_map/ppermute | solution.py:480
  19.2 30.6 %copy-start.2 = (bf16[256,1024]{1,0:T(8,128)(2,1)S(1)}, bf16[256,1024]{1,0:T(8,128)(2,1)}, u32[]{:S(2)}) copy-start(bf16[256,1024]{1,0:T(8,128)(2,1)} %weight0) | copy-start | bytes 1572868
  44.4 15.8 %copy-start.7 = (f32[4,64]{1,0:T(4,128)S(1)}, f32[4,64]{1,0:T(4,128)}, u32[]{:S(2)}) copy-start(f32[4,64]{1,0:T(4,128)} %gain.3) | copy-start | bytes 3076
  45.2 15.0 %all-to-all-start.1 = ((bf16[32,16,128]{2,1,0:T(8,128)(2,1)}), bf16[32,16,128]{2,1,0:T(8,128)(2,1)S(1)}, u32[]{:S(2)}, u32[]{:S(2)}) async-start(bf16[32,16,128]{2,1,0:T(8,128)(2,1)} %shard_map.123), calls=%async_computation.1 | async-start | bytes 262144 | tf_op jit(solution)/shard_map/all_to_all | solution.py:598
  49.9 21.3 %collective-permute-start.10 = (bf16[256,1024]{1,0:T(8,128)(2,1)S(1)}, bf16[256,1024]{1,0:T(8,128)(2,1)S(1)}, u32[]{:S(2)}, u32[]{:S(2)}) collective-permute-start(bf16[256,1024]{1,0:T(8,128)(2,1)S(1)} %copy-done.2), channel_id=1, source_target_pairs={{0,2},{1,3},{2,0},{3,1},{4,6},{5,7},{6,4},{7,5},{8,10},{9,11},{10,... | collective-permute-start | bytes 1572872 | tf_op jit(solution)/shard_map/ppermute | solution.py:480
  51.6 25.3 %collective-permute-start.11 = (bf16[256,1024]{1,0:T(8,128)(2,1)S(1)}, bf16[256,1024]{1,0:T(8,128)(2,1)S(1)}, u32[]{:S(2)}, u32[]{:S(2)}) collective-permute-start(bf16[256,1024]{1,0:T(8,128)(2,1)S(1)} %copy-done.2), channel_id=1, source_target_pairs={{0,3},{1,0},{2,1},{3,2},{4,7},{5,4},{6,5},{7,6},{8,11},{9,8},{10,9... | collective-permute-start | bytes 1572872 | tf_op jit(solution)/shard_map/ppermute | solution.py:480
  53.4 23.6 %collective-permute-start.9 = (bf16[256,1024]{1,0:T(8,128)(2,1)S(1)}, bf16[256,1024]{1,0:T(8,128)(2,1)S(1)}, u32[]{:S(2)}, u32[]{:S(2)}) collective-permute-start(bf16[256,1024]{1,0:T(8,128)(2,1)S(1)} %copy-done.2), channel_id=1, source_target_pairs={{0,1},{1,2},{2,3},{3,0},{4,5},{5,6},{6,7},{7,4},{8,9},{9,10},{10,1... | collective-permute-start | bytes 1572872 | tf_op jit(solution)/shard_map/ppermute | solution.py:480
  53.4 15.5 %collective-permute-start.12 = (bf16[4,128,256]{2,1,0:T(8,128)(2,1)}, bf16[4,128,256]{2,1,0:T(8,128)(2,1)S(1)}, u32[]{:S(2)}, u32[]{:S(2)}) collective-permute-start(bf16[4,128,256]{2,1,0:T(8,128)(2,1)} %get-tuple-element.58), channel_id=1, source_target_pairs={{0,4},{4,0},{1,5},{5,1},{2,6},{6,2},{3,7},{7,3},{8,12},{12,8},{9,1... | collective-permute-start | bytes 786440 | tf_op jit(solution)/shard_map/ppermute | solution.py:575
  62.7 18.5 %copy-start.1 = (bf16[1024,1024]{1,0:T(8,128)(2,1)S(1)}, bf16[1024,1024]{1,0:T(8,128)(2,1)}, u32[]{:S(2)}) copy-start(bf16[1024,1024]{1,0:T(8,128)(2,1)} %up.1) | copy-start | bytes 6291460
  62.7 18.5 %copy-start.5 = (f32[1024]{0:T(1024)S(1)}, f32[1024]{0:T(1024)}, u32[]{:S(2)}) copy-start(f32[1024]{0:T(1024)} %param.21) | copy-start | bytes 12292
  62.7 5.1 %collective-permute-start.5 = (bf16[128,256]{1,0:T(8,128)(2,1)S(1)}, bf16[128,256]{1,0:T(8,128)(2,1)S(1)}, u32[]{:S(2)}, u32[]{:S(2)}) collective-permute-start(bf16[128,256]{1,0:T(8,128)(2,1)S(1)} %shard_map.125), channel_id=1, source_target_pairs={{0,4},{4,0},{1,5},{5,1},{2,6},{6,2},{3,7},{7,3},{8,12},{12,8},{9,1... | collective-permute-start | bytes 196616 | tf_op jit(solution)/shard_map/ppermute | solution.py:626
  67.8 12.9 %collective-permute-start.6 = (bf16[256,256]{1,0:T(8,128)(2,1)S(1)}, bf16[256,256]{1,0:T(8,128)(2,1)S(1)}, u32[]{:S(2)}, u32[]{:S(2)}) collective-permute-start(bf16[256,256]{1,0:T(8,128)(2,1)S(1)} %pad_maximum_fusion.1.part0), channel_id=1, source_target_pairs={{0,1},{1,2},{2,3},{3,0},{4,5},{5,6},{6,7},{7,4},{8,9},{9,10},{10,1... | collective-permute-start | bytes 393224 | tf_op jit(solution)/shard_map/ppermute | solution.py:480
  68.9 12.3 %copy-start.8 = (bf16[4,128,256]{2,1,0:T(8,128)(2,1)}, bf16[4,128,256]{2,1,0:T(8,128)(2,1)S(1)}, u32[]{:S(2)}) copy-start(bf16[4,128,256]{2,1,0:T(8,128)(2,1)S(1)} %collective-permute-done.12.passed_in) | copy-start | bytes 786436
  68.9 11.8 %collective-permute-start.7 = (bf16[256,256]{1,0:T(8,128)(2,1)S(1)}, bf16[256,256]{1,0:T(8,128)(2,1)S(1)}, u32[]{:S(2)}, u32[]{:S(2)}) collective-permute-start(bf16[256,256]{1,0:T(8,128)(2,1)S(1)} %pad_maximum_fusion.1.part0), channel_id=1, source_target_pairs={{0,2},{1,3},{2,0},{3,1},{4,6},{5,7},{6,4},{7,5},{8,10},{9,11},{10,... | collective-permute-start | bytes 393224 | tf_op jit(solution)/shard_map/ppermute | solution.py:480
  71.2 10.0 %collective-permute-start.8 = (bf16[256,256]{1,0:T(8,128)(2,1)S(1)}, bf16[256,256]{1,0:T(8,128)(2,1)S(1)}, u32[]{:S(2)}, u32[]{:S(2)}) collective-permute-start(bf16[256,256]{1,0:T(8,128)(2,1)S(1)} %pad_maximum_fusion.1.part0), channel_id=1, source_target_pairs={{0,3},{1,0},{2,1},{3,2},{4,7},{5,4},{6,5},{7,6},{8,11},{9,8},{10,9... | collective-permute-start | bytes 393224 | tf_op jit(solution)/shard_map/ppermute | solution.py:480
  84.8 6.4 %collective-permute-start.13 = (bf16[256,256]{1,0:T(8,128)(2,1)S(1)}, bf16[256,256]{1,0:T(8,128)(2,1)S(1)}, u32[]{:S(2)}, u32[]{:S(2)}) collective-permute-start(bf16[256,256]{1,0:T(8,128)(2,1)S(1)} %get-tuple-element.60), channel_id=1, source_target_pairs={{0,1},{1,2},{2,3},{3,0},{4,5},{5,6},{6,7},{7,4},{8,9},{9,10},{10,1... | collective-permute-start | bytes 393224 | tf_op jit(solution)/shard_map/ppermute | solution.py:480
  86.9 8.6 %collective-permute-start.14 = (bf16[256,256]{1,0:T(8,128)(2,1)S(1)}, bf16[256,256]{1,0:T(8,128)(2,1)S(1)}, u32[]{:S(2)}, u32[]{:S(2)}) collective-permute-start(bf16[256,256]{1,0:T(8,128)(2,1)S(1)} %get-tuple-element.61), channel_id=1, source_target_pairs={{0,2},{1,3},{2,0},{3,1},{4,6},{5,7},{6,4},{7,5},{8,10},{9,11},{10,... | collective-permute-start | bytes 393224 | tf_op jit(solution)/shard_map/ppermute | solution.py:480
  89.6 5.9 %collective-permute-start.15 = (bf16[256,256]{1,0:T(8,128)(2,1)S(1)}, bf16[256,256]{1,0:T(8,128)(2,1)S(1)}, u32[]{:S(2)}, u32[]{:S(2)}) collective-permute-start(bf16[256,256]{1,0:T(8,128)(2,1)S(1)} %get-tuple-element.62), channel_id=1, source_target_pairs={{0,3},{1,0},{2,1},{3,2},{4,7},{5,4},{6,5},{7,6},{8,11},{9,8},{10,9... | collective-permute-start | bytes 393224 | tf_op jit(solution)/shard_map/ppermute | solution.py:480

commit v4 on v3

--- a/solution.py
+++ b/solution.py
@@ -14,7 +14,6 @@
 EPSILON = 1e-06
 BF16 = jnp.bfloat16
 F32 = jnp.float32
-HIGHEST = lax.Precision.HIGHEST
 SPAN = 64
 ROWS = 256
 LANES = 256
@@ -64,6 +63,16 @@
     for k in (6, 5, 4, 3, 2):
         series = 1.0 + x * (1.0 / k) * series
     return jnp.where(x > -0.3, -x * series, 1.0 - jnp.exp(x))
+
+
+def exact(matmul, values, zeros_and_ones):
+    high = values.astype(BF16)
+    rest = values - high.astype(F32)
+    middle = rest.astype(BF16)
+    low = (rest - middle.astype(F32)).astype(BF16)
+    return (
+        matmul(low, zeros_and_ones) + matmul(middle, zeros_and_ones)
+    ) + matmul(high, zeros_and_ones)
 
 
 def as_column(row):
@@ -96,8 +105,32 @@
     )
 
 
-def warm_kernel(qkv_weight, gate_weight, qkv_out, gate_out, semaphores):
-    finish(begin([(qkv_weight, qkv_out), (gate_weight, gate_out)], semaphores))
+def warm_kernel(qkv_weight, gate_weight, out_weight, qkv_out, gate_out, half_out, semaphores):
+    rows = pl.ds(pl.multiple_of(lax.axis_index("core") * 128, 128), 128)
+    finish(
+        begin(
+            [
+                (qkv_weight, qkv_out),
+                (gate_weight, gate_out),
+                (out_weight.at[rows, :], half_out),
+            ],
+            semaphores,
+        )
+    )
+
+
+def warm_tail_kernel(
+    weight0, mine1, mine2, mine3, theirs1, theirs2, theirs3, kept, passed, down,
+    weights_out, tokens_out, down_out, semaphores,
+):
+    core = lax.axis_index("core")
+    own = pl.ds(pl.multiple_of(core * 128, 128), 128)
+    other = pl.ds(pl.multiple_of((1 - core) * 128, 128), 128)
+    pairs = [(weight0, weights_out.at[0])]
+    for k, mine, theirs in ((1, mine1, theirs1), (2, mine2, theirs2), (3, mine3, theirs3)):
+        pairs += [(mine, weights_out.at[k, own]), (theirs, weights_out.at[k, other])]
+    pairs += [(kept, tokens_out.at[:, 0:128]), (passed, tokens_out.at[:, 128:256])]
+    finish(begin(pairs + [(down, down_out)], semaphores))
 
 
 def edge_kernel(tokens_in, extra_in, edge_out, swap_out, mine_out, tokens, extra, semaphores):
@@ -187,32 +220,35 @@
     inflow = minus_expm1(log_decay)
     row, col = iota((ROWS, ROWS), 0), iota((ROWS, ROWS), 1)
     same = (row // SPAN) == (col // SPAN)
-    earlier = (same & (col <= row)).astype(F32)
-    later = (same & (col >= row)).astype(F32)
-    spans = (iota((ROWS, 128 * SPANS), 0) // SPAN == iota((ROWS, 128 * SPANS), 1) // 128).astype(F32)
+    earlier = (same & (col <= row)).astype(BF16)
+    later = (same & (col >= row)).astype(BF16)
+    spans = (iota((ROWS, 128 * SPANS), 0) // SPAN == iota((ROWS, 128 * SPANS), 1) // 128).astype(BF16)
     for direction in range(2):
-        cum[direction] = nn(later if direction else earlier, log_decay, HIGHEST)
+        order = later if direction else earlier
+        cum[direction] = exact(lambda part, ones: nn(ones, part), log_decay, order)
         shrink[direction] = (jnp.exp(-cum[direction]) * inflow).astype(BF16)
     going += begin([(cum, cum_out), (shrink, shrink_out)], semaphores.at[pl.ds(4, 2)])
-    span_totals = tn(log_decay, spans, HIGHEST)
+    span_totals = exact(tn, log_decay, spans)
     totals = [compact_rows(span_totals[:, n * 128 : (n + 1) * 128]) for n in range(SPANS)]
     factors = [jnp.exp(total) for total in totals]
+    units = [(direction, n) for direction in range(2) for n in range(SPANS)]
+    added = {}
+    for direction, n in units:
+        rows = slice(n * SPAN, (n + 1) * SPAN)
+        local = cum[direction, rows, :]
+        last = local[0:1] if direction else local[SPAN - 1 : SPAN]
+        remain = (jnp.exp(last - local) * inflow[rows]).astype(BF16)
+        for which in range(2):
+            added[direction, n, which] = compact(tn(remain, kv[direction, which, rows, :]))
     ends = []
     for direction in range(2):
-        cumulative = cum[direction]
         states = [jnp.zeros((SPAN, LANES), F32), jnp.zeros((SPAN, LANES), F32)]
         passed = jnp.zeros((SPAN, LANES), F32)
         for n in reversed(range(SPANS)) if direction else range(SPANS):
-            rows = slice(n * SPAN, (n + 1) * SPAN)
-            start[direction, n, 0] = states[0].astype(BF16)
-            start[direction, n, 1] = states[1].astype(BF16)
             reach[direction, n] = jnp.exp(passed)
-            local = cumulative[rows]
-            last = local[0:1] if direction else local[SPAN - 1 : SPAN]
-            remain = (jnp.exp(last - local) * inflow[rows]).astype(BF16)
             for which in range(2):
-                added = compact(tn(remain, kv[direction, which, rows, :]))
-                states[which] = factors[n] * states[which] + added
+                start[direction, n, which] = states[which].astype(BF16)
+                states[which] = factors[n] * states[which] + added[direction, n, which]
             passed = passed + totals[n]
         ends.append(states)
     going += begin([(start, start_out), (reach, reach_out)], semaphores.at[pl.ds(6, 2)])
@@ -393,24 +429,17 @@
 
 
 def tail_kernel(
-    part0, part1, part2, part3, weight0, weight1, weight2, weight3, kept_in, passed_in, gain, up, down_in,
-    base_out, out1, out2, out3, residual, update, tokens, down, semaphores,
+    part0, part1, part2, part3, weights, tokens, gain, up, down,
+    base_out, out1, out2, out3, residual, update,
 ):
     head = lax.axis_index("head")
-    coming = begin(
-        [(kept_in, tokens.at[:, 0:128]), (passed_in, tokens.at[:, 128:256]), (down_in, down)],
-        semaphores,
-    )
     parts = (part0, part1, part2, part3)
-    weights = (weight0, weight1, weight2, weight3)
     square = jnp.zeros((ROWS, 1), F32)
     for j in range(4):
         columns = slice(j * 256, (j + 1) * 256)
-        total = nn(parts[0][...], weights[0][:, columns])
+        total = nn(parts[0][...], weights[0, :, columns])
         for k in range(1, 4):
-            total = total + nn(parts[k][...], weights[k][:, columns])
-        if j == 0:
-            finish(coming[:2])
+            total = total + nn(parts[k][...], weights[k, :, columns])
         value = (tokens[j].astype(F32) + total).astype(BF16).astype(F32)
         residual[j] = value
         square = square + jnp.sum(value * value, axis=1, keepdims=True)
@@ -425,7 +454,6 @@
         ],
         axis=1,
     )
-    coming[2].wait()
     for j in range(4):
         update[j] = nn(hidden, down[:, j * 256 : (j + 1) * 256])
     base_out[...] = residual[head] + update[head]
@@ -512,17 +540,21 @@
     other = lax.ppermute(swap, "core", swap_pairs)
     rows = jnp.concatenate([mine, other[:128], kept_edge, other[136:]], axis=0)
     qkv_weight = jnp.transpose(query_key_value_weight, (1, 0, 2))
-    rows, qkv_weight, gate_weight = lax.optimization_barrier(
-        (rows, qkv_weight, forget_gate_weight)
+    rows, qkv_weight, gate_weight, out_weight = lax.optimization_barrier(
+        (rows, qkv_weight, forget_gate_weight, output_projection_weight)
     )
     parts = [rows] + [shifted(rows, k) for k in (1, 2, 3)]
-    qkv_weight, gate_weight = kernel(
+    qkv_weight, gate_weight, half_weight = kernel(
         warm_kernel,
-        "hh",
-        [((3, 1024, 256), BF16, "v"), ((1024, 256), BF16, "v")],
-        copies=2,
+        "hhh",
+        [
+            ((3, 1024, 256), BF16, "v"),
+            ((1024, 256), BF16, "v"),
+            ((128, 1024), BF16, "v"),
+        ],
+        copies=3,
         flops=10**9,
-    )(qkv_weight, gate_weight)
+    )(qkv_weight, gate_weight, out_weight)
     taps = jnp.transpose(convolution_filter_taps, (0, 2, 1, 3))
     halves = (2, ROWS, LANES)
     starts = (2, SPANS, 2, SPAN, LANES)
@@ -565,13 +597,12 @@
         extra_forget_log,
         other[128:136],
     )
-    pieces, out_weight, passed = lax.optimization_barrier(
-        (pieces, output_projection_weight, passed)
-    )
+    pieces, half_weight, passed = lax.optimization_barrier((pieces, half_weight, passed))
     held = lax.all_to_all(pieces, CHIPS, split_axis=0, concat_axis=0, tiled=True)
-    out_weights = [out_weight]
+    own_weights, other_weights = [], []
     for k in (1, 2, 3):
-        out_weights.append(shifted(out_weight, k))
+        own_weights.append(shifted(half_weight, k))
+        other_weights.append(lax.ppermute(own_weights[-1], "core", swap_pairs))
     passed = lax.ppermute(passed, "core", swap_pairs)
     meeting = kernel(
         meeting_kernel,
@@ -625,27 +656,37 @@
         )
     swapped = lax.ppermute(attention[0], "core", swap_pairs)
     attention = jnp.concatenate([attention[1], swapped], axis=0)
-    attended = [attention] + [shifted(attention, k) for k in (1, 2, 3)]
+    attention, down_weight = lax.optimization_barrier((attention, down_projection_weight))
+    attended = [attention]
+    for k in (1, 2, 3):
+        attended.append(shifted(attention, k))
+    warm_tail = kernel(
+        warm_tail_kernel,
+        "h" * 10,
+        [
+            ((4, 256, 1024), BF16, "v"),
+            ((4, ROWS, 256), BF16, "v"),
+            ((1024, 1024), BF16, "v"),
+        ],
+        copies=10,
+        flops=10**9,
+    )
+    weights, whole_tokens, down_weight = warm_tail(
+        output_projection_weight, *own_weights, *other_weights, kept, passed, down_weight
+    )
     base, out1, out2, out3 = kernel(
         tail_kernel,
-        "v" * 8 + "hhvvh",
+        "v" * 9,
         [((ROWS, 256), F32, "v")] + [((ROWS, 256), BF16, "v")] * 3,
-        [
-            ((4, ROWS, 256), F32),
-            ((4, ROWS, 256), F32),
-            ((4, ROWS, 256), BF16),
-            ((1024, 1024), BF16),
-        ],
-        copies=3,
+        [((4, ROWS, 256), F32), ((4, ROWS, 256), F32)],
         flops=2 * 10**9,
     )(
         *attended,
-        *out_weights,
-        kept,
-        passed,
+        weights,
+        whole_tokens,
         feedforward_norm_gain.reshape(8, 128),
         up_projection_weight,
-        down_projection_weight,
+        down_weight,
     )
     (out,) = kernel(finish_kernel, "vvvv", [((2, 128, 256), BF16, "v")])(
         base, shifted(out1, 1), shifted(out2, 2), shifted(out3, 3)

time: 96.6 us -> 91.7 us (0.949)
  blocking collectives: 21.1 us -> 0 us
  starting transfers between devices: 33.4 us -> 46.7 us
  Pallas kernels: 20 us -> 21.9 us
    all_to_all x1 -> x0, blocking collectives: 21.1 us -> none  [local(): lax.all_to_all(pieces, CHIPS, split_axis=0, concat_axis=0, tiled=True)]
    all_to_all x0 -> x1, starting transfers between devices: none -> 11.9 us  [local(): lax.all_to_all(pieces, CHIPS, split_axis=0, concat_axis=0, tiled=True)]
    ppermute x12, waiting for transfers between devices: 19 us -> 11.7 us  [shifted(): lax.ppermute(value, 'head', [(j, (j + k) % count) for j in range(count)])]
    all_to_all x0 -> x1, waiting for transfers between devices: none -> 5.18 us  [local(): lax.all_to_all(pieces, CHIPS, split_axis=0, concat_axis=0, tiled=True)]
    all_to_all x1, waiting for transfers between devices: 0.01 us -> 2.19 us  [local(): lax.all_to_all(prefixes, CHIPS, split_axis=0, concat_axis=0, tiled=True)]
    pallas_call x10 -> x11, Pallas kernels: 20 us -> 21.9 us  [placed(): call(*[pltpu.with_memory_space_constraint(array, pltpu.HBM) if place == '...]
    ppermute x1, starting transfers between devices: 2.69 us -> 3.94 us  [local(): swapped = lax.ppermute(attention[0], 'core', swap_pairs)]
  transfers between devices with their start and end apart: 17 -> 21, of which waited for: 8 -> 8; matrix products, arithmetic and copies ran while one was open for 0% -> 0% of each run, Pallas kernels for 10% -> 14%
where the time goes in v4:
time: 91.7 us; the launch traced here: 91.4 us
  starting transfers between devices  46.7 us (51%)
  Pallas kernels  21.9 us (24%)
  waiting for transfers between devices  21.7 us (24%)
    pallas_call x11, Pallas kernels, placed(): call(*[pltpu.with_memory_space_constraint(array, pltpu.HBM) if place == '...  21.9 us
    ppermute x12, starting transfers between devices, shifted(): lax.ppermute(value, 'head', [(j, (j + k) % count) for j in range(count)])  17.7 us
    all_to_all x1, starting transfers between devices, local(): lax.all_to_all(pieces, CHIPS, split_axis=0, concat_axis=0, tiled=True)  11.9 us
    ppermute x12, waiting for transfers between devices, shifted(): lax.ppermute(value, 'head', [(j, (j + k) % count) for j in range(count)])  11.7 us
    all_to_all x1, waiting for transfers between devices, local(): lax.all_to_all(pieces, CHIPS, split_axis=0, concat_axis=0, tiled=True)  5.18 us
    ppermute x1, starting transfers between devices, local(): edges = lax.ppermute(edges, SEQ, ahead + behind)  4.92 us
    all_to_all x1, starting transfers between devices, local(): lax.all_to_all(prefixes, CHIPS, split_axis=0, concat_axis=0, tiled=True)  4.6 us
    ppermute x1, starting transfers between devices, local(): swapped = lax.ppermute(attention[0], 'core', swap_pairs)  3.94 us
  transfers between devices with their start and end apart: 21, of which 8 were waited for; matrix products, arithmetic and copies ran while one was open for 0% of the time, Pallas kernels for 14%

profile of v4, /device:TPU:1, one launch (start us, length us, event | category | flops | bytes accessed | tf_op | source)
XLA Modules:
  0.0 91.4 jit_solution(5355045909561144520)
XLA Ops:
  0.0 0.9 %shard_map.118 = (bf16[2,8,256]{2,1,0:T(8,128)(2,1)S(1)}, bf16[136,256]{1,0:T(8,128)(2,1)S(1)}, bf16[128,256]{1,0:T(8,128)(2,1)S(1)}) custom-call(bf16[2,128,256]{2,1,0:T(8,128)(2,1)} %tokens_in.1, f32[2,128]{1,0:T(2,128)} %extra.1), custom_call_target="tpu_custom_call" | custom-call | bytes 1048576 | tf_op jit(solution)/shard_map/pallas_call | solution.py:496
  0.9 4.9 %collective-permute-start = (bf16[2,8,256]{2,1,0:T(8,128)(2,1)S(1)}, bf16[2,8,256]{2,1,0:T(8,128)(2,1)S(1)}, u32[]{:S(2)}, u32[]{:S(2)}) collective-permute-start(bf16[2,8,256]{2,1,0:T(8,128)(2,1)S(1)} %get-tuple-element.43), channel_id=1, source_target_pairs={{4,8},{12,16},{20,24},{28,32},{36,40},{44,48},{52,56},{60,64},{68,... | collective-permute-start | bytes 24584 | tf_op jit(solution)/shard_map/ppermute | solution.py:536
  5.9 1.3 %collective-permute-done.edges = bf16[2,8,256]{2,1,0:T(8,128)(2,1)S(1)} collective-permute-done((bf16[2,8,256]{2,1,0:T(8,128)(2,1)S(1)}, bf16[2,8,256]{2,1,0:T(8,128)(2,1)S(1)}, u32[]{:S(2)}, u32[]{:S(2)}) %collective-permute-start) | collective-permute-done | bytes 8224 | tf_op jit(solution)/shard_map/ppermute | solution.py:536
  7.2 0.1 collective-permute-start.1
  7.3 1.3 %collective-permute-done.1 = bf16[144,256]{1,0:T(8,128)(2,1)S(1)} collective-permute-done((bf16[144,256]{1,0:T(8,128)(2,1)S(1)}, bf16[144,256]{1,0:T(8,128)(2,1)S(1)}, u32[]{:S(2)}, u32[]{:S(2)}) %collective-permute-start.1) | collective-permute-done | bytes 73760 | tf_op jit(solution)/shard_map/ppermute | solution.py:540
  8.6 1.4 %collective-permute-start.2 = (bf16[272,256]{1,0:T(8,128)(2,1)S(1)}, bf16[272,256]{1,0:T(8,128)(2,1)S(1)}, u32[]{:S(2)}, u32[]{:S(2)}) collective-permute-start(bf16[272,256]{1,0:T(8,128)(2,1)S(1)} %pad_maximum_fusion.part0), channel_id=1, source_target_pairs={{0,1},{1,2},{2,3},{3,0},{4,5},{5,6},{6,7},{7,4},{8,9},{9,10},{10,1... | collective-permute-start | bytes 417800 | tf_op jit(solution)/shard_map/ppermute | solution.py:508
  10.0 2.6 %collective-permute-start.3 = (bf16[272,256]{1,0:T(8,128)(2,1)S(1)}, bf16[272,256]{1,0:T(8,128)(2,1)S(1)}, u32[]{:S(2)}, u32[]{:S(2)}) collective-permute-start(bf16[272,256]{1,0:T(8,128)(2,1)S(1)} %pad_maximum_fusion.part0), channel_id=1, source_target_pairs={{0,2},{1,3},{2,0},{3,1},{4,6},{5,7},{6,4},{7,5},{8,10},{9,11},{10,... | collective-permute-start | bytes 417800 | tf_op jit(solution)/shard_map/ppermute | solution.py:508
  12.6 1.1 %collective-permute-start.4 = (bf16[272,256]{1,0:T(8,128)(2,1)S(1)}, bf16[272,256]{1,0:T(8,128)(2,1)S(1)}, u32[]{:S(2)}, u32[]{:S(2)}) collective-permute-start(bf16[272,256]{1,0:T(8,128)(2,1)S(1)} %pad_maximum_fusion.part0), channel_id=1, source_target_pairs={{0,3},{1,0},{2,1},{3,2},{4,7},{5,4},{6,5},{7,6},{8,11},{9,8},{10,9... | collective-permute-start | bytes 417800 | tf_op jit(solution)/shard_map/ppermute | solution.py:508
  13.7 1.6 %shard_map.120 = (bf16[3,1024,256]{2,1,0:T(8,128)(2,1)S(1)}, bf16[1024,256]{1,0:T(8,128)(2,1)S(1)}, bf16[128,1024]{1,0:T(8,128)(2,1)S(1)}) custom-call(bf16[3,1024,256]{2,1,0:T(8,128)(2,1)} %bitcast.8, bf16[1024,256]{1,0:T(8,128)(2,1)} %gate_weight, bf16[256,1024]{1,0:T(8,128)(2,1)} %weight0.1), custom_call_target="tpu_custom_call" | custom-call | flops 1000000000 | bytes 1048576 | tf_op jit(solution)/shard_map/pallas_call | solution.py:496
  15.3 0.0 collective-permute-done.2.part1
  15.3 3.9 %collective-permute-done.3.part2 = bf16[272,256]{1,0:T(8,128)(2,1)S(1)} collective-permute-done((bf16[272,256]{1,0:T(8,128)(2,1)S(1)}, bf16[272,256]{1,0:T(8,128)(2,1)S(1)}, u32[]{:S(2)}, u32[]{:S(2)}) %collective-permute-start.3) | collective-permute-done | bytes 139296 | tf_op jit(solution)/shard_map/ppermute | solution.py:508
  19.2 0.0 collective-permute-done.4.part3
  19.2 0.0 copy-done
  19.2 0.0 copy-done.2
  19.2 0.0 copy-done.3
  19.2 0.0 copy-done.5
  19.2 4.6 %shard_map.121 = (bf16[32,24,128]{2,1,0:T(8,128)(2,1)}, bf16[272,256]{1,0:T(8,128)(2,1)}, bf16[2,2,256,256]{3,2,1,0:T(8,128)(2,1)}, f32[2,256,256]{2,1,0:T(8,128...) custom-call(bf16[272,256]{1,0:T(8,128)(2,1)S(1)} %pad_maximum_fusion, ...), custom_call_target="tpu_custom_call" | custom-call | flops 1000000000 | bytes 1048576 | tf_op jit(solution)/shard_map/pallas_call | solution.py:496
  23.9 11.9 %all-to-all-start = ((bf16[32,24,128]{2,1,0:T(8,128)(2,1)}), bf16[32,24,128]{2,1,0:T(8,128)(2,1)S(1)}, u32[]{:S(2)}, u32[]{:S(2)}) async-start(bf16[32,24,128]{2,1,0:T(8,128)(2,1)} %get-tuple-element.64), calls=%async_computation | async-start | bytes 393216 | tf_op jit(solution)/shard_map/all_to_all | solution.py:601
  35.8 0.0 copy-start.6
  35.8 1.1 %collective-permute-start.9 = (bf16[128,1024]{1,0:T(8,128)(2,1)S(1)}, bf16[128,1024]{1,0:T(8,128)(2,1)S(1)}, u32[]{:S(2)}, u32[]{:S(2)}) collective-permute-start(bf16[128,1024]{1,0:T(8,128)(2,1)S(1)} %get-tuple-element.66), channel_id=1, source_target_pairs={{0,1},{1,2},{2,3},{3,0},{4,5},{5,6},{6,7},{7,4},{8,9},{9,10},{10,1... | collective-permute-start | bytes 786440 | tf_op jit(solution)/shard_map/ppermute | solution.py:508
  36.8 2.3 %collective-permute-start.10 = (bf16[128,1024]{1,0:T(8,128)(2,1)S(1)}, bf16[128,1024]{1,0:T(8,128)(2,1)S(1)}, u32[]{:S(2)}, u32[]{:S(2)}) collective-permute-start(bf16[128,1024]{1,0:T(8,128)(2,1)S(1)} %get-tuple-element.66), channel_id=1, source_target_pairs={{0,2},{1,3},{2,0},{3,1},{4,6},{5,7},{6,4},{7,5},{8,10},{9,11},{10,... | collective-permute-start | bytes 786440 | tf_op jit(solution)/shard_map/ppermute | solution.py:508
  39.1 0.8 collective-permute-start.11
  40.0 5.2 %all-to-all-done.pieces = bf16[32,24,128]{2,1,0:T(8,128)(2,1)S(1)} async-done(((bf16[32,24,128]{2,1,0:T(8,128)(2,1)}), bf16[32,24,128]{2,1,0:T(8,128)(2,1)S(1)}, u32[]{:S(2)}, u32[]{:S(2)}) %all-to-all-start) | async-done | bytes 196640 | tf_op jit(solution)/shard_map/all_to_all | solution.py:601
  45.1 0.8 shard_map.123
  45.9 4.6 %all-to-all-start.1 = ((bf16[32,16,128]{2,1,0:T(8,128)(2,1)}), bf16[32,16,128]{2,1,0:T(8,128)(2,1)S(1)}, u32[]{:S(2)}, u32[]{:S(2)}) async-start(bf16[32,16,128]{2,1,0:T(8,128)(2,1)} %shard_map.123), calls=%async_computation.1 | async-start | bytes 262144 | tf_op jit(solution)/shard_map/all_to_all | solution.py:629
  50.6 2.7 %collective-permute-start.15 = (bf16[4,128,256]{2,1,0:T(8,128)(2,1)}, bf16[4,128,256]{2,1,0:T(8,128)(2,1)S(1)}, u32[]{:S(2)}, u32[]{:S(2)}) collective-permute-start(bf16[4,128,256]{2,1,0:T(8,128)(2,1)} %get-tuple-element.68), channel_id=1, source_target_pairs={{0,4},{4,0},{1,5},{5,1},{2,6},{6,2},{3,7},{7,3},{8,12},{12,8},{9,1... | collective-permute-start | bytes 786440 | tf_op jit(solution)/shard_map/ppermute | solution.py:606
  53.2 3.4 %shard_map.122 = (bf16[2,256,256]{2,1,0:T(8,128)(2,1)}, f32[2,256,256]{2,1,0:T(8,128)}, f32[2,256,256]{2,1,0:T(8,128)}) custom-call(bf16[272,256]{1,0:T(8,128)(2,1)} %get-tuple-element.52.query_in, bf16[2,2,256,256]{3,2,1,0:T(8,128)(2,1)} %get-tuple-element.53.kv_in, f32[2,256,256]{2,1,0:T(8,128)} %get-tuple-element.54.cum_in, ...), custom_call_target="tpu_custom_call" | custom-call | flops 1000000000 | bytes 1048576 | tf_op jit(solution)/shard_map/pallas_call | solution.py:496
  56.6 0.0 collective-permute-done.9.mine1
  56.6 0.1 collective-permute-start.12
  56.7 0.0 collective-permute-done.10.mine2
  56.7 0.0 copy-start.8
  56.8 0.5 collective-permute-start.13
  57.2 0.0 collective-permute-done.11.mine3
  57.2 0.3 collective-permute-start.14
  57.5 2.2 %all-to-all-done.1.arrived = bf16[32,16,128]{2,1,0:T(8,128)(2,1)S(1)} async-done(((bf16[32,16,128]{2,1,0:T(8,128)(2,1)}), bf16[32,16,128]{2,1,0:T(8,128)(2,1)S(1)}, u32[]{:S(2)}, u32[]{:S(2)}) %all-to-all-start.1) | async-done | bytes 131104 | tf_op jit(solution)/shard_map/all_to_all | solution.py:629
  59.7 0.0 copy-done.6
  59.7 2.4 %shard_map.125 = bf16[128,256]{1,0:T(8,128)(2,1)S(1)} custom-call(bf16[2,256,256]{2,1,0:T(8,128)(2,1)} %get-tuple-element.57.queries_in, bf16[2,2,256,256]{3,2,1,0:T(8,128)(2,1)} %get-tuple-element.53.kv_in, bf16[2,256,256]{2,1,0:T(8,128)(2,1)} %get-tuple-element.55.shrink_in, bf16[2,4,2,64,256]{4,3,2,1,0:T(8,128)(2,1)} %get-tuple-element.56.start_in, ...), custom_call_target="tpu_custom_call" | custom-call | flops 1000000000 | bytes 1048576 | tf_op jit(solution)/shard_map/pallas_call | solution.py:496
  62.2 3.9 %collective-permute-start.5 = (bf16[128,256]{1,0:T(8,128)(2,1)S(1)}, bf16[128,256]{1,0:T(8,128)(2,1)S(1)}, u32[]{:S(2)}, u32[]{:S(2)}) collective-permute-start(bf16[128,256]{1,0:T(8,128)(2,1)S(1)} %shard_map.125), channel_id=1, source_target_pairs={{0,4},{4,0},{1,5},{5,1},{2,6},{6,2},{3,7},{7,3},{8,12},{12,8},{9,1... | collective-permute-start | bytes 196616 | tf_op jit(solution)/shard_map/ppermute | solution.py:657
  66.1 2.4 %shard_map.124 = bf16[128,256]{1,0:T(8,128)(2,1)S(1)} custom-call(bf16[2,256,256]{2,1,0:T(8,128)(2,1)} %get-tuple-element.57.queries_in, bf16[2,2,256,256]{3,2,1,0:T(8,128)(2,1)} %get-tuple-element.53.kv_in, bf16[2,256,256]{2,1,0:T(8,128)(2,1)} %get-tuple-element.55.shrink_in, bf16[2,4,2,64,256]{4,3,2,1,0:T(8,128)(2,1)} %get-tuple-element.56.start_in, ...), custom_call_target="tpu_custom_call" | custom-call | flops 1000000000 | bytes 1048576 | tf_op jit(solution)/shard_map/pallas_call | solution.py:496
  68.6 0.0 collective-permute-done.5
  68.6 0.8 collective-permute-start.6
  69.4 0.0 collective-permute-done.15.passed
  69.4 2.3 %collective-permute-start.7 = (bf16[256,256]{1,0:T(8,128)(2,1)S(1)}, bf16[256,256]{1,0:T(8,128)(2,1)S(1)}, u32[]{:S(2)}, u32[]{:S(2)}) collective-permute-start(bf16[256,256]{1,0:T(8,128)(2,1)S(1)} %pad_maximum_fusion.1.part0), channel_id=1, source_target_pairs={{0,2},{1,3},{2,0},{3,1},{4,6},{5,7},{6,4},{7,5},{8,10},{9,11},{10,... | collective-permute-start | bytes 393224 | tf_op jit(solution)/shard_map/ppermute | solution.py:508
  71.7 0.0 collective-permute-done.12.theirs1
  71.8 0.9 collective-permute-start.8
  72.6 0.0 collective-permute-done.13.theirs2
  72.6 0.0 collective-permute-done.14.theirs3
  72.6 0.0 copy-start.13
  72.7 0.0 copy-done.10
  72.7 0.0 copy-done.11
  72.7 0.7 copy-done.12
  73.4 0.1 copy-done.13
  73.4 2.6 %shard_map.126 = (bf16[4,256,1024]{2,1,0:T(8,128)(2,1)S(1)}, bf16[4,256,256]{2,1,0:T(8,128)(2,1)S(1)}, bf16[1024,1024]{1,0:T(8,128)(2,1)S(1)}) custom-call(bf16[256,1024]{1,0:T(8,128)(2,1)} %weight0.1, bf16[128,1024]{1,0:T(8,128)(2,1)} %copy-done.7, bf16[128,1024]{1,0:T(8,128)(2,1)} %copy-done.8, bf16[128,1024]{1,0:T(8,128)(2,1)} %copy-done.9, ...), custom_call_target="tpu_custom_call" | custom-call | flops 1000000000 | bytes 1048576 | tf_op jit(solution)/shard_map/pallas_call | solution.py:496
  76.0 0.0 collective-permute-done.6.part1
  76.1 2.1 %collective-permute-done.7.part2 = bf16[256,256]{1,0:T(8,128)(2,1)S(1)} collective-permute-done((bf16[256,256]{1,0:T(8,128)(2,1)S(1)}, bf16[256,256]{1,0:T(8,128)(2,1)S(1)}, u32[]{:S(2)}, u32[]{:S(2)}) %collective-permute-start.7) | collective-permute-done | bytes 131104 | tf_op jit(solution)/shard_map/ppermute | solution.py:508
  78.1 0.0 collective-permute-done.8.part3
  78.1 2.4 %shard_map.127 = (f32[256,256]{1,0:T(8,128)S(1)}, bf16[256,256]{1,0:T(8,128)(2,1)S(1)}, bf16[256,256]{1,0:T(8,128)(2,1)S(1)}, bf16[256,256]{1,0:T(8,128)(2,1)S(1)}) custom-call(bf16[256,256]{1,0:T(8,128)(2,1)S(1)} %pad_maximum_fusion.1.part0, bf16[256,256]{1,0:T(8,128)(2,1)S(1)} %collective-permute-done.6.part1, ...), custom_call_target="tpu_custom_call" | custom-call | flops 2000000000 | bytes 1048576 | tf_op jit(solution)/shard_map/pallas_call | solution.py:496
  80.5 1.9 %collective-permute-start.16 = (bf16[256,256]{1,0:T(8,128)(2,1)S(1)}, bf16[256,256]{1,0:T(8,128)(2,1)S(1)}, u32[]{:S(2)}, u32[]{:S(2)}) collective-permute-start(bf16[256,256]{1,0:T(8,128)(2,1)S(1)} %get-tuple-element.74), channel_id=1, source_target_pairs={{0,1},{1,2},{2,3},{3,0},{4,5},{5,6},{6,7},{7,4},{8,9},{9,10},{10,1... | collective-permute-start | bytes 393224 | tf_op jit(solution)/shard_map/ppermute | solution.py:508
  82.4 2.3 %collective-permute-start.17 = (bf16[256,256]{1,0:T(8,128)(2,1)S(1)}, bf16[256,256]{1,0:T(8,128)(2,1)S(1)}, u32[]{:S(2)}, u32[]{:S(2)}) collective-permute-start(bf16[256,256]{1,0:T(8,128)(2,1)S(1)} %get-tuple-element.75), channel_id=1, source_target_pairs={{0,2},{1,3},{2,0},{3,1},{4,6},{5,7},{6,4},{7,5},{8,10},{9,11},{10,... | collective-permute-start | bytes 393224 | tf_op jit(solution)/shard_map/ppermute | solution.py:508
  84.8 0.2 collective-permute-start.18
  84.9 1.5 %collective-permute-done.16.part1 = bf16[256,256]{1,0:T(8,128)(2,1)S(1)} collective-permute-done((bf16[256,256]{1,0:T(8,128)(2,1)S(1)}, bf16[256,256]{1,0:T(8,128)(2,1)S(1)}, u32[]{:S(2)}, u32[]{:S(2)}) %collective-permute-start.16) | collective-permute-done | bytes 131104 | tf_op jit(solution)/shard_map/ppermute | solution.py:508
  86.4 4.2 %collective-permute-done.17.part2 = bf16[256,256]{1,0:T(8,128)(2,1)S(1)} collective-permute-done((bf16[256,256]{1,0:T(8,128)(2,1)S(1)}, bf16[256,256]{1,0:T(8,128)(2,1)S(1)}, u32[]{:S(2)}, u32[]{:S(2)}) %collective-permute-start.17) | collective-permute-done | bytes 131104 | tf_op jit(solution)/shard_map/ppermute | solution.py:508
  90.7 0.0 collective-permute-done.18.part3
  90.7 0.7 shard_map.128
  (21 shorter events, 0.1 us)
Async XLA Ops:
  0.9 6.3 %collective-permute-start = (bf16[2,8,256]{2,1,0:T(8,128)(2,1)S(1)}, bf16[2,8,256]{2,1,0:T(8,128)(2,1)S(1)}, u32[]{:S(2)}, u32[]{:S(2)}) collective-permute-start(bf16[2,8,256]{2,1,0:T(8,128)(2,1)S(1)} %get-tuple-element.43), channel_id=1, source_target_pairs={{4,8},{12,16},{20,24},{28,32},{36,40},{44,48},{52,56},{60,64},{68,... | collective-permute-start | bytes 24584 | tf_op jit(solution)/shard_map/ppermute | solution.py:536
  7.2 12.0 %copy-start = (f32[2,128]{1,0:T(2,128)S(1)}, f32[2,128]{1,0:T(2,128)}, u32[]{:S(2)}) copy-start(f32[2,128]{1,0:T(2,128)} %extra.1) | copy-start | bytes 3076
  7.2 12.0 %copy-start.2 = (f32[2,4,3,256]{3,1,2,0:T(4,128)S(1)}, f32[2,4,3,256]{3,1,2,0:T(4,128)}, u32[]{:S(2)}) copy-start(f32[2,4,3,256]{3,1,2,0:T(4,128)} %param.16) | copy-start | bytes 73732
  7.2 12.0 %copy-start.3 = (f32[1024]{0:T(1024)S(1)}, f32[1024]{0:T(1024)}, u32[]{:S(2)}) copy-start(f32[1024]{0:T(1024)} %param.13) | copy-start | bytes 12292
  7.2 12.0 %copy-start.5 = (f32[4,64]{1,0:T(4,128)S(1)}, f32[4,64]{1,0:T(4,128)}, u32[]{:S(2)}) copy-start(f32[4,64]{1,0:T(4,128)} %rate.1) | copy-start | bytes 3076
  7.2 1.4 %collective-permute-start.1 = (bf16[144,256]{1,0:T(8,128)(2,1)S(1)}, bf16[144,256]{1,0:T(8,128)(2,1)S(1)}, u32[]{:S(2)}, u32[]{:S(2)}) collective-permute-start(bf16[144,256]{1,0:T(8,128)(2,1)S(1)} %get-tuple-element.44), channel_id=1, source_target_pairs={{0,4},{4,0},{1,5},{5,1},{2,6},{6,2},{3,7},{7,3},{8,12},{12,8},{9,1... | collective-permute-start | bytes 221192 | tf_op jit(solution)/shard_map/ppermute | solution.py:540
  8.6 6.7 %collective-permute-start.2 = (bf16[272,256]{1,0:T(8,128)(2,1)S(1)}, bf16[272,256]{1,0:T(8,128)(2,1)S(1)}, u32[]{:S(2)}, u32[]{:S(2)}) collective-permute-start(bf16[272,256]{1,0:T(8,128)(2,1)S(1)} %pad_maximum_fusion.part0), channel_id=1, source_target_pairs={{0,1},{1,2},{2,3},{3,0},{4,5},{5,6},{6,7},{7,4},{8,9},{9,10},{10,1... | collective-permute-start | bytes 417800 | tf_op jit(solution)/shard_map/ppermute | solution.py:508
  10.0 9.2 %collective-permute-start.3 = (bf16[272,256]{1,0:T(8,128)(2,1)S(1)}, bf16[272,256]{1,0:T(8,128)(2,1)S(1)}, u32[]{:S(2)}, u32[]{:S(2)}) collective-permute-start(bf16[272,256]{1,0:T(8,128)(2,1)S(1)} %pad_maximum_fusion.part0), channel_id=1, source_target_pairs={{0,2},{1,3},{2,0},{3,1},{4,6},{5,7},{6,4},{7,5},{8,10},{9,11},{10,... | collective-permute-start | bytes 417800 | tf_op jit(solution)/shard_map/ppermute | solution.py:508
  12.6 6.6 %collective-permute-start.4 = (bf16[272,256]{1,0:T(8,128)(2,1)S(1)}, bf16[272,256]{1,0:T(8,128)(2,1)S(1)}, u32[]{:S(2)}, u32[]{:S(2)}) collective-permute-start(bf16[272,256]{1,0:T(8,128)(2,1)S(1)} %pad_maximum_fusion.part0), channel_id=1, source_target_pairs={{0,3},{1,0},{2,1},{3,2},{4,7},{5,4},{6,5},{7,6},{8,11},{9,8},{10,9... | collective-permute-start | bytes 417800 | tf_op jit(solution)/shard_map/ppermute | solution.py:508
  23.9 21.3 %all-to-all-start = ((bf16[32,24,128]{2,1,0:T(8,128)(2,1)}), bf16[32,24,128]{2,1,0:T(8,128)(2,1)S(1)}, u32[]{:S(2)}, u32[]{:S(2)}) async-start(bf16[32,24,128]{2,1,0:T(8,128)(2,1)} %get-tuple-element.64), calls=%async_computation | async-start | bytes 393216 | tf_op jit(solution)/shard_map/all_to_all | solution.py:601
  35.8 24.0 %copy-start.6 = (f32[4,64]{1,0:T(4,128)S(1)}, f32[4,64]{1,0:T(4,128)}, u32[]{:S(2)}) copy-start(f32[4,64]{1,0:T(4,128)} %gain.3) | copy-start | bytes 3076
  35.8 20.8 %collective-permute-start.9 = (bf16[128,1024]{1,0:T(8,128)(2,1)S(1)}, bf16[128,1024]{1,0:T(8,128)(2,1)S(1)}, u32[]{:S(2)}, u32[]{:S(2)}) collective-permute-start(bf16[128,1024]{1,0:T(8,128)(2,1)S(1)} %get-tuple-element.66), channel_id=1, source_target_pairs={{0,1},{1,2},{2,3},{3,0},{4,5},{5,6},{6,7},{7,4},{8,9},{9,10},{10,1... | collective-permute-start | bytes 786440 | tf_op jit(solution)/shard_map/ppermute | solution.py:508
  36.8 19.9 %collective-permute-start.10 = (bf16[128,1024]{1,0:T(8,128)(2,1)S(1)}, bf16[128,1024]{1,0:T(8,128)(2,1)S(1)}, u32[]{:S(2)}, u32[]{:S(2)}) collective-permute-start(bf16[128,1024]{1,0:T(8,128)(2,1)S(1)} %get-tuple-element.66), channel_id=1, source_target_pairs={{0,2},{1,3},{2,0},{3,1},{4,6},{5,7},{6,4},{7,5},{8,10},{9,11},{10,... | collective-permute-start | bytes 786440 | tf_op jit(solution)/shard_map/ppermute | solution.py:508
  39.1 18.1 %collective-permute-start.11 = (bf16[128,1024]{1,0:T(8,128)(2,1)S(1)}, bf16[128,1024]{1,0:T(8,128)(2,1)S(1)}, u32[]{:S(2)}, u32[]{:S(2)}) collective-permute-start(bf16[128,1024]{1,0:T(8,128)(2,1)S(1)} %get-tuple-element.66), channel_id=1, source_target_pairs={{0,3},{1,0},{2,1},{3,2},{4,7},{5,4},{6,5},{7,6},{8,11},{9,8},{10,9... | collective-permute-start | bytes 786440 | tf_op jit(solution)/shard_map/ppermute | solution.py:508
  45.9 13.8 %all-to-all-start.1 = ((bf16[32,16,128]{2,1,0:T(8,128)(2,1)}), bf16[32,16,128]{2,1,0:T(8,128)(2,1)S(1)}, u32[]{:S(2)}, u32[]{:S(2)}) async-start(bf16[32,16,128]{2,1,0:T(8,128)(2,1)} %shard_map.123), calls=%async_computation.1 | async-start | bytes 262144 | tf_op jit(solution)/shard_map/all_to_all | solution.py:629
  50.6 18.9 %collective-permute-start.15 = (bf16[4,128,256]{2,1,0:T(8,128)(2,1)}, bf16[4,128,256]{2,1,0:T(8,128)(2,1)S(1)}, u32[]{:S(2)}, u32[]{:S(2)}) collective-permute-start(bf16[4,128,256]{2,1,0:T(8,128)(2,1)} %get-tuple-element.68), channel_id=1, source_target_pairs={{0,4},{4,0},{1,5},{5,1},{2,6},{6,2},{3,7},{7,3},{8,12},{12,8},{9,1... | collective-permute-start | bytes 786440 | tf_op jit(solution)/shard_map/ppermute | solution.py:606
  56.6 11.9 %copy-start.7 = (bf16[128,1024]{1,0:T(8,128)(2,1)}, bf16[128,1024]{1,0:T(8,128)(2,1)S(1)}, u32[]{:S(2)}) copy-start(bf16[128,1024]{1,0:T(8,128)(2,1)S(1)} %collective-permute-done.9.mine1) | copy-start | bytes 786436
  56.6 15.1 %collective-permute-start.12 = (bf16[128,1024]{1,0:T(8,128)(2,1)S(1)}, bf16[128,1024]{1,0:T(8,128)(2,1)S(1)}, u32[]{:S(2)}, u32[]{:S(2)}) collective-permute-start(bf16[128,1024]{1,0:T(8,128)(2,1)S(1)} %collective-permute-done.9.mine1), channel_id=1, source_target_pairs={{0,4},{4,0},{1,5},{5,1},{2,6},{6,2},{3,7},{7,3},{8,12},{12,8},{9,1... | collective-permute-start | bytes 786440 | tf_op jit(solution)/shard_map/ppermute | solution.py:605
  56.7 11.8 %copy-start.8 = (bf16[128,1024]{1,0:T(8,128)(2,1)}, bf16[128,1024]{1,0:T(8,128)(2,1)S(1)}, u32[]{:S(2)}) copy-start(bf16[128,1024]{1,0:T(8,128)(2,1)S(1)} %collective-permute-done.10.mine2) | copy-start | bytes 786436
  56.8 15.9 %collective-permute-start.13 = (bf16[128,1024]{1,0:T(8,128)(2,1)S(1)}, bf16[128,1024]{1,0:T(8,128)(2,1)S(1)}, u32[]{:S(2)}, u32[]{:S(2)}) collective-permute-start(bf16[128,1024]{1,0:T(8,128)(2,1)S(1)} %collective-permute-done.10.mine2), channel_id=1, source_target_pairs={{0,4},{4,0},{1,5},{5,1},{2,6},{6,2},{3,7},{7,3},{8,12},{12,8},{9,1... | collective-permute-start | bytes 786440 | tf_op jit(solution)/shard_map/ppermute | solution.py:605
  57.2 11.3 %copy-start.9 = (bf16[128,1024]{1,0:T(8,128)(2,1)}, bf16[128,1024]{1,0:T(8,128)(2,1)S(1)}, u32[]{:S(2)}) copy-start(bf16[128,1024]{1,0:T(8,128)(2,1)S(1)} %collective-permute-done.11.mine3) | copy-start | bytes 786436
  57.2 15.4 %collective-permute-start.14 = (bf16[128,1024]{1,0:T(8,128)(2,1)S(1)}, bf16[128,1024]{1,0:T(8,128)(2,1)S(1)}, u32[]{:S(2)}, u32[]{:S(2)}) collective-permute-start(bf16[128,1024]{1,0:T(8,128)(2,1)S(1)} %collective-permute-done.11.mine3), channel_id=1, source_target_pairs={{0,4},{4,0},{1,5},{5,1},{2,6},{6,2},{3,7},{7,3},{8,12},{12,8},{9,1... | collective-permute-start | bytes 786440 | tf_op jit(solution)/shard_map/ppermute | solution.py:605
  62.2 6.4 %collective-permute-start.5 = (bf16[128,256]{1,0:T(8,128)(2,1)S(1)}, bf16[128,256]{1,0:T(8,128)(2,1)S(1)}, u32[]{:S(2)}, u32[]{:S(2)}) collective-permute-start(bf16[128,256]{1,0:T(8,128)(2,1)S(1)} %shard_map.125), channel_id=1, source_target_pairs={{0,4},{4,0},{1,5},{5,1},{2,6},{6,2},{3,7},{7,3},{8,12},{12,8},{9,1... | collective-permute-start | bytes 196616 | tf_op jit(solution)/shard_map/ppermute | solution.py:657
  68.6 7.5 %collective-permute-start.6 = (bf16[256,256]{1,0:T(8,128)(2,1)S(1)}, bf16[256,256]{1,0:T(8,128)(2,1)S(1)}, u32[]{:S(2)}, u32[]{:S(2)}) collective-permute-start(bf16[256,256]{1,0:T(8,128)(2,1)S(1)} %pad_maximum_fusion.1.part0), channel_id=1, source_target_pairs={{0,1},{1,2},{2,3},{3,0},{4,5},{5,6},{6,7},{7,4},{8,9},{9,10},{10,1... | collective-permute-start | bytes 393224 | tf_op jit(solution)/shard_map/ppermute | solution.py:508
  69.4 3.2 %copy-start.10 = (bf16[4,128,256]{2,1,0:T(8,128)(2,1)}, bf16[4,128,256]{2,1,0:T(8,128)(2,1)S(1)}, u32[]{:S(2)}) copy-start(bf16[4,128,256]{2,1,0:T(8,128)(2,1)S(1)} %collective-permute-done.15.passed) | copy-start | bytes 786436
  69.4 8.7 %collective-permute-start.7 = (bf16[256,256]{1,0:T(8,128)(2,1)S(1)}, bf16[256,256]{1,0:T(8,128)(2,1)S(1)}, u32[]{:S(2)}, u32[]{:S(2)}) collective-permute-start(bf16[256,256]{1,0:T(8,128)(2,1)S(1)} %pad_maximum_fusion.1.part0), channel_id=1, source_target_pairs={{0,2},{1,3},{2,0},{3,1},{4,6},{5,7},{6,4},{7,5},{8,10},{9,11},{10,... | collective-permute-start | bytes 393224 | tf_op jit(solution)/shard_map/ppermute | solution.py:508
  71.8 0.9 copy-start.11
  71.8 6.4 %collective-permute-start.8 = (bf16[256,256]{1,0:T(8,128)(2,1)S(1)}, bf16[256,256]{1,0:T(8,128)(2,1)S(1)}, u32[]{:S(2)}, u32[]{:S(2)}) collective-permute-start(bf16[256,256]{1,0:T(8,128)(2,1)S(1)} %pad_maximum_fusion.1.part0), channel_id=1, source_target_pairs={{0,3},{1,0},{2,1},{3,2},{4,7},{5,4},{6,5},{7,6},{8,11},{9,8},{10,9... | collective-permute-start | bytes 393224 | tf_op jit(solution)/shard_map/ppermute | solution.py:508
  72.6 0.7 copy-start.12
  72.6 0.8 copy-start.13
  73.4 4.7 %copy-start.1 = (bf16[1024,1024]{1,0:T(8,128)(2,1)S(1)}, bf16[1024,1024]{1,0:T(8,128)(2,1)}, u32[]{:S(2)}) copy-start(bf16[1024,1024]{1,0:T(8,128)(2,1)} %up.1) | copy-start | bytes 6291460
  73.4 4.7 %copy-start.4 = (f32[1024]{0:T(1024)S(1)}, f32[1024]{0:T(1024)}, u32[]{:S(2)}) copy-start(f32[1024]{0:T(1024)} %param.21) | copy-start | bytes 12292
  80.5 5.9 %collective-permute-start.16 = (bf16[256,256]{1,0:T(8,128)(2,1)S(1)}, bf16[256,256]{1,0:T(8,128)(2,1)S(1)}, u32[]{:S(2)}, u32[]{:S(2)}) collective-permute-start(bf16[256,256]{1,0:T(8,128)(2,1)S(1)} %get-tuple-element.74), channel_id=1, source_target_pairs={{0,1},{1,2},{2,3},{3,0},{4,5},{5,6},{6,7},{7,4},{8,9},{9,10},{10,1... | collective-permute-start | bytes 393224 | tf_op jit(solution)/shard_map/ppermute | solution.py:508
  82.4 8.2 %collective-permute-start.17 = (bf16[256,256]{1,0:T(8,128)(2,1)S(1)}, bf16[256,256]{1,0:T(8,128)(2,1)S(1)}, u32[]{:S(2)}, u32[]{:S(2)}) collective-permute-start(bf16[256,256]{1,0:T(8,128)(2,1)S(1)} %get-tuple-element.75), channel_id=1, source_target_pairs={{0,2},{1,3},{2,0},{3,1},{4,6},{5,7},{6,4},{7,5},{8,10},{9,11},{10,... | collective-permute-start | bytes 393224 | tf_op jit(solution)/shard_map/ppermute | solution.py:508
  84.8 5.9 %collective-permute-start.18 = (bf16[256,256]{1,0:T(8,128)(2,1)S(1)}, bf16[256,256]{1,0:T(8,128)(2,1)S(1)}, u32[]{:S(2)}, u32[]{:S(2)}) collective-permute-start(bf16[256,256]{1,0:T(8,128)(2,1)S(1)} %get-tuple-element.76), channel_id=1, source_target_pairs={{0,3},{1,0},{2,1},{3,2},{4,7},{5,4},{6,5},{7,6},{8,11},{9,8},{10,9... | collective-permute-start | bytes 393224 | tf_op jit(solution)/shard_map/ppermute | solution.py:508

commit v5 on v4

--- a/solution.py
+++ b/solution.py
@@ -543,7 +543,9 @@
     rows, qkv_weight, gate_weight, out_weight = lax.optimization_barrier(
         (rows, qkv_weight, forget_gate_weight, output_projection_weight)
     )
-    parts = [rows] + [shifted(rows, k) for k in (1, 2, 3)]
+    parts = [rows]
+    for k in (1, 2, 3):
+        parts.append(shifted(rows, k))
     qkv_weight, gate_weight, half_weight = kernel(
         warm_kernel,
         "hhh",
@@ -688,9 +690,10 @@
         up_projection_weight,
         down_weight,
     )
-    (out,) = kernel(finish_kernel, "vvvv", [((2, 128, 256), BF16, "v")])(
-        base, shifted(out1, 1), shifted(out2, 2), shifted(out3, 3)
-    )
+    sums = [base]
+    for k, part in ((1, out1), (2, out2), (3, out3)):
+        sums.append(shifted(part, k))
+    (out,) = kernel(finish_kernel, "vvvv", [((2, 128, 256), BF16, "v")])(*sums)
     return out
 
 

time: 91.7 us -> 91.7 us (level)
  no operation moved by 1% of the time
where the time goes in v5:
time: 91.7 us; the launch traced here: 91.4 us
  starting transfers between devices  46.7 us (51%)
  Pallas kernels  21.9 us (24%)
  waiting for transfers between devices  21.7 us (24%)
    pallas_call x11, Pallas kernels, placed(): call(*[pltpu.with_memory_space_constraint(array, pltpu.HBM) if place == '...  21.9 us
    ppermute x12, starting transfers between devices, shifted(): lax.ppermute(value, 'head', [(j, (j + k) % count) for j in range(count)])  17.7 us
    all_to_all x1, starting transfers between devices, local(): lax.all_to_all(pieces, CHIPS, split_axis=0, concat_axis=0, tiled=True)  11.9 us
    ppermute x12, waiting for transfers between devices, shifted(): lax.ppermute(value, 'head', [(j, (j + k) % count) for j in range(count)])  11.7 us
    all_to_all x1, waiting for transfers between devices, local(): lax.all_to_all(pieces, CHIPS, split_axis=0, concat_axis=0, tiled=True)  5.18 us
    ppermute x1, starting transfers between devices, local(): edges = lax.ppermute(edges, SEQ, ahead + behind)  4.92 us
    all_to_all x1, starting transfers between devices, local(): lax.all_to_all(prefixes, CHIPS, split_axis=0, concat_axis=0, tiled=True)  4.6 us
    ppermute x1, starting transfers between devices, local(): swapped = lax.ppermute(attention[0], 'core', swap_pairs)  3.94 us
  transfers between devices with their start and end apart: 21, of which 8 were waited for; matrix products, arithmetic and copies ran while one was open for 0% of the time, Pallas kernels for 14%

profile of v5, /device:TPU:1, one launch (start us, length us, event | category | flops | bytes accessed | tf_op | source)
XLA Modules:
  0.0 91.4 jit_solution(5355045909561144520)
XLA Ops:
  0.0 0.9 %shard_map.118 = (bf16[2,8,256]{2,1,0:T(8,128)(2,1)S(1)}, bf16[136,256]{1,0:T(8,128)(2,1)S(1)}, bf16[128,256]{1,0:T(8,128)(2,1)S(1)}) custom-call(bf16[2,128,256]{2,1,0:T(8,128)(2,1)} %tokens_in.1, f32[2,128]{1,0:T(2,128)} %extra.1), custom_call_target="tpu_custom_call" | custom-call | bytes 1048576 | tf_op jit(solution)/shard_map/pallas_call | solution.py:496
  0.9 4.9 %collective-permute-start = (bf16[2,8,256]{2,1,0:T(8,128)(2,1)S(1)}, bf16[2,8,256]{2,1,0:T(8,128)(2,1)S(1)}, u32[]{:S(2)}, u32[]{:S(2)}) collective-permute-start(bf16[2,8,256]{2,1,0:T(8,128)(2,1)S(1)} %get-tuple-element.43), channel_id=1, source_target_pairs={{4,8},{12,16},{20,24},{28,32},{36,40},{44,48},{52,56},{60,64},{68,... | collective-permute-start | bytes 24584 | tf_op jit(solution)/shard_map/ppermute | solution.py:536
  5.9 1.3 %collective-permute-done.edges = bf16[2,8,256]{2,1,0:T(8,128)(2,1)S(1)} collective-permute-done((bf16[2,8,256]{2,1,0:T(8,128)(2,1)S(1)}, bf16[2,8,256]{2,1,0:T(8,128)(2,1)S(1)}, u32[]{:S(2)}, u32[]{:S(2)}) %collective-permute-start) | collective-permute-done | bytes 8224 | tf_op jit(solution)/shard_map/ppermute | solution.py:536
  7.2 0.1 collective-permute-start.1
  7.3 1.3 %collective-permute-done.1 = bf16[144,256]{1,0:T(8,128)(2,1)S(1)} collective-permute-done((bf16[144,256]{1,0:T(8,128)(2,1)S(1)}, bf16[144,256]{1,0:T(8,128)(2,1)S(1)}, u32[]{:S(2)}, u32[]{:S(2)}) %collective-permute-start.1) | collective-permute-done | bytes 73760 | tf_op jit(solution)/shard_map/ppermute | solution.py:540
  8.6 1.4 %collective-permute-start.2 = (bf16[272,256]{1,0:T(8,128)(2,1)S(1)}, bf16[272,256]{1,0:T(8,128)(2,1)S(1)}, u32[]{:S(2)}, u32[]{:S(2)}) collective-permute-start(bf16[272,256]{1,0:T(8,128)(2,1)S(1)} %pad_maximum_fusion.part0), channel_id=1, source_target_pairs={{0,1},{1,2},{2,3},{3,0},{4,5},{5,6},{6,7},{7,4},{8,9},{9,10},{10,1... | collective-permute-start | bytes 417800 | tf_op jit(solution)/shard_map/ppermute | solution.py:508
  10.0 2.6 %collective-permute-start.3 = (bf16[272,256]{1,0:T(8,128)(2,1)S(1)}, bf16[272,256]{1,0:T(8,128)(2,1)S(1)}, u32[]{:S(2)}, u32[]{:S(2)}) collective-permute-start(bf16[272,256]{1,0:T(8,128)(2,1)S(1)} %pad_maximum_fusion.part0), channel_id=1, source_target_pairs={{0,2},{1,3},{2,0},{3,1},{4,6},{5,7},{6,4},{7,5},{8,10},{9,11},{10,... | collective-permute-start | bytes 417800 | tf_op jit(solution)/shard_map/ppermute | solution.py:508
  12.6 1.1 %collective-permute-start.4 = (bf16[272,256]{1,0:T(8,128)(2,1)S(1)}, bf16[272,256]{1,0:T(8,128)(2,1)S(1)}, u32[]{:S(2)}, u32[]{:S(2)}) collective-permute-start(bf16[272,256]{1,0:T(8,128)(2,1)S(1)} %pad_maximum_fusion.part0), channel_id=1, source_target_pairs={{0,3},{1,0},{2,1},{3,2},{4,7},{5,4},{6,5},{7,6},{8,11},{9,8},{10,9... | collective-permute-start | bytes 417800 | tf_op jit(solution)/shard_map/ppermute | solution.py:508
  13.7 1.6 %shard_map.120 = (bf16[3,1024,256]{2,1,0:T(8,128)(2,1)S(1)}, bf16[1024,256]{1,0:T(8,128)(2,1)S(1)}, bf16[128,1024]{1,0:T(8,128)(2,1)S(1)}) custom-call(bf16[3,1024,256]{2,1,0:T(8,128)(2,1)} %bitcast.8, bf16[1024,256]{1,0:T(8,128)(2,1)} %gate_weight, bf16[256,1024]{1,0:T(8,128)(2,1)} %weight0.1), custom_call_target="tpu_custom_call" | custom-call | flops 1000000000 | bytes 1048576 | tf_op jit(solution)/shard_map/pallas_call | solution.py:496
  15.3 0.0 collective-permute-done.2.part1
  15.3 3.9 %collective-permute-done.3.part2 = bf16[272,256]{1,0:T(8,128)(2,1)S(1)} collective-permute-done((bf16[272,256]{1,0:T(8,128)(2,1)S(1)}, bf16[272,256]{1,0:T(8,128)(2,1)S(1)}, u32[]{:S(2)}, u32[]{:S(2)}) %collective-permute-start.3) | collective-permute-done | bytes 139296 | tf_op jit(solution)/shard_map/ppermute | solution.py:508
  19.2 0.0 collective-permute-done.4.part3
  19.2 0.0 copy-done
  19.2 0.0 copy-done.2
  19.2 0.0 copy-done.3
  19.2 0.0 copy-done.5
  19.2 4.6 %shard_map.121 = (bf16[32,24,128]{2,1,0:T(8,128)(2,1)}, bf16[272,256]{1,0:T(8,128)(2,1)}, bf16[2,2,256,256]{3,2,1,0:T(8,128)(2,1)}, f32[2,256,256]{2,1,0:T(8,128...) custom-call(bf16[272,256]{1,0:T(8,128)(2,1)S(1)} %pad_maximum_fusion, ...), custom_call_target="tpu_custom_call" | custom-call | flops 1000000000 | bytes 1048576 | tf_op jit(solution)/shard_map/pallas_call | solution.py:496
  23.9 11.9 %all-to-all-start = ((bf16[32,24,128]{2,1,0:T(8,128)(2,1)}), bf16[32,24,128]{2,1,0:T(8,128)(2,1)S(1)}, u32[]{:S(2)}, u32[]{:S(2)}) async-start(bf16[32,24,128]{2,1,0:T(8,128)(2,1)} %get-tuple-element.64), calls=%async_computation | async-start | bytes 393216 | tf_op jit(solution)/shard_map/all_to_all | solution.py:603
  35.8 0.0 copy-start.6
  35.8 1.1 %collective-permute-start.9 = (bf16[128,1024]{1,0:T(8,128)(2,1)S(1)}, bf16[128,1024]{1,0:T(8,128)(2,1)S(1)}, u32[]{:S(2)}, u32[]{:S(2)}) collective-permute-start(bf16[128,1024]{1,0:T(8,128)(2,1)S(1)} %get-tuple-element.66), channel_id=1, source_target_pairs={{0,1},{1,2},{2,3},{3,0},{4,5},{5,6},{6,7},{7,4},{8,9},{9,10},{10,1... | collective-permute-start | bytes 786440 | tf_op jit(solution)/shard_map/ppermute | solution.py:508
  36.8 2.3 %collective-permute-start.10 = (bf16[128,1024]{1,0:T(8,128)(2,1)S(1)}, bf16[128,1024]{1,0:T(8,128)(2,1)S(1)}, u32[]{:S(2)}, u32[]{:S(2)}) collective-permute-start(bf16[128,1024]{1,0:T(8,128)(2,1)S(1)} %get-tuple-element.66), channel_id=1, source_target_pairs={{0,2},{1,3},{2,0},{3,1},{4,6},{5,7},{6,4},{7,5},{8,10},{9,11},{10,... | collective-permute-start | bytes 786440 | tf_op jit(solution)/shard_map/ppermute | solution.py:508
  39.1 0.8 collective-permute-start.11
  40.0 5.2 %all-to-all-done.pieces = bf16[32,24,128]{2,1,0:T(8,128)(2,1)S(1)} async-done(((bf16[32,24,128]{2,1,0:T(8,128)(2,1)}), bf16[32,24,128]{2,1,0:T(8,128)(2,1)S(1)}, u32[]{:S(2)}, u32[]{:S(2)}) %all-to-all-start) | async-done | bytes 196640 | tf_op jit(solution)/shard_map/all_to_all | solution.py:603
  45.1 0.8 shard_map.123
  45.9 4.6 %all-to-all-start.1 = ((bf16[32,16,128]{2,1,0:T(8,128)(2,1)}), bf16[32,16,128]{2,1,0:T(8,128)(2,1)S(1)}, u32[]{:S(2)}, u32[]{:S(2)}) async-start(bf16[32,16,128]{2,1,0:T(8,128)(2,1)} %shard_map.123), calls=%async_computation.1 | async-start | bytes 262144 | tf_op jit(solution)/shard_map/all_to_all | solution.py:631
  50.6 2.7 %collective-permute-start.15 = (bf16[4,128,256]{2,1,0:T(8,128)(2,1)}, bf16[4,128,256]{2,1,0:T(8,128)(2,1)S(1)}, u32[]{:S(2)}, u32[]{:S(2)}) collective-permute-start(bf16[4,128,256]{2,1,0:T(8,128)(2,1)} %get-tuple-element.68), channel_id=1, source_target_pairs={{0,4},{4,0},{1,5},{5,1},{2,6},{6,2},{3,7},{7,3},{8,12},{12,8},{9,1... | collective-permute-start | bytes 786440 | tf_op jit(solution)/shard_map/ppermute | solution.py:608
  53.2 3.4 %shard_map.122 = (bf16[2,256,256]{2,1,0:T(8,128)(2,1)}, f32[2,256,256]{2,1,0:T(8,128)}, f32[2,256,256]{2,1,0:T(8,128)}) custom-call(bf16[272,256]{1,0:T(8,128)(2,1)} %get-tuple-element.52.query_in, bf16[2,2,256,256]{3,2,1,0:T(8,128)(2,1)} %get-tuple-element.53.kv_in, f32[2,256,256]{2,1,0:T(8,128)} %get-tuple-element.54.cum_in, ...), custom_call_target="tpu_custom_call" | custom-call | flops 1000000000 | bytes 1048576 | tf_op jit(solution)/shard_map/pallas_call | solution.py:496
  56.6 0.0 collective-permute-done.9.mine1
  56.6 0.1 collective-permute-start.12
  56.7 0.0 collective-permute-done.10.mine2
  56.7 0.0 copy-start.8
  56.8 0.5 collective-permute-start.13
  57.2 0.0 collective-permute-done.11.mine3
  57.2 0.3 collective-permute-start.14
  57.5 2.2 %all-to-all-done.1.arrived = bf16[32,16,128]{2,1,0:T(8,128)(2,1)S(1)} async-done(((bf16[32,16,128]{2,1,0:T(8,128)(2,1)}), bf16[32,16,128]{2,1,0:T(8,128)(2,1)S(1)}, u32[]{:S(2)}, u32[]{:S(2)}) %all-to-all-start.1) | async-done | bytes 131104 | tf_op jit(solution)/shard_map/all_to_all | solution.py:631
  59.7 0.0 copy-done.6
  59.7 2.4 %shard_map.125 = bf16[128,256]{1,0:T(8,128)(2,1)S(1)} custom-call(bf16[2,256,256]{2,1,0:T(8,128)(2,1)} %get-tuple-element.57.queries_in, bf16[2,2,256,256]{3,2,1,0:T(8,128)(2,1)} %get-tuple-element.53.kv_in, bf16[2,256,256]{2,1,0:T(8,128)(2,1)} %get-tuple-element.55.shrink_in, bf16[2,4,2,64,256]{4,3,2,1,0:T(8,128)(2,1)} %get-tuple-element.56.start_in, ...), custom_call_target="tpu_custom_call" | custom-call | flops 1000000000 | bytes 1048576 | tf_op jit(solution)/shard_map/pallas_call | solution.py:496
  62.2 3.9 %collective-permute-start.5 = (bf16[128,256]{1,0:T(8,128)(2,1)S(1)}, bf16[128,256]{1,0:T(8,128)(2,1)S(1)}, u32[]{:S(2)}, u32[]{:S(2)}) collective-permute-start(bf16[128,256]{1,0:T(8,128)(2,1)S(1)} %shard_map.125), channel_id=1, source_target_pairs={{0,4},{4,0},{1,5},{5,1},{2,6},{6,2},{3,7},{7,3},{8,12},{12,8},{9,1... | collective-permute-start | bytes 196616 | tf_op jit(solution)/shard_map/ppermute | solution.py:659
  66.1 2.4 %shard_map.124 = bf16[128,256]{1,0:T(8,128)(2,1)S(1)} custom-call(bf16[2,256,256]{2,1,0:T(8,128)(2,1)} %get-tuple-element.57.queries_in, bf16[2,2,256,256]{3,2,1,0:T(8,128)(2,1)} %get-tuple-element.53.kv_in, bf16[2,256,256]{2,1,0:T(8,128)(2,1)} %get-tuple-element.55.shrink_in, bf16[2,4,2,64,256]{4,3,2,1,0:T(8,128)(2,1)} %get-tuple-element.56.start_in, ...), custom_call_target="tpu_custom_call" | custom-call | flops 1000000000 | bytes 1048576 | tf_op jit(solution)/shard_map/pallas_call | solution.py:496
  68.6 0.0 collective-permute-done.5
  68.6 0.8 collective-permute-start.6
  69.4 0.0 collective-permute-done.15.passed
  69.4 2.3 %collective-permute-start.7 = (bf16[256,256]{1,0:T(8,128)(2,1)S(1)}, bf16[256,256]{1,0:T(8,128)(2,1)S(1)}, u32[]{:S(2)}, u32[]{:S(2)}) collective-permute-start(bf16[256,256]{1,0:T(8,128)(2,1)S(1)} %pad_maximum_fusion.1.part0), channel_id=1, source_target_pairs={{0,2},{1,3},{2,0},{3,1},{4,6},{5,7},{6,4},{7,5},{8,10},{9,11},{10,... | collective-permute-start | bytes 393224 | tf_op jit(solution)/shard_map/ppermute | solution.py:508
  71.7 0.0 collective-permute-done.12.theirs1
  71.8 0.9 collective-permute-start.8
  72.6 0.0 collective-permute-done.13.theirs2
  72.6 0.0 collective-permute-done.14.theirs3
  72.6 0.0 copy-start.13
  72.7 0.0 copy-done.10
  72.7 0.0 copy-done.11
  72.7 0.7 copy-done.12
  73.4 0.1 copy-done.13
  73.4 2.6 %shard_map.126 = (bf16[4,256,1024]{2,1,0:T(8,128)(2,1)S(1)}, bf16[4,256,256]{2,1,0:T(8,128)(2,1)S(1)}, bf16[1024,1024]{1,0:T(8,128)(2,1)S(1)}) custom-call(bf16[256,1024]{1,0:T(8,128)(2,1)} %weight0.1, bf16[128,1024]{1,0:T(8,128)(2,1)} %copy-done.7, bf16[128,1024]{1,0:T(8,128)(2,1)} %copy-done.8, bf16[128,1024]{1,0:T(8,128)(2,1)} %copy-done.9, ...), custom_call_target="tpu_custom_call" | custom-call | flops 1000000000 | bytes 1048576 | tf_op jit(solution)/shard_map/pallas_call | solution.py:496
  76.0 0.0 collective-permute-done.6.part1
  76.1 2.1 %collective-permute-done.7.part2 = bf16[256,256]{1,0:T(8,128)(2,1)S(1)} collective-permute-done((bf16[256,256]{1,0:T(8,128)(2,1)S(1)}, bf16[256,256]{1,0:T(8,128)(2,1)S(1)}, u32[]{:S(2)}, u32[]{:S(2)}) %collective-permute-start.7) | collective-permute-done | bytes 131104 | tf_op jit(solution)/shard_map/ppermute | solution.py:508
  78.1 0.0 collective-permute-done.8.part3
  78.1 2.4 %shard_map.127 = (f32[256,256]{1,0:T(8,128)S(1)}, bf16[256,256]{1,0:T(8,128)(2,1)S(1)}, bf16[256,256]{1,0:T(8,128)(2,1)S(1)}, bf16[256,256]{1,0:T(8,128)(2,1)S(1)}) custom-call(bf16[256,256]{1,0:T(8,128)(2,1)S(1)} %pad_maximum_fusion.1.part0, bf16[256,256]{1,0:T(8,128)(2,1)S(1)} %collective-permute-done.6.part1, ...), custom_call_target="tpu_custom_call" | custom-call | flops 2000000000 | bytes 1048576 | tf_op jit(solution)/shard_map/pallas_call | solution.py:496
  80.5 1.9 %collective-permute-start.16 = (bf16[256,256]{1,0:T(8,128)(2,1)S(1)}, bf16[256,256]{1,0:T(8,128)(2,1)S(1)}, u32[]{:S(2)}, u32[]{:S(2)}) collective-permute-start(bf16[256,256]{1,0:T(8,128)(2,1)S(1)} %get-tuple-element.74), channel_id=1, source_target_pairs={{0,1},{1,2},{2,3},{3,0},{4,5},{5,6},{6,7},{7,4},{8,9},{9,10},{10,1... | collective-permute-start | bytes 393224 | tf_op jit(solution)/shard_map/ppermute | solution.py:508
  82.4 2.3 %collective-permute-start.17 = (bf16[256,256]{1,0:T(8,128)(2,1)S(1)}, bf16[256,256]{1,0:T(8,128)(2,1)S(1)}, u32[]{:S(2)}, u32[]{:S(2)}) collective-permute-start(bf16[256,256]{1,0:T(8,128)(2,1)S(1)} %get-tuple-element.75), channel_id=1, source_target_pairs={{0,2},{1,3},{2,0},{3,1},{4,6},{5,7},{6,4},{7,5},{8,10},{9,11},{10,... | collective-permute-start | bytes 393224 | tf_op jit(solution)/shard_map/ppermute | solution.py:508
  84.8 0.2 collective-permute-start.18
  84.9 1.5 %collective-permute-done.16.part1 = bf16[256,256]{1,0:T(8,128)(2,1)S(1)} collective-permute-done((bf16[256,256]{1,0:T(8,128)(2,1)S(1)}, bf16[256,256]{1,0:T(8,128)(2,1)S(1)}, u32[]{:S(2)}, u32[]{:S(2)}) %collective-permute-start.16) | collective-permute-done | bytes 131104 | tf_op jit(solution)/shard_map/ppermute | solution.py:508
  86.4 4.2 %collective-permute-done.17.part2 = bf16[256,256]{1,0:T(8,128)(2,1)S(1)} collective-permute-done((bf16[256,256]{1,0:T(8,128)(2,1)S(1)}, bf16[256,256]{1,0:T(8,128)(2,1)S(1)}, u32[]{:S(2)}, u32[]{:S(2)}) %collective-permute-start.17) | collective-permute-done | bytes 131104 | tf_op jit(solution)/shard_map/ppermute | solution.py:508
  90.7 0.0 collective-permute-done.18.part3
  90.7 0.7 shard_map.128
  (21 shorter events, 0.1 us)
Async XLA Ops:
  0.9 6.3 %collective-permute-start = (bf16[2,8,256]{2,1,0:T(8,128)(2,1)S(1)}, bf16[2,8,256]{2,1,0:T(8,128)(2,1)S(1)}, u32[]{:S(2)}, u32[]{:S(2)}) collective-permute-start(bf16[2,8,256]{2,1,0:T(8,128)(2,1)S(1)} %get-tuple-element.43), channel_id=1, source_target_pairs={{4,8},{12,16},{20,24},{28,32},{36,40},{44,48},{52,56},{60,64},{68,... | collective-permute-start | bytes 24584 | tf_op jit(solution)/shard_map/ppermute | solution.py:536
  7.2 12.0 %copy-start = (f32[2,128]{1,0:T(2,128)S(1)}, f32[2,128]{1,0:T(2,128)}, u32[]{:S(2)}) copy-start(f32[2,128]{1,0:T(2,128)} %extra.1) | copy-start | bytes 3076
  7.2 12.0 %copy-start.2 = (f32[2,4,3,256]{3,1,2,0:T(4,128)S(1)}, f32[2,4,3,256]{3,1,2,0:T(4,128)}, u32[]{:S(2)}) copy-start(f32[2,4,3,256]{3,1,2,0:T(4,128)} %param.16) | copy-start | bytes 73732
  7.2 12.0 %copy-start.3 = (f32[1024]{0:T(1024)S(1)}, f32[1024]{0:T(1024)}, u32[]{:S(2)}) copy-start(f32[1024]{0:T(1024)} %param.13) | copy-start | bytes 12292
  7.2 12.0 %copy-start.5 = (f32[4,64]{1,0:T(4,128)S(1)}, f32[4,64]{1,0:T(4,128)}, u32[]{:S(2)}) copy-start(f32[4,64]{1,0:T(4,128)} %rate.1) | copy-start | bytes 3076
  7.2 1.4 %collective-permute-start.1 = (bf16[144,256]{1,0:T(8,128)(2,1)S(1)}, bf16[144,256]{1,0:T(8,128)(2,1)S(1)}, u32[]{:S(2)}, u32[]{:S(2)}) collective-permute-start(bf16[144,256]{1,0:T(8,128)(2,1)S(1)} %get-tuple-element.44), channel_id=1, source_target_pairs={{0,4},{4,0},{1,5},{5,1},{2,6},{6,2},{3,7},{7,3},{8,12},{12,8},{9,1... | collective-permute-start | bytes 221192 | tf_op jit(solution)/shard_map/ppermute | solution.py:540
  8.6 6.7 %collective-permute-start.2 = (bf16[272,256]{1,0:T(8,128)(2,1)S(1)}, bf16[272,256]{1,0:T(8,128)(2,1)S(1)}, u32[]{:S(2)}, u32[]{:S(2)}) collective-permute-start(bf16[272,256]{1,0:T(8,128)(2,1)S(1)} %pad_maximum_fusion.part0), channel_id=1, source_target_pairs={{0,1},{1,2},{2,3},{3,0},{4,5},{5,6},{6,7},{7,4},{8,9},{9,10},{10,1... | collective-permute-start | bytes 417800 | tf_op jit(solution)/shard_map/ppermute | solution.py:508
  10.0 9.2 %collective-permute-start.3 = (bf16[272,256]{1,0:T(8,128)(2,1)S(1)}, bf16[272,256]{1,0:T(8,128)(2,1)S(1)}, u32[]{:S(2)}, u32[]{:S(2)}) collective-permute-start(bf16[272,256]{1,0:T(8,128)(2,1)S(1)} %pad_maximum_fusion.part0), channel_id=1, source_target_pairs={{0,2},{1,3},{2,0},{3,1},{4,6},{5,7},{6,4},{7,5},{8,10},{9,11},{10,... | collective-permute-start | bytes 417800 | tf_op jit(solution)/shard_map/ppermute | solution.py:508
  12.6 6.6 %collective-permute-start.4 = (bf16[272,256]{1,0:T(8,128)(2,1)S(1)}, bf16[272,256]{1,0:T(8,128)(2,1)S(1)}, u32[]{:S(2)}, u32[]{:S(2)}) collective-permute-start(bf16[272,256]{1,0:T(8,128)(2,1)S(1)} %pad_maximum_fusion.part0), channel_id=1, source_target_pairs={{0,3},{1,0},{2,1},{3,2},{4,7},{5,4},{6,5},{7,6},{8,11},{9,8},{10,9... | collective-permute-start | bytes 417800 | tf_op jit(solution)/shard_map/ppermute | solution.py:508
  23.9 21.3 %all-to-all-start = ((bf16[32,24,128]{2,1,0:T(8,128)(2,1)}), bf16[32,24,128]{2,1,0:T(8,128)(2,1)S(1)}, u32[]{:S(2)}, u32[]{:S(2)}) async-start(bf16[32,24,128]{2,1,0:T(8,128)(2,1)} %get-tuple-element.64), calls=%async_computation | async-start | bytes 393216 | tf_op jit(solution)/shard_map/all_to_all | solution.py:603
  35.8 24.0 %copy-start.6 = (f32[4,64]{1,0:T(4,128)S(1)}, f32[4,64]{1,0:T(4,128)}, u32[]{:S(2)}) copy-start(f32[4,64]{1,0:T(4,128)} %gain.3) | copy-start | bytes 3076
  35.8 20.8 %collective-permute-start.9 = (bf16[128,1024]{1,0:T(8,128)(2,1)S(1)}, bf16[128,1024]{1,0:T(8,128)(2,1)S(1)}, u32[]{:S(2)}, u32[]{:S(2)}) collective-permute-start(bf16[128,1024]{1,0:T(8,128)(2,1)S(1)} %get-tuple-element.66), channel_id=1, source_target_pairs={{0,1},{1,2},{2,3},{3,0},{4,5},{5,6},{6,7},{7,4},{8,9},{9,10},{10,1... | collective-permute-start | bytes 786440 | tf_op jit(solution)/shard_map/ppermute | solution.py:508
  36.8 19.9 %collective-permute-start.10 = (bf16[128,1024]{1,0:T(8,128)(2,1)S(1)}, bf16[128,1024]{1,0:T(8,128)(2,1)S(1)}, u32[]{:S(2)}, u32[]{:S(2)}) collective-permute-start(bf16[128,1024]{1,0:T(8,128)(2,1)S(1)} %get-tuple-element.66), channel_id=1, source_target_pairs={{0,2},{1,3},{2,0},{3,1},{4,6},{5,7},{6,4},{7,5},{8,10},{9,11},{10,... | collective-permute-start | bytes 786440 | tf_op jit(solution)/shard_map/ppermute | solution.py:508
  39.1 18.1 %collective-permute-start.11 = (bf16[128,1024]{1,0:T(8,128)(2,1)S(1)}, bf16[128,1024]{1,0:T(8,128)(2,1)S(1)}, u32[]{:S(2)}, u32[]{:S(2)}) collective-permute-start(bf16[128,1024]{1,0:T(8,128)(2,1)S(1)} %get-tuple-element.66), channel_id=1, source_target_pairs={{0,3},{1,0},{2,1},{3,2},{4,7},{5,4},{6,5},{7,6},{8,11},{9,8},{10,9... | collective-permute-start | bytes 786440 | tf_op jit(solution)/shard_map/ppermute | solution.py:508
  45.9 13.8 %all-to-all-start.1 = ((bf16[32,16,128]{2,1,0:T(8,128)(2,1)}), bf16[32,16,128]{2,1,0:T(8,128)(2,1)S(1)}, u32[]{:S(2)}, u32[]{:S(2)}) async-start(bf16[32,16,128]{2,1,0:T(8,128)(2,1)} %shard_map.123), calls=%async_computation.1 | async-start | bytes 262144 | tf_op jit(solution)/shard_map/all_to_all | solution.py:631
  50.6 18.9 %collective-permute-start.15 = (bf16[4,128,256]{2,1,0:T(8,128)(2,1)}, bf16[4,128,256]{2,1,0:T(8,128)(2,1)S(1)}, u32[]{:S(2)}, u32[]{:S(2)}) collective-permute-start(bf16[4,128,256]{2,1,0:T(8,128)(2,1)} %get-tuple-element.68), channel_id=1, source_target_pairs={{0,4},{4,0},{1,5},{5,1},{2,6},{6,2},{3,7},{7,3},{8,12},{12,8},{9,1... | collective-permute-start | bytes 786440 | tf_op jit(solution)/shard_map/ppermute | solution.py:608
  56.6 11.9 %copy-start.7 = (bf16[128,1024]{1,0:T(8,128)(2,1)}, bf16[128,1024]{1,0:T(8,128)(2,1)S(1)}, u32[]{:S(2)}) copy-start(bf16[128,1024]{1,0:T(8,128)(2,1)S(1)} %collective-permute-done.9.mine1) | copy-start | bytes 786436
  56.6 15.1 %collective-permute-start.12 = (bf16[128,1024]{1,0:T(8,128)(2,1)S(1)}, bf16[128,1024]{1,0:T(8,128)(2,1)S(1)}, u32[]{:S(2)}, u32[]{:S(2)}) collective-permute-start(bf16[128,1024]{1,0:T(8,128)(2,1)S(1)} %collective-permute-done.9.mine1), channel_id=1, source_target_pairs={{0,4},{4,0},{1,5},{5,1},{2,6},{6,2},{3,7},{7,3},{8,12},{12,8},{9,1... | collective-permute-start | bytes 786440 | tf_op jit(solution)/shard_map/ppermute | solution.py:607
  56.7 11.8 %copy-start.8 = (bf16[128,1024]{1,0:T(8,128)(2,1)}, bf16[128,1024]{1,0:T(8,128)(2,1)S(1)}, u32[]{:S(2)}) copy-start(bf16[128,1024]{1,0:T(8,128)(2,1)S(1)} %collective-permute-done.10.mine2) | copy-start | bytes 786436
  56.8 15.9 %collective-permute-start.13 = (bf16[128,1024]{1,0:T(8,128)(2,1)S(1)}, bf16[128,1024]{1,0:T(8,128)(2,1)S(1)}, u32[]{:S(2)}, u32[]{:S(2)}) collective-permute-start(bf16[128,1024]{1,0:T(8,128)(2,1)S(1)} %collective-permute-done.10.mine2), channel_id=1, source_target_pairs={{0,4},{4,0},{1,5},{5,1},{2,6},{6,2},{3,7},{7,3},{8,12},{12,8},{9,1... | collective-permute-start | bytes 786440 | tf_op jit(solution)/shard_map/ppermute | solution.py:607
  57.2 11.3 %copy-start.9 = (bf16[128,1024]{1,0:T(8,128)(2,1)}, bf16[128,1024]{1,0:T(8,128)(2,1)S(1)}, u32[]{:S(2)}) copy-start(bf16[128,1024]{1,0:T(8,128)(2,1)S(1)} %collective-permute-done.11.mine3) | copy-start | bytes 786436
  57.2 15.4 %collective-permute-start.14 = (bf16[128,1024]{1,0:T(8,128)(2,1)S(1)}, bf16[128,1024]{1,0:T(8,128)(2,1)S(1)}, u32[]{:S(2)}, u32[]{:S(2)}) collective-permute-start(bf16[128,1024]{1,0:T(8,128)(2,1)S(1)} %collective-permute-done.11.mine3), channel_id=1, source_target_pairs={{0,4},{4,0},{1,5},{5,1},{2,6},{6,2},{3,7},{7,3},{8,12},{12,8},{9,1... | collective-permute-start | bytes 786440 | tf_op jit(solution)/shard_map/ppermute | solution.py:607
  62.2 6.4 %collective-permute-start.5 = (bf16[128,256]{1,0:T(8,128)(2,1)S(1)}, bf16[128,256]{1,0:T(8,128)(2,1)S(1)}, u32[]{:S(2)}, u32[]{:S(2)}) collective-permute-start(bf16[128,256]{1,0:T(8,128)(2,1)S(1)} %shard_map.125), channel_id=1, source_target_pairs={{0,4},{4,0},{1,5},{5,1},{2,6},{6,2},{3,7},{7,3},{8,12},{12,8},{9,1... | collective-permute-start | bytes 196616 | tf_op jit(solution)/shard_map/ppermute | solution.py:659
  68.6 7.5 %collective-permute-start.6 = (bf16[256,256]{1,0:T(8,128)(2,1)S(1)}, bf16[256,256]{1,0:T(8,128)(2,1)S(1)}, u32[]{:S(2)}, u32[]{:S(2)}) collective-permute-start(bf16[256,256]{1,0:T(8,128)(2,1)S(1)} %pad_maximum_fusion.1.part0), channel_id=1, source_target_pairs={{0,1},{1,2},{2,3},{3,0},{4,5},{5,6},{6,7},{7,4},{8,9},{9,10},{10,1... | collective-permute-start | bytes 393224 | tf_op jit(solution)/shard_map/ppermute | solution.py:508
  69.4 3.2 %copy-start.10 = (bf16[4,128,256]{2,1,0:T(8,128)(2,1)}, bf16[4,128,256]{2,1,0:T(8,128)(2,1)S(1)}, u32[]{:S(2)}) copy-start(bf16[4,128,256]{2,1,0:T(8,128)(2,1)S(1)} %collective-permute-done.15.passed) | copy-start | bytes 786436
  69.4 8.7 %collective-permute-start.7 = (bf16[256,256]{1,0:T(8,128)(2,1)S(1)}, bf16[256,256]{1,0:T(8,128)(2,1)S(1)}, u32[]{:S(2)}, u32[]{:S(2)}) collective-permute-start(bf16[256,256]{1,0:T(8,128)(2,1)S(1)} %pad_maximum_fusion.1.part0), channel_id=1, source_target_pairs={{0,2},{1,3},{2,0},{3,1},{4,6},{5,7},{6,4},{7,5},{8,10},{9,11},{10,... | collective-permute-start | bytes 393224 | tf_op jit(solution)/shard_map/ppermute | solution.py:508
  71.8 0.9 copy-start.11
  71.8 6.4 %collective-permute-start.8 = (bf16[256,256]{1,0:T(8,128)(2,1)S(1)}, bf16[256,256]{1,0:T(8,128)(2,1)S(1)}, u32[]{:S(2)}, u32[]{:S(2)}) collective-permute-start(bf16[256,256]{1,0:T(8,128)(2,1)S(1)} %pad_maximum_fusion.1.part0), channel_id=1, source_target_pairs={{0,3},{1,0},{2,1},{3,2},{4,7},{5,4},{6,5},{7,6},{8,11},{9,8},{10,9... | collective-permute-start | bytes 393224 | tf_op jit(solution)/shard_map/ppermute | solution.py:508
  72.6 0.7 copy-start.12
  72.6 0.8 copy-start.13
  73.4 4.7 %copy-start.1 = (bf16[1024,1024]{1,0:T(8,128)(2,1)S(1)}, bf16[1024,1024]{1,0:T(8,128)(2,1)}, u32[]{:S(2)}) copy-start(bf16[1024,1024]{1,0:T(8,128)(2,1)} %up.1) | copy-start | bytes 6291460
  73.4 4.7 %copy-start.4 = (f32[1024]{0:T(1024)S(1)}, f32[1024]{0:T(1024)}, u32[]{:S(2)}) copy-start(f32[1024]{0:T(1024)} %param.21) | copy-start | bytes 12292
  80.5 5.9 %collective-permute-start.16 = (bf16[256,256]{1,0:T(8,128)(2,1)S(1)}, bf16[256,256]{1,0:T(8,128)(2,1)S(1)}, u32[]{:S(2)}, u32[]{:S(2)}) collective-permute-start(bf16[256,256]{1,0:T(8,128)(2,1)S(1)} %get-tuple-element.74), channel_id=1, source_target_pairs={{0,1},{1,2},{2,3},{3,0},{4,5},{5,6},{6,7},{7,4},{8,9},{9,10},{10,1... | collective-permute-start | bytes 393224 | tf_op jit(solution)/shard_map/ppermute | solution.py:508
  82.4 8.2 %collective-permute-start.17 = (bf16[256,256]{1,0:T(8,128)(2,1)S(1)}, bf16[256,256]{1,0:T(8,128)(2,1)S(1)}, u32[]{:S(2)}, u32[]{:S(2)}) collective-permute-start(bf16[256,256]{1,0:T(8,128)(2,1)S(1)} %get-tuple-element.75), channel_id=1, source_target_pairs={{0,2},{1,3},{2,0},{3,1},{4,6},{5,7},{6,4},{7,5},{8,10},{9,11},{10,... | collective-permute-start | bytes 393224 | tf_op jit(solution)/shard_map/ppermute | solution.py:508
  84.8 5.9 %collective-permute-start.18 = (bf16[256,256]{1,0:T(8,128)(2,1)S(1)}, bf16[256,256]{1,0:T(8,128)(2,1)S(1)}, u32[]{:S(2)}, u32[]{:S(2)}) collective-permute-start(bf16[256,256]{1,0:T(8,128)(2,1)S(1)} %get-tuple-element.76), channel_id=1, source_target_pairs={{0,3},{1,0},{2,1},{3,2},{4,7},{5,4},{6,5},{7,6},{8,11},{9,8},{10,9... | collective-permute-start | bytes 393224 | tf_op jit(solution)/shard_map/ppermute | solution.py:508

commit v6 on v5

--- a/solution.py
+++ b/solution.py
@@ -152,35 +152,38 @@
     swap_out[128:136] = packed.astype(BF16)
 
 
-def swap_kernel(local_part, edges, swap_out, kept_out):
+def pick_kernel(edges, sent_out, kept_out):
     core = lax.axis_index("core")
-    swap_out[0:136] = local_part[...]
-    swap_out[136:144] = edges[1 - core]
+    sent_out[...] = edges[1 - core]
     kept_out[...] = edges[core]
 
 
 def front_kernel(
-    part0, part1, part2, part3, gain, qkv_weight, gate_weight, taps, rate, extra, extra_other,
+    part0, part1, part2, part3, halo0, halo1, halo2, halo3, gain, qkv_weight, gate_weight, taps, rate, extra, extra_other,
     sent_out, query_out, kv_out, cum_out, shrink_out, start_out, reach_out, kept_out, passed_out,
     padded, decay, query, kv, cum, shrink, start, reach, kept, passed_on, semaphores,
 ):
     core = lax.axis_index("core")
     head = lax.axis_index("head")
     parts = (part0, part1, part2, part3)
+    halos = (halo0, halo1, halo2, halo3)
     sources = [lax.rem(head + 4 - k, 4) for k in range(4)]
     own_rows = pl.multiple_of(core * 128, 128)
     other_rows = pl.multiple_of((1 - core) * 128, 128)
     square = jnp.zeros((ROWS + 16, 1), F32)
     for k in range(4):
-        values = parts[k][...]
-        kept[sources[k]] = values[0:128]
-        passed_on[sources[k]] = values[128:256]
-        wide = values.astype(F32)
+        kept[sources[k]] = parts[k][0:128]
+        passed_on[sources[k]] = parts[k][128:256]
+        wide = jnp.concatenate([parts[k][...], halos[k][...]], axis=0).astype(F32)
         square = square + jnp.sum(wide * wide, axis=1, keepdims=True)
     going = begin([(kept, kept_out), (passed_on, passed_out)], semaphores.at[pl.ds(0, 2)])
     scale = lax.rsqrt(square * (1.0 / 1024.0) + EPSILON)
     normed = [
-        (parts[k][...].astype(F32) * scale * gain_of(gain, sources[k])).astype(BF16)
+        (
+            jnp.concatenate([parts[k][...], halos[k][...]], axis=0).astype(F32)
+            * scale
+            * gain_of(gain, sources[k])
+        ).astype(BF16)
         for k in range(4)
     ]
     starts = [pl.multiple_of(source * 256, 256) for source in sources]
@@ -534,11 +537,15 @@
     ahead = [(2 * i - 1, 2 * i) for i in range(1, chips)]
     behind = [(2 * i + 2, 2 * i + 1) for i in range(chips - 1)]
     edges = lax.ppermute(edges, SEQ, ahead + behind)
-    swap, kept_edge = kernel(
-        swap_kernel, "vv", [((144, 256), BF16, "v"), ((8, 256), BF16, "v")]
-    )(swap, edges)
     other = lax.ppermute(swap, "core", swap_pairs)
-    rows = jnp.concatenate([mine, other[:128], kept_edge, other[136:]], axis=0)
+    rows = jnp.concatenate([mine, other[:128]], axis=0)
+    pick = kernel(pick_kernel, "v", [((8, 256), BF16, "v"), ((8, 256), BF16, "v")])
+    sent_edge, kept_edge = pick(edges)
+    other_edge = lax.ppermute(sent_edge, "core", swap_pairs)
+    halo = jnp.concatenate([kept_edge, other_edge], axis=0)
+    halos = [halo]
+    for k in (1, 2, 3):
+        halos.append(shifted(halo, k))
     qkv_weight = jnp.transpose(query_key_value_weight, (1, 0, 2))
     rows, qkv_weight, gate_weight, out_weight = lax.optimization_barrier(
         (rows, qkv_weight, forget_gate_weight, output_projection_weight)
@@ -563,7 +570,7 @@
     reaches = (2, SPANS, SPAN, LANES)
     pieces, query, kv, cum, shrink, start, reach, kept, passed = kernel(
         front_kernel,
-        "v" * 11,
+        "v" * 15,
         [
             ((32, 24, 128), BF16, "v"),
             ((ROWS + 16, 256), BF16, "h"),
@@ -591,6 +598,7 @@
         flops=10**9,
     )(
         *parts,
+        *halos,
         input_norm_gain.reshape(8, 128),
         qkv_weight,
         gate_weight,

time: 91.7 us -> 94.5 us (1.031)
  starting transfers between devices: 46.7 us -> 51.1 us
  waiting for transfers between devices: 21.7 us -> 19.5 us
    ppermute x1, starting transfers between devices: 2.66 us -> 4.48 us  [local(): passed = lax.ppermute(passed, 'core', swap_pairs)]
    all_to_all x1, waiting for transfers between devices: 2.19 us -> 0.52 us  [local(): lax.all_to_all(prefixes, CHIPS, split_axis=0, concat_axis=0, tiled=True)]
    ppermute x1, starting transfers between devices: 3.94 us -> 5.44 us  [local(): swapped = lax.ppermute(attention[0], 'core', swap_pairs)]
    ppermute x1, waiting for transfers between devices: 1.25 us -> 0.02 us  [local(): other = lax.ppermute(swap, 'core', swap_pairs)]
    all_to_all x1, starting transfers between devices: 11.9 us -> 12.9 us  [local(): lax.all_to_all(pieces, CHIPS, split_axis=0, concat_axis=0, tiled=True)]
    all_to_all x1, waiting for transfers between devices: 5.18 us -> 6.13 us  [local(): lax.all_to_all(pieces, CHIPS, split_axis=0, concat_axis=0, tiled=True)]
    ppermute x12 -> x15, starting transfers between devices: 17.7 us -> 18.3 us  [shifted(): lax.ppermute(value, 'head', [(j, (j + k) % count) for j in range(count)])]
    ppermute x12 -> x15, waiting for transfers between devices: 11.7 us -> 11.6 us  [shifted(): lax.ppermute(value, 'head', [(j, (j + k) % count) for j in range(count)])]
  transfers between devices with their start and end apart: 21 -> 25, of which waited for: 8 -> 8; matrix products, arithmetic and copies ran while one was open for 0% -> 0% of each run, Pallas kernels for 14% -> 14%
where the time goes in v6:
time: 94.5 us; the launch traced here: 94.1 us
  starting transfers between devices  51.1 us (54%)
  Pallas kernels  22.3 us (24%)
  waiting for transfers between devices  19.5 us (21%)
    pallas_call x11, Pallas kernels, placed(): call(*[pltpu.with_memory_space_constraint(array, pltpu.HBM) if place == '...  22.3 us
    ppermute x15, starting transfers between devices, shifted(): lax.ppermute(value, 'head', [(j, (j + k) % count) for j in range(count)])  18.3 us
    all_to_all x1, starting transfers between devices, local(): lax.all_to_all(pieces, CHIPS, split_axis=0, concat_axis=0, tiled=True)  12.9 us
    ppermute x15, waiting for transfers between devices, shifted(): lax.ppermute(value, 'head', [(j, (j + k) % count) for j in range(count)])  11.6 us
    all_to_all x1, waiting for transfers between devices, local(): lax.all_to_all(pieces, CHIPS, split_axis=0, concat_axis=0, tiled=True)  6.13 us
    ppermute x1, starting transfers between devices, local(): swapped = lax.ppermute(attention[0], 'core', swap_pairs)  5.44 us
    ppermute x1, starting transfers between devices, local(): edges = lax.ppermute(edges, SEQ, ahead + behind)  5.06 us
    ppermute x1, starting transfers between devices, local(): passed = lax.ppermute(passed, 'core', swap_pairs)  4.48 us
  transfers between devices with their start and end apart: 25, of which 8 were waited for; matrix products, arithmetic and copies ran while one was open for 0% of the time, Pallas kernels for 14%

profile of v6, /device:TPU:1, one launch (start us, length us, event | category | flops | bytes accessed | tf_op | source)
XLA Modules:
  0.0 94.1 jit_solution(11095854307544514206)
XLA Ops:
  0.0 0.9 %shard_map.118 = (bf16[2,8,256]{2,1,0:T(8,128)(2,1)S(1)}, bf16[136,256]{1,0:T(8,128)(2,1)S(1)}, bf16[128,256]{1,0:T(8,128)(2,1)S(1)}) custom-call(bf16[2,128,256]{2,1,0:T(8,128)(2,1)} %tokens_in.1, f32[2,128]{1,0:T(2,128)} %extra.1), custom_call_target="tpu_custom_call" | custom-call | bytes 1048576 | tf_op jit(solution)/shard_map/pallas_call | solution.py:499
  0.9 0.0 copy-start
  1.0 0.0 copy-start.2
  1.0 0.0 copy-start.3
  1.0 0.0 copy-start.5
  1.0 5.1 %collective-permute-start.4 = (bf16[2,8,256]{2,1,0:T(8,128)(2,1)S(1)}, bf16[2,8,256]{2,1,0:T(8,128)(2,1)S(1)}, u32[]{:S(2)}, u32[]{:S(2)}) collective-permute-start(bf16[2,8,256]{2,1,0:T(8,128)(2,1)S(1)} %get-tuple-element.44), channel_id=1, source_target_pairs={{4,8},{12,16},{20,24},{28,32},{36,40},{44,48},{52,56},{60,64},{68,... | collective-permute-start | bytes 24584 | tf_op jit(solution)/shard_map/ppermute | solution.py:539
  6.1 0.1 collective-permute-start
  6.2 1.2 %collective-permute-done.4.edges = bf16[2,8,256]{2,1,0:T(8,128)(2,1)S(1)} collective-permute-done((bf16[2,8,256]{2,1,0:T(8,128)(2,1)S(1)}, bf16[2,8,256]{2,1,0:T(8,128)(2,1)S(1)}, u32[]{:S(2)}, u32[]{:S(2)}) %collective-permute-start.4) | collective-permute-done | bytes 8224 | tf_op jit(solution)/shard_map/ppermute | solution.py:539
  7.4 0.0 collective-permute-start.5
  7.4 0.0 collective-permute-done
  7.4 1.4 %collective-permute-start.1 = (bf16[256,256]{1,0:T(8,128)(2,1)S(1)}, bf16[256,256]{1,0:T(8,128)(2,1)S(1)}, u32[]{:S(2)}, u32[]{:S(2)}) collective-permute-start(bf16[256,256]{1,0:T(8,128)(2,1)S(1)} %pad_maximum_fusion.part0), channel_id=1, source_target_pairs={{0,1},{1,2},{2,3},{3,0},{4,5},{5,6},{6,7},{7,4},{8,9},{9,10},{10,1... | collective-permute-start | bytes 393224 | tf_op jit(solution)/shard_map/ppermute | solution.py:511
  8.8 2.6 %collective-permute-start.2 = (bf16[256,256]{1,0:T(8,128)(2,1)S(1)}, bf16[256,256]{1,0:T(8,128)(2,1)S(1)}, u32[]{:S(2)}, u32[]{:S(2)}) collective-permute-start(bf16[256,256]{1,0:T(8,128)(2,1)S(1)} %pad_maximum_fusion.part0), channel_id=1, source_target_pairs={{0,2},{1,3},{2,0},{3,1},{4,6},{5,7},{6,4},{7,5},{8,10},{9,11},{10,... | collective-permute-start | bytes 393224 | tf_op jit(solution)/shard_map/ppermute | solution.py:511
  11.4 1.1 %collective-permute-start.3 = (bf16[256,256]{1,0:T(8,128)(2,1)S(1)}, bf16[256,256]{1,0:T(8,128)(2,1)S(1)}, u32[]{:S(2)}, u32[]{:S(2)}) collective-permute-start(bf16[256,256]{1,0:T(8,128)(2,1)S(1)} %pad_maximum_fusion.part0), channel_id=1, source_target_pairs={{0,3},{1,0},{2,1},{3,2},{4,7},{5,4},{6,5},{7,6},{8,11},{9,8},{10,9... | collective-permute-start | bytes 393224 | tf_op jit(solution)/shard_map/ppermute | solution.py:511
  12.5 0.0 collective-permute-done.5
  12.5 0.4 collective-permute-start.6
  12.9 0.9 collective-permute-start.7
  13.8 2.8 %collective-permute-done.6.halo1 = bf16[16,256]{1,0:T(8,128)(2,1)S(1)} collective-permute-done((bf16[16,256]{1,0:T(8,128)(2,1)S(1)}, bf16[16,256]{1,0:T(8,128)(2,1)S(1)}, u32[]{:S(2)}, u32[]{:S(2)}) %collective-permute-start.6) | collective-permute-done | bytes 8224 | tf_op jit(solution)/shard_map/ppermute | solution.py:511
  16.5 1.3 %collective-permute-start.8 = (bf16[16,256]{1,0:T(8,128)(2,1)S(1)}, bf16[16,256]{1,0:T(8,128)(2,1)S(1)}, u32[]{:S(2)}, u32[]{:S(2)}) collective-permute-start(bf16[16,256]{1,0:T(8,128)(2,1)S(1)} %constant_dynamic-update-slice_fusion.halo0), channel_id=1, source_target_pairs={{0,3},{1,0},{2,1},{3,2},{4,7},{5,4},{6,5},{7,6},{8,11},{9,8},{10,9... | collective-permute-start | bytes 24584 | tf_op jit(solution)/shard_map/ppermute | solution.py:511
  17.8 1.6 %shard_map.120 = (bf16[3,1024,256]{2,1,0:T(8,128)(2,1)S(1)}, bf16[1024,256]{1,0:T(8,128)(2,1)S(1)}, bf16[128,1024]{1,0:T(8,128)(2,1)S(1)}) custom-call(bf16[3,1024,256]{2,1,0:T(8,128)(2,1)} %bitcast.8, bf16[1024,256]{1,0:T(8,128)(2,1)} %gate_weight, bf16[256,1024]{1,0:T(8,128)(2,1)} %weight0.1), custom_call_target="tpu_custom_call" | custom-call | flops 1000000000 | bytes 1048576 | tf_op jit(solution)/shard_map/pallas_call | solution.py:499
  19.4 0.0 collective-permute-done.7.halo2
  19.4 0.0 collective-permute-done.8.halo3
  19.4 0.0 collective-permute-done.1.part1
  19.5 0.0 collective-permute-done.2.part2
  19.5 0.0 collective-permute-done.3.part3
  19.5 5.0 %shard_map.121 = (bf16[32,24,128]{2,1,0:T(8,128)(2,1)}, bf16[272,256]{1,0:T(8,128)(2,1)}, bf16[2,2,256,256]{3,2,1,0:T(8,128)(2,1)}, f32[2,256,256]{2,1,0:T(8,128...) custom-call(bf16[256,256]{1,0:T(8,128)(2,1)S(1)} %pad_maximum_fusion, ...), custom_call_target="tpu_custom_call" | custom-call | flops 1000000000 | bytes 1048576 | tf_op jit(solution)/shard_map/pallas_call | solution.py:499
  24.5 12.9 %all-to-all-start = ((bf16[32,24,128]{2,1,0:T(8,128)(2,1)}), bf16[32,24,128]{2,1,0:T(8,128)(2,1)S(1)}, u32[]{:S(2)}, u32[]{:S(2)}) async-start(bf16[32,24,128]{2,1,0:T(8,128)(2,1)} %get-tuple-element.64), calls=%async_computation | async-start | bytes 393216 | tf_op jit(solution)/shard_map/all_to_all | solution.py:611
  37.4 0.0 copy-start.6
  37.4 0.6 collective-permute-start.13
  38.0 2.7 %collective-permute-start.14 = (bf16[128,1024]{1,0:T(8,128)(2,1)S(1)}, bf16[128,1024]{1,0:T(8,128)(2,1)S(1)}, u32[]{:S(2)}, u32[]{:S(2)}) collective-permute-start(bf16[128,1024]{1,0:T(8,128)(2,1)S(1)} %get-tuple-element.66), channel_id=1, source_target_pairs={{0,2},{1,3},{2,0},{3,1},{4,6},{5,7},{6,4},{7,5},{8,10},{9,11},{10,... | collective-permute-start | bytes 786440 | tf_op jit(solution)/shard_map/ppermute | solution.py:511
  40.8 0.0 collective-permute-start.15
  40.8 6.1 %all-to-all-done.pieces = bf16[32,24,128]{2,1,0:T(8,128)(2,1)S(1)} async-done(((bf16[32,24,128]{2,1,0:T(8,128)(2,1)}), bf16[32,24,128]{2,1,0:T(8,128)(2,1)S(1)}, u32[]{:S(2)}, u32[]{:S(2)}) %all-to-all-start) | async-done | bytes 196640 | tf_op jit(solution)/shard_map/all_to_all | solution.py:611
  46.9 0.8 shard_map.123
  47.7 4.1 %all-to-all-start.1 = ((bf16[32,16,128]{2,1,0:T(8,128)(2,1)}), bf16[32,16,128]{2,1,0:T(8,128)(2,1)S(1)}, u32[]{:S(2)}, u32[]{:S(2)}) async-start(bf16[32,16,128]{2,1,0:T(8,128)(2,1)} %shard_map.123), calls=%async_computation.1 | async-start | bytes 262144 | tf_op jit(solution)/shard_map/all_to_all | solution.py:639
  51.8 4.5 %collective-permute-start.19 = (bf16[4,128,256]{2,1,0:T(8,128)(2,1)}, bf16[4,128,256]{2,1,0:T(8,128)(2,1)S(1)}, u32[]{:S(2)}, u32[]{:S(2)}) collective-permute-start(bf16[4,128,256]{2,1,0:T(8,128)(2,1)} %get-tuple-element.68), channel_id=1, source_target_pairs={{0,4},{4,0},{1,5},{5,1},{2,6},{6,2},{3,7},{7,3},{8,12},{12,8},{9,1... | collective-permute-start | bytes 786440 | tf_op jit(solution)/shard_map/ppermute | solution.py:616
  56.3 3.4 %shard_map.122 = (bf16[2,256,256]{2,1,0:T(8,128)(2,1)}, f32[2,256,256]{2,1,0:T(8,128)}, f32[2,256,256]{2,1,0:T(8,128)}) custom-call(bf16[272,256]{1,0:T(8,128)(2,1)} %get-tuple-element.52.query_in, bf16[2,2,256,256]{3,2,1,0:T(8,128)(2,1)} %get-tuple-element.53.kv_in, f32[2,256,256]{2,1,0:T(8,128)} %get-tuple-element.54.cum_in, ...), custom_call_target="tpu_custom_call" | custom-call | flops 1000000000 | bytes 1048576 | tf_op jit(solution)/shard_map/pallas_call | solution.py:499
  59.7 0.1 collective-permute-start.16
  59.8 0.0 collective-permute-done.14.mine2
  59.8 0.5 collective-permute-start.17
  60.3 0.0 collective-permute-done.15.mine3
  60.3 0.1 collective-permute-start.18
  60.4 0.5 all-to-all-done.1.arrived
  60.9 2.4 %shard_map.125 = bf16[128,256]{1,0:T(8,128)(2,1)S(1)} custom-call(bf16[2,256,256]{2,1,0:T(8,128)(2,1)} %get-tuple-element.57.queries_in, bf16[2,2,256,256]{3,2,1,0:T(8,128)(2,1)} %get-tuple-element.53.kv_in, bf16[2,256,256]{2,1,0:T(8,128)(2,1)} %get-tuple-element.55.shrink_in, bf16[2,4,2,64,256]{4,3,2,1,0:T(8,128)(2,1)} %get-tuple-element.56.start_in, ...), custom_call_target="tpu_custom_call" | custom-call | flops 1000000000 | bytes 1048576 | tf_op jit(solution)/shard_map/pallas_call | solution.py:499
  63.4 5.4 %collective-permute-start.9 = (bf16[128,256]{1,0:T(8,128)(2,1)S(1)}, bf16[128,256]{1,0:T(8,128)(2,1)S(1)}, u32[]{:S(2)}, u32[]{:S(2)}) collective-permute-start(bf16[128,256]{1,0:T(8,128)(2,1)S(1)} %shard_map.125), channel_id=1, source_target_pairs={{0,4},{4,0},{1,5},{5,1},{2,6},{6,2},{3,7},{7,3},{8,12},{12,8},{9,1... | collective-permute-start | bytes 196616 | tf_op jit(solution)/shard_map/ppermute | solution.py:667
  68.8 2.4 %shard_map.124 = bf16[128,256]{1,0:T(8,128)(2,1)S(1)} custom-call(bf16[2,256,256]{2,1,0:T(8,128)(2,1)} %get-tuple-element.57.queries_in, bf16[2,2,256,256]{3,2,1,0:T(8,128)(2,1)} %get-tuple-element.53.kv_in, bf16[2,256,256]{2,1,0:T(8,128)(2,1)} %get-tuple-element.55.shrink_in, bf16[2,4,2,64,256]{4,3,2,1,0:T(8,128)(2,1)} %get-tuple-element.56.start_in, ...), custom_call_target="tpu_custom_call" | custom-call | flops 1000000000 | bytes 1048576 | tf_op jit(solution)/shard_map/pallas_call | solution.py:499
  71.3 0.1 collective-permute-start.10
  71.4 2.6 %collective-permute-start.11 = (bf16[256,256]{1,0:T(8,128)(2,1)S(1)}, bf16[256,256]{1,0:T(8,128)(2,1)S(1)}, u32[]{:S(2)}, u32[]{:S(2)}) collective-permute-start(bf16[256,256]{1,0:T(8,128)(2,1)S(1)} %pad_maximum_fusion.1.part0), channel_id=1, source_target_pairs={{0,2},{1,3},{2,0},{3,1},{4,6},{5,7},{6,4},{7,5},{8,10},{9,11},{10,... | collective-permute-start | bytes 393224 | tf_op jit(solution)/shard_map/ppermute | solution.py:511
  74.0 0.0 collective-permute-done.16.theirs1
  74.0 0.4 collective-permute-start.12
  74.4 0.0 collective-permute-done.18.theirs3
  74.4 0.3 copy-done.11
  74.8 0.4 copy-done.12
  75.1 0.1 copy-done.13
  75.2 2.6 %shard_map.126 = (bf16[4,256,1024]{2,1,0:T(8,128)(2,1)S(1)}, bf16[4,256,256]{2,1,0:T(8,128)(2,1)S(1)}, bf16[1024,1024]{1,0:T(8,128)(2,1)S(1)}) custom-call(bf16[256,1024]{1,0:T(8,128)(2,1)} %weight0.1, bf16[128,1024]{1,0:T(8,128)(2,1)} %copy-done.7, bf16[128,1024]{1,0:T(8,128)(2,1)} %copy-done.8, bf16[128,1024]{1,0:T(8,128)(2,1)} %copy-done.9, ...), custom_call_target="tpu_custom_call" | custom-call | flops 1000000000 | bytes 1048576 | tf_op jit(solution)/shard_map/pallas_call | solution.py:499
  77.8 0.0 collective-permute-done.10.part1
  77.9 2.6 %collective-permute-done.11.part2 = bf16[256,256]{1,0:T(8,128)(2,1)S(1)} collective-permute-done((bf16[256,256]{1,0:T(8,128)(2,1)S(1)}, bf16[256,256]{1,0:T(8,128)(2,1)S(1)}, u32[]{:S(2)}, u32[]{:S(2)}) %collective-permute-start.11) | collective-permute-done | bytes 131104 | tf_op jit(solution)/shard_map/ppermute | solution.py:511
  80.4 0.4 collective-permute-done.12.part3
  80.8 2.4 %shard_map.127 = (f32[256,256]{1,0:T(8,128)S(1)}, bf16[256,256]{1,0:T(8,128)(2,1)S(1)}, bf16[256,256]{1,0:T(8,128)(2,1)S(1)}, bf16[256,256]{1,0:T(8,128)(2,1)S(1)}) custom-call(bf16[256,256]{1,0:T(8,128)(2,1)S(1)} %pad_maximum_fusion.1.part0, bf16[256,256]{1,0:T(8,128)(2,1)S(1)} %collective-permute-done.10.part1, ...), custom_call_target="tpu_custom_call" | custom-call | flops 2000000000 | bytes 1048576 | tf_op jit(solution)/shard_map/pallas_call | solution.py:499
  83.2 1.0 %collective-permute-start.20 = (bf16[256,256]{1,0:T(8,128)(2,1)S(1)}, bf16[256,256]{1,0:T(8,128)(2,1)S(1)}, u32[]{:S(2)}, u32[]{:S(2)}) collective-permute-start(bf16[256,256]{1,0:T(8,128)(2,1)S(1)} %get-tuple-element.74), channel_id=1, source_target_pairs={{0,1},{1,2},{2,3},{3,0},{4,5},{5,6},{6,7},{7,4},{8,9},{9,10},{10,1... | collective-permute-start | bytes 393224 | tf_op jit(solution)/shard_map/ppermute | solution.py:511
  84.2 3.2 %collective-permute-start.21 = (bf16[256,256]{1,0:T(8,128)(2,1)S(1)}, bf16[256,256]{1,0:T(8,128)(2,1)S(1)}, u32[]{:S(2)}, u32[]{:S(2)}) collective-permute-start(bf16[256,256]{1,0:T(8,128)(2,1)S(1)} %get-tuple-element.75), channel_id=1, source_target_pairs={{0,2},{1,3},{2,0},{3,1},{4,6},{5,7},{6,4},{7,5},{8,10},{9,11},{10,... | collective-permute-start | bytes 393224 | tf_op jit(solution)/shard_map/ppermute | solution.py:511
  87.5 0.0 collective-permute-start.22
  87.5 1.6 %collective-permute-done.20.part1 = bf16[256,256]{1,0:T(8,128)(2,1)S(1)} collective-permute-done((bf16[256,256]{1,0:T(8,128)(2,1)S(1)}, bf16[256,256]{1,0:T(8,128)(2,1)S(1)}, u32[]{:S(2)}, u32[]{:S(2)}) %collective-permute-start.20) | collective-permute-done | bytes 131104 | tf_op jit(solution)/shard_map/ppermute | solution.py:511
  89.1 4.3 %collective-permute-done.21.part2 = bf16[256,256]{1,0:T(8,128)(2,1)S(1)} collective-permute-done((bf16[256,256]{1,0:T(8,128)(2,1)S(1)}, bf16[256,256]{1,0:T(8,128)(2,1)S(1)}, u32[]{:S(2)}, u32[]{:S(2)}) %collective-permute-start.21) | collective-permute-done | bytes 131104 | tf_op jit(solution)/shard_map/ppermute | solution.py:511
  93.4 0.0 collective-permute-done.22.part3
  93.4 0.7 shard_map.128
  (31 shorter events, 0.1 us)
Async XLA Ops:
  0.9 18.5 %copy-start = (f32[2,128]{1,0:T(2,128)S(1)}, f32[2,128]{1,0:T(2,128)}, u32[]{:S(2)}) copy-start(f32[2,128]{1,0:T(2,128)} %extra.1) | copy-start | bytes 3076
  1.0 18.5 %copy-start.2 = (f32[2,4,3,256]{3,1,2,0:T(4,128)S(1)}, f32[2,4,3,256]{3,1,2,0:T(4,128)}, u32[]{:S(2)}) copy-start(f32[2,4,3,256]{3,1,2,0:T(4,128)} %param.16) | copy-start | bytes 73732
  1.0 18.5 %copy-start.3 = (f32[1024]{0:T(1024)S(1)}, f32[1024]{0:T(1024)}, u32[]{:S(2)}) copy-start(f32[1024]{0:T(1024)} %param.13) | copy-start | bytes 12292
  1.0 18.5 %copy-start.5 = (f32[4,64]{1,0:T(4,128)S(1)}, f32[4,64]{1,0:T(4,128)}, u32[]{:S(2)}) copy-start(f32[4,64]{1,0:T(4,128)} %rate.1) | copy-start | bytes 3076
  1.0 6.4 %collective-permute-start.4 = (bf16[2,8,256]{2,1,0:T(8,128)(2,1)S(1)}, bf16[2,8,256]{2,1,0:T(8,128)(2,1)S(1)}, u32[]{:S(2)}, u32[]{:S(2)}) collective-permute-start(bf16[2,8,256]{2,1,0:T(8,128)(2,1)S(1)} %get-tuple-element.44), channel_id=1, source_target_pairs={{4,8},{12,16},{20,24},{28,32},{36,40},{44,48},{52,56},{60,64},{68,... | collective-permute-start | bytes 24584 | tf_op jit(solution)/shard_map/ppermute | solution.py:539
  6.1 1.3 %collective-permute-start = (bf16[136,256]{1,0:T(8,128)(2,1)S(1)}, bf16[136,256]{1,0:T(8,128)(2,1)S(1)}, u32[]{:S(2)}, u32[]{:S(2)}) collective-permute-start(bf16[136,256]{1,0:T(8,128)(2,1)S(1)} %get-tuple-element.42), channel_id=1, source_target_pairs={{0,4},{4,0},{1,5},{5,1},{2,6},{6,2},{3,7},{7,3},{8,12},{12,8},{9,1... | collective-permute-start | bytes 208904 | tf_op jit(solution)/shard_map/ppermute | solution.py:540
  7.4 5.1 %collective-permute-start.5 = (bf16[8,256]{1,0:T(8,128)(2,1)S(1)}, bf16[8,256]{1,0:T(8,128)(2,1)S(1)}, u32[]{:S(2)}, u32[]{:S(2)}) collective-permute-start(bf16[8,256]{1,0:T(8,128)(2,1)S(1)} %get-tuple-element.46), channel_id=1, source_target_pairs={{0,4},{4,0},{1,5},{5,1},{2,6},{6,2},{3,7},{7,3},{8,12},{12,8},{9,1... | collective-permute-start | bytes 12296 | tf_op jit(solution)/shard_map/ppermute | solution.py:544
  7.4 12.0 %collective-permute-start.1 = (bf16[256,256]{1,0:T(8,128)(2,1)S(1)}, bf16[256,256]{1,0:T(8,128)(2,1)S(1)}, u32[]{:S(2)}, u32[]{:S(2)}) collective-permute-start(bf16[256,256]{1,0:T(8,128)(2,1)S(1)} %pad_maximum_fusion.part0), channel_id=1, source_target_pairs={{0,1},{1,2},{2,3},{3,0},{4,5},{5,6},{6,7},{7,4},{8,9},{9,10},{10,1... | collective-permute-start | bytes 393224 | tf_op jit(solution)/shard_map/ppermute | solution.py:511
  8.8 10.6 %collective-permute-start.2 = (bf16[256,256]{1,0:T(8,128)(2,1)S(1)}, bf16[256,256]{1,0:T(8,128)(2,1)S(1)}, u32[]{:S(2)}, u32[]{:S(2)}) collective-permute-start(bf16[256,256]{1,0:T(8,128)(2,1)S(1)} %pad_maximum_fusion.part0), channel_id=1, source_target_pairs={{0,2},{1,3},{2,0},{3,1},{4,6},{5,7},{6,4},{7,5},{8,10},{9,11},{10,... | collective-permute-start | bytes 393224 | tf_op jit(solution)/shard_map/ppermute | solution.py:511
  11.4 8.0 %collective-permute-start.3 = (bf16[256,256]{1,0:T(8,128)(2,1)S(1)}, bf16[256,256]{1,0:T(8,128)(2,1)S(1)}, u32[]{:S(2)}, u32[]{:S(2)}) collective-permute-start(bf16[256,256]{1,0:T(8,128)(2,1)S(1)} %pad_maximum_fusion.part0), channel_id=1, source_target_pairs={{0,3},{1,0},{2,1},{3,2},{4,7},{5,4},{6,5},{7,6},{8,11},{9,8},{10,9... | collective-permute-start | bytes 393224 | tf_op jit(solution)/shard_map/ppermute | solution.py:511
  12.5 4.0 %collective-permute-start.6 = (bf16[16,256]{1,0:T(8,128)(2,1)S(1)}, bf16[16,256]{1,0:T(8,128)(2,1)S(1)}, u32[]{:S(2)}, u32[]{:S(2)}) collective-permute-start(bf16[16,256]{1,0:T(8,128)(2,1)S(1)} %constant_dynamic-update-slice_fusion.halo0), channel_id=1, source_target_pairs={{0,1},{1,2},{2,3},{3,0},{4,5},{5,6},{6,7},{7,4},{8,9},{9,10},{10,1... | collective-permute-start | bytes 24584 | tf_op jit(solution)/shard_map/ppermute | solution.py:511
  12.9 6.5 %collective-permute-start.7 = (bf16[16,256]{1,0:T(8,128)(2,1)S(1)}, bf16[16,256]{1,0:T(8,128)(2,1)S(1)}, u32[]{:S(2)}, u32[]{:S(2)}) collective-permute-start(bf16[16,256]{1,0:T(8,128)(2,1)S(1)} %constant_dynamic-update-slice_fusion.halo0), channel_id=1, source_target_pairs={{0,2},{1,3},{2,0},{3,1},{4,6},{5,7},{6,4},{7,5},{8,10},{9,11},{10,... | collective-permute-start | bytes 24584 | tf_op jit(solution)/shard_map/ppermute | solution.py:511
  16.5 2.9 %collective-permute-start.8 = (bf16[16,256]{1,0:T(8,128)(2,1)S(1)}, bf16[16,256]{1,0:T(8,128)(2,1)S(1)}, u32[]{:S(2)}, u32[]{:S(2)}) collective-permute-start(bf16[16,256]{1,0:T(8,128)(2,1)S(1)} %constant_dynamic-update-slice_fusion.halo0), channel_id=1, source_target_pairs={{0,3},{1,0},{2,1},{3,2},{4,7},{5,4},{6,5},{7,6},{8,11},{9,8},{10,9... | collective-permute-start | bytes 24584 | tf_op jit(solution)/shard_map/ppermute | solution.py:511
  24.5 22.4 %all-to-all-start = ((bf16[32,24,128]{2,1,0:T(8,128)(2,1)}), bf16[32,24,128]{2,1,0:T(8,128)(2,1)S(1)}, u32[]{:S(2)}, u32[]{:S(2)}) async-start(bf16[32,24,128]{2,1,0:T(8,128)(2,1)} %get-tuple-element.64), calls=%async_computation | async-start | bytes 393216 | tf_op jit(solution)/shard_map/all_to_all | solution.py:611
  37.4 23.5 %copy-start.6 = (f32[4,64]{1,0:T(4,128)S(1)}, f32[4,64]{1,0:T(4,128)}, u32[]{:S(2)}) copy-start(f32[4,64]{1,0:T(4,128)} %gain.3) | copy-start | bytes 3076
  37.4 22.2 %collective-permute-start.13 = (bf16[128,1024]{1,0:T(8,128)(2,1)S(1)}, bf16[128,1024]{1,0:T(8,128)(2,1)S(1)}, u32[]{:S(2)}, u32[]{:S(2)}) collective-permute-start(bf16[128,1024]{1,0:T(8,128)(2,1)S(1)} %get-tuple-element.66), channel_id=1, source_target_pairs={{0,1},{1,2},{2,3},{3,0},{4,5},{5,6},{6,7},{7,4},{8,9},{9,10},{10,1... | collective-permute-start | bytes 786440 | tf_op jit(solution)/shard_map/ppermute | solution.py:511
  38.0 21.8 %collective-permute-start.14 = (bf16[128,1024]{1,0:T(8,128)(2,1)S(1)}, bf16[128,1024]{1,0:T(8,128)(2,1)S(1)}, u32[]{:S(2)}, u32[]{:S(2)}) collective-permute-start(bf16[128,1024]{1,0:T(8,128)(2,1)S(1)} %get-tuple-element.66), channel_id=1, source_target_pairs={{0,2},{1,3},{2,0},{3,1},{4,6},{5,7},{6,4},{7,5},{8,10},{9,11},{10,... | collective-permute-start | bytes 786440 | tf_op jit(solution)/shard_map/ppermute | solution.py:511
  40.8 19.5 %collective-permute-start.15 = (bf16[128,1024]{1,0:T(8,128)(2,1)S(1)}, bf16[128,1024]{1,0:T(8,128)(2,1)S(1)}, u32[]{:S(2)}, u32[]{:S(2)}) collective-permute-start(bf16[128,1024]{1,0:T(8,128)(2,1)S(1)} %get-tuple-element.66), channel_id=1, source_target_pairs={{0,3},{1,0},{2,1},{3,2},{4,7},{5,4},{6,5},{7,6},{8,11},{9,8},{10,9... | collective-permute-start | bytes 786440 | tf_op jit(solution)/shard_map/ppermute | solution.py:511
  47.7 13.2 %all-to-all-start.1 = ((bf16[32,16,128]{2,1,0:T(8,128)(2,1)}), bf16[32,16,128]{2,1,0:T(8,128)(2,1)S(1)}, u32[]{:S(2)}, u32[]{:S(2)}) async-start(bf16[32,16,128]{2,1,0:T(8,128)(2,1)} %shard_map.123), calls=%async_computation.1 | async-start | bytes 262144 | tf_op jit(solution)/shard_map/all_to_all | solution.py:639
  51.8 19.6 %collective-permute-start.19 = (bf16[4,128,256]{2,1,0:T(8,128)(2,1)}, bf16[4,128,256]{2,1,0:T(8,128)(2,1)S(1)}, u32[]{:S(2)}, u32[]{:S(2)}) collective-permute-start(bf16[4,128,256]{2,1,0:T(8,128)(2,1)} %get-tuple-element.68), channel_id=1, source_target_pairs={{0,4},{4,0},{1,5},{5,1},{2,6},{6,2},{3,7},{7,3},{8,12},{12,8},{9,1... | collective-permute-start | bytes 786440 | tf_op jit(solution)/shard_map/ppermute | solution.py:616
  59.7 11.6 %copy-start.7 = (bf16[128,1024]{1,0:T(8,128)(2,1)}, bf16[128,1024]{1,0:T(8,128)(2,1)S(1)}, u32[]{:S(2)}) copy-start(bf16[128,1024]{1,0:T(8,128)(2,1)S(1)} %collective-permute-done.13.mine1) | copy-start | bytes 786436
  59.7 14.4 %collective-permute-start.16 = (bf16[128,1024]{1,0:T(8,128)(2,1)S(1)}, bf16[128,1024]{1,0:T(8,128)(2,1)S(1)}, u32[]{:S(2)}, u32[]{:S(2)}) collective-permute-start(bf16[128,1024]{1,0:T(8,128)(2,1)S(1)} %collective-permute-done.13.mine1), channel_id=1, source_target_pairs={{0,4},{4,0},{1,5},{5,1},{2,6},{6,2},{3,7},{7,3},{8,12},{12,8},{9,1... | collective-permute-start | bytes 786440 | tf_op jit(solution)/shard_map/ppermute | solution.py:615
  59.8 11.5 %copy-start.8 = (bf16[128,1024]{1,0:T(8,128)(2,1)}, bf16[128,1024]{1,0:T(8,128)(2,1)S(1)}, u32[]{:S(2)}) copy-start(bf16[128,1024]{1,0:T(8,128)(2,1)S(1)} %collective-permute-done.14.mine2) | copy-start | bytes 786436
  59.8 14.6 %collective-permute-start.17 = (bf16[128,1024]{1,0:T(8,128)(2,1)S(1)}, bf16[128,1024]{1,0:T(8,128)(2,1)S(1)}, u32[]{:S(2)}, u32[]{:S(2)}) collective-permute-start(bf16[128,1024]{1,0:T(8,128)(2,1)S(1)} %collective-permute-done.14.mine2), channel_id=1, source_target_pairs={{0,4},{4,0},{1,5},{5,1},{2,6},{6,2},{3,7},{7,3},{8,12},{12,8},{9,1... | collective-permute-start | bytes 786440 | tf_op jit(solution)/shard_map/ppermute | solution.py:615
  60.3 11.0 %copy-start.9 = (bf16[128,1024]{1,0:T(8,128)(2,1)}, bf16[128,1024]{1,0:T(8,128)(2,1)S(1)}, u32[]{:S(2)}) copy-start(bf16[128,1024]{1,0:T(8,128)(2,1)S(1)} %collective-permute-done.15.mine3) | copy-start | bytes 786436
  60.3 14.1 %collective-permute-start.18 = (bf16[128,1024]{1,0:T(8,128)(2,1)S(1)}, bf16[128,1024]{1,0:T(8,128)(2,1)S(1)}, u32[]{:S(2)}, u32[]{:S(2)}) collective-permute-start(bf16[128,1024]{1,0:T(8,128)(2,1)S(1)} %collective-permute-done.15.mine3), channel_id=1, source_target_pairs={{0,4},{4,0},{1,5},{5,1},{2,6},{6,2},{3,7},{7,3},{8,12},{12,8},{9,1... | collective-permute-start | bytes 786440 | tf_op jit(solution)/shard_map/ppermute | solution.py:615
  63.4 7.9 %collective-permute-start.9 = (bf16[128,256]{1,0:T(8,128)(2,1)S(1)}, bf16[128,256]{1,0:T(8,128)(2,1)S(1)}, u32[]{:S(2)}, u32[]{:S(2)}) collective-permute-start(bf16[128,256]{1,0:T(8,128)(2,1)S(1)} %shard_map.125), channel_id=1, source_target_pairs={{0,4},{4,0},{1,5},{5,1},{2,6},{6,2},{3,7},{7,3},{8,12},{12,8},{9,1... | collective-permute-start | bytes 196616 | tf_op jit(solution)/shard_map/ppermute | solution.py:667
  71.3 6.5 %collective-permute-start.10 = (bf16[256,256]{1,0:T(8,128)(2,1)S(1)}, bf16[256,256]{1,0:T(8,128)(2,1)S(1)}, u32[]{:S(2)}, u32[]{:S(2)}) collective-permute-start(bf16[256,256]{1,0:T(8,128)(2,1)S(1)} %pad_maximum_fusion.1.part0), channel_id=1, source_target_pairs={{0,1},{1,2},{2,3},{3,0},{4,5},{5,6},{6,7},{7,4},{8,9},{9,10},{10,1... | collective-permute-start | bytes 393224 | tf_op jit(solution)/shard_map/ppermute | solution.py:511
  71.4 3.0 %copy-start.10 = (bf16[4,128,256]{2,1,0:T(8,128)(2,1)}, bf16[4,128,256]{2,1,0:T(8,128)(2,1)S(1)}, u32[]{:S(2)}) copy-start(bf16[4,128,256]{2,1,0:T(8,128)(2,1)S(1)} %collective-permute-done.19.passed) | copy-start | bytes 786436
  71.4 9.0 %collective-permute-start.11 = (bf16[256,256]{1,0:T(8,128)(2,1)S(1)}, bf16[256,256]{1,0:T(8,128)(2,1)S(1)}, u32[]{:S(2)}, u32[]{:S(2)}) collective-permute-start(bf16[256,256]{1,0:T(8,128)(2,1)S(1)} %pad_maximum_fusion.1.part0), channel_id=1, source_target_pairs={{0,2},{1,3},{2,0},{3,1},{4,6},{5,7},{6,4},{7,5},{8,10},{9,11},{10,... | collective-permute-start | bytes 393224 | tf_op jit(solution)/shard_map/ppermute | solution.py:511
  74.0 0.7 copy-start.11
  74.0 6.7 %collective-permute-start.12 = (bf16[256,256]{1,0:T(8,128)(2,1)S(1)}, bf16[256,256]{1,0:T(8,128)(2,1)S(1)}, u32[]{:S(2)}, u32[]{:S(2)}) collective-permute-start(bf16[256,256]{1,0:T(8,128)(2,1)S(1)} %pad_maximum_fusion.1.part0), channel_id=1, source_target_pairs={{0,3},{1,0},{2,1},{3,2},{4,7},{5,4},{6,5},{7,6},{8,11},{9,8},{10,9... | collective-permute-start | bytes 393224 | tf_op jit(solution)/shard_map/ppermute | solution.py:511
  74.4 0.7 copy-start.12
  74.4 0.8 copy-start.13
  75.2 5.6 %copy-start.1 = (bf16[1024,1024]{1,0:T(8,128)(2,1)S(1)}, bf16[1024,1024]{1,0:T(8,128)(2,1)}, u32[]{:S(2)}) copy-start(bf16[1024,1024]{1,0:T(8,128)(2,1)} %up.1) | copy-start | bytes 6291460
  75.2 5.6 %copy-start.4 = (f32[1024]{0:T(1024)S(1)}, f32[1024]{0:T(1024)}, u32[]{:S(2)}) copy-start(f32[1024]{0:T(1024)} %param.21) | copy-start | bytes 12292
  83.2 5.9 %collective-permute-start.20 = (bf16[256,256]{1,0:T(8,128)(2,1)S(1)}, bf16[256,256]{1,0:T(8,128)(2,1)S(1)}, u32[]{:S(2)}, u32[]{:S(2)}) collective-permute-start(bf16[256,256]{1,0:T(8,128)(2,1)S(1)} %get-tuple-element.74), channel_id=1, source_target_pairs={{0,1},{1,2},{2,3},{3,0},{4,5},{5,6},{6,7},{7,4},{8,9},{9,10},{10,1... | collective-permute-start | bytes 393224 | tf_op jit(solution)/shard_map/ppermute | solution.py:511
  84.2 9.1 %collective-permute-start.21 = (bf16[256,256]{1,0:T(8,128)(2,1)S(1)}, bf16[256,256]{1,0:T(8,128)(2,1)S(1)}, u32[]{:S(2)}, u32[]{:S(2)}) collective-permute-start(bf16[256,256]{1,0:T(8,128)(2,1)S(1)} %get-tuple-element.75), channel_id=1, source_target_pairs={{0,2},{1,3},{2,0},{3,1},{4,6},{5,7},{6,4},{7,5},{8,10},{9,11},{10,... | collective-permute-start | bytes 393224 | tf_op jit(solution)/shard_map/ppermute | solution.py:511
  87.5 5.9 %collective-permute-start.22 = (bf16[256,256]{1,0:T(8,128)(2,1)S(1)}, bf16[256,256]{1,0:T(8,128)(2,1)S(1)}, u32[]{:S(2)}, u32[]{:S(2)}) collective-permute-start(bf16[256,256]{1,0:T(8,128)(2,1)S(1)} %get-tuple-element.76), channel_id=1, source_target_pairs={{0,3},{1,0},{2,1},{3,2},{4,7},{5,4},{6,5},{7,6},{8,11},{9,8},{10,9... | collective-permute-start | bytes 393224 | tf_op jit(solution)/shard_map/ppermute | solution.py:511

commit v7 on v5

--- a/solution.py
+++ b/solution.py
@@ -1,5 +1,3 @@
-import functools
-
 import jax
 import jax.numpy as jnp
 from jax import lax
@@ -363,28 +361,33 @@
     return jnp.concatenate(halves, axis=1)
 
 
-def attention_kernel(
-    own_half,
-    queries_in, kv_in, shrink_in, start_in, reach_in, scores_in, growth_in, arrived, gain,
-    out,
-    queries, values, shrink, start, reach, scores, growth, weighted, mixing, result, entering,
-    semaphores,
+def attend_other_kernel(
+    reach_in, queries_in, growth_in, scores_in, shrink_in, start_in, kv_in, arrived, gain,
+    out, entering,
+    next_reach, next_queries, next_growth, next_scores, next_shrink, next_start, next_values,
+    reach, queries, growth, scores, shrink, start, values, weighted, mixing, result, semaphores,
 ):
     core = lax.axis_index("core")
-    half_index = core if own_half else 1 - core
-    rows = pl.ds(pl.multiple_of(half_index * 128, 128), 128)
-    spans = pl.ds(half_index * 2, 2)
-    coming = begin(
-        [
-            (reach_in.at[:, spans], reach),
-            (queries_in.at[:, rows, :], queries),
-            (growth_in.at[:, rows, :], growth),
-            (scores_in.at[:, rows, :], scores),
-            (shrink_in.at[:, rows, :], shrink),
-            (start_in.at[:, spans, 1], start),
-            (kv_in.at[:, 1, rows, :], values),
-        ],
-        semaphores,
+
+    def copies(half_index, targets, first):
+        rows = pl.ds(pl.multiple_of(half_index * 128, 128), 128)
+        spans = pl.ds(half_index * 2, 2)
+        sources = (
+            reach_in.at[:, spans],
+            queries_in.at[:, rows, :],
+            growth_in.at[:, rows, :],
+            scores_in.at[:, rows, :],
+            shrink_in.at[:, rows, :],
+            start_in.at[:, spans, 1],
+            kv_in.at[:, 1, rows, :],
+        )
+        return begin(list(zip(sources, targets)), semaphores.at[pl.ds(first, 7)])
+
+    coming = copies(1 - core, (reach, queries, growth, scores, shrink, start, values), 0)
+    later = copies(
+        core,
+        (next_reach, next_queries, next_growth, next_scores, next_shrink, next_start, next_values),
+        7,
     )
     for m in range(32):
         which, half, block = m // 16, (m // 8) % 2, m % 8
@@ -393,22 +396,32 @@
             entering[direction, which, block * 8 : block * 8 + 8, half * 128 : half * 128 + 128] = (
                 piece[direction * 8 : direction * 8 + 8]
             )
+    finish(coming)
+    attend(
+        reach, queries, growth, scores, shrink, start, values, entering, gain,
+        out, scores, weighted, mixing, result,
+    )
+    finish(later)
+
+
+def attend(
+    reach, queries, growth, scores, shrink, start, values, entering, gain,
+    out, totals, weighted, mixing, result,
+):
     own = own_head()
     gains = in_lanes(gain[...])
     units = [(direction, n) for direction in range(2) for n in range(2)]
-    finish(coming[:4])
     for direction, n in units:
         span = slice(n * SPAN, (n + 1) * SPAN)
         key_state = expand((reach[direction, n] * entering[direction, 0]).astype(BF16), own)
-        scores[direction, span, :] = scores[direction, span, :] + growth[
+        totals[direction, span, :] = scores[direction, span, :] + growth[
             direction, span, :
         ] * nt(queries[direction, span, :], key_state)
     for direction in range(2):
-        total = scores[direction]
+        total = totals[direction]
         powers = jnp.exp(total - head_max(total))
         attend = powers / nn(powers.astype(BF16), own)
         weighted[direction] = (attend * growth[direction]).astype(BF16)
-    finish(coming[4:])
     for direction, n in units:
         span = slice(n * SPAN, (n + 1) * SPAN)
         lessen = expand(shrink[direction, span, :], own)
@@ -631,31 +644,33 @@
     arrived = lax.all_to_all(prefixes, CHIPS, split_axis=0, concat_axis=0, tiled=True)
     half = (2, 128, LANES)
     reached = (2, 2, SPAN, LANES)
-    attention = []
-    for own_half in (False, True):
-        attend = kernel(
-            functools.partial(attention_kernel, own_half),
-            "hhhhhhhvv",
-            [((128, LANES), BF16, "v")],
-            [
-                (half, BF16),
-                (half, BF16),
-                (half, BF16),
-                (reached, BF16),
-                (reached, F32),
-                (half, F32),
-                (half, F32),
-                (half, BF16),
-                (half, BF16),
-                (half, F32),
-                ((2, 2, SPAN, LANES), F32),
-            ],
-            copies=7,
-            flops=10**9,
-        )
-        attention += attend(
-            queries, kv, shrink, start, reach, scores, growth, arrived, head_norm_gain
-        )
+    buffers = [
+        (reached, F32),
+        (half, BF16),
+        (half, F32),
+        (half, F32),
+        (half, BF16),
+        (reached, BF16),
+        (half, BF16),
+    ]
+    work = [(half, BF16), (half, BF16), (half, F32)]
+    attend_other = kernel(
+        attend_other_kernel,
+        "hhhhhhhvv",
+        [((128, LANES), BF16, "v"), ((2, 2, SPAN, LANES), F32, "v")]
+        + [(*buffer, "v") for buffer in buffers],
+        buffers + work,
+        copies=14,
+        flops=10**9,
+    )
+    attend_own = kernel(
+        attend, "v" * 9, [((128, LANES), BF16, "v")], [(half, F32)] + work, flops=10**9
+    )
+    other_rows, entering, *later = attend_other(
+        reach, queries, growth, scores, shrink, start, kv, arrived, head_norm_gain
+    )
+    (own_rows,) = attend_own(*later, entering, head_norm_gain)
+    attention = [other_rows, own_rows]
     swapped = lax.ppermute(attention[0], "core", swap_pairs)
     attention = jnp.concatenate([attention[1], swapped], axis=0)
     attention, down_weight = lax.optimization_barrier((attention, down_projection_weight))

time: 91.7 us -> 90 us (0.981)
  Pallas kernels: 21.9 us -> 20.4 us
    pallas_call x11, Pallas kernels: 21.9 us -> 20.4 us  [placed(): call(*[pltpu.with_memory_space_constraint(array, pltpu.HBM) if place == '...]
  transfers between devices with their start and end apart: 21 -> 21, of which waited for: 8 -> 8; matrix products, arithmetic and copies ran while one was open for 0% -> 0% of each run, Pallas kernels for 14% -> 13%
where the time goes in v7:
time: 90 us; the launch traced here: 89.7 us
  starting transfers between devices  46.9 us (52%)
  waiting for transfers between devices  21.2 us (24%)
  Pallas kernels  20.4 us (23%)
    pallas_call x11, Pallas kernels, placed(): call(*[pltpu.with_memory_space_constraint(array, pltpu.HBM) if place == '...  20.4 us
    ppermute x12, starting transfers between devices, shifted(): lax.ppermute(value, 'head', [(j, (j + k) % count) for j in range(count)])  17.9 us
    all_to_all x1, starting transfers between devices, local(): lax.all_to_all(pieces, CHIPS, split_axis=0, concat_axis=0, tiled=True)  11.9 us
    ppermute x12, waiting for transfers between devices, shifted(): lax.ppermute(value, 'head', [(j, (j + k) % count) for j in range(count)])  11.3 us
    all_to_all x1, waiting for transfers between devices, local(): lax.all_to_all(pieces, CHIPS, split_axis=0, concat_axis=0, tiled=True)  5.18 us
    ppermute x1, starting transfers between devices, local(): edges = lax.ppermute(edges, SEQ, ahead + behind)  4.92 us
    all_to_all x1, starting transfers between devices, local(): lax.all_to_all(prefixes, CHIPS, split_axis=0, concat_axis=0, tiled=True)  4.6 us
    ppermute x1, starting transfers between devices, local(): swapped = lax.ppermute(attention[0], 'core', swap_pairs)  3.94 us
  transfers between devices with their start and end apart: 21, of which 8 were waited for; matrix products, arithmetic and copies ran while one was open for 0% of the time, Pallas kernels for 13%

profile of v7, /device:TPU:1, one launch (start us, length us, event | category | flops | bytes accessed | tf_op | source)
XLA Modules:
  0.0 89.7 jit_solution(12541791947140753962)
XLA Ops:
  0.0 0.9 %shard_map.118 = (bf16[2,8,256]{2,1,0:T(8,128)(2,1)S(1)}, bf16[136,256]{1,0:T(8,128)(2,1)S(1)}, bf16[128,256]{1,0:T(8,128)(2,1)S(1)}) custom-call(bf16[2,128,256]{2,1,0:T(8,128)(2,1)} %tokens_in.1, f32[2,128]{1,0:T(2,128)} %extra.1), custom_call_target="tpu_custom_call" | custom-call | bytes 1048576 | tf_op jit(solution)/shard_map/pallas_call | solution.py:509
  0.9 4.9 %collective-permute-start = (bf16[2,8,256]{2,1,0:T(8,128)(2,1)S(1)}, bf16[2,8,256]{2,1,0:T(8,128)(2,1)S(1)}, u32[]{:S(2)}, u32[]{:S(2)}) collective-permute-start(bf16[2,8,256]{2,1,0:T(8,128)(2,1)S(1)} %get-tuple-element.52), channel_id=1, source_target_pairs={{4,8},{12,16},{20,24},{28,32},{36,40},{44,48},{52,56},{60,64},{68,... | collective-permute-start | bytes 24584 | tf_op jit(solution)/shard_map/ppermute | solution.py:549
  5.9 1.3 %collective-permute-done.edges = bf16[2,8,256]{2,1,0:T(8,128)(2,1)S(1)} collective-permute-done((bf16[2,8,256]{2,1,0:T(8,128)(2,1)S(1)}, bf16[2,8,256]{2,1,0:T(8,128)(2,1)S(1)}, u32[]{:S(2)}, u32[]{:S(2)}) %collective-permute-start) | collective-permute-done | bytes 8224 | tf_op jit(solution)/shard_map/ppermute | solution.py:549
  7.2 0.1 collective-permute-start.1
  7.3 1.3 %collective-permute-done.1 = bf16[144,256]{1,0:T(8,128)(2,1)S(1)} collective-permute-done((bf16[144,256]{1,0:T(8,128)(2,1)S(1)}, bf16[144,256]{1,0:T(8,128)(2,1)S(1)}, u32[]{:S(2)}, u32[]{:S(2)}) %collective-permute-start.1) | collective-permute-done | bytes 73760 | tf_op jit(solution)/shard_map/ppermute | solution.py:553
  8.6 1.4 %collective-permute-start.2 = (bf16[272,256]{1,0:T(8,128)(2,1)S(1)}, bf16[272,256]{1,0:T(8,128)(2,1)S(1)}, u32[]{:S(2)}, u32[]{:S(2)}) collective-permute-start(bf16[272,256]{1,0:T(8,128)(2,1)S(1)} %pad_maximum_fusion.part0), channel_id=1, source_target_pairs={{0,1},{1,2},{2,3},{3,0},{4,5},{5,6},{6,7},{7,4},{8,9},{9,10},{10,1... | collective-permute-start | bytes 417800 | tf_op jit(solution)/shard_map/ppermute | solution.py:521
  10.0 2.6 %collective-permute-start.3 = (bf16[272,256]{1,0:T(8,128)(2,1)S(1)}, bf16[272,256]{1,0:T(8,128)(2,1)S(1)}, u32[]{:S(2)}, u32[]{:S(2)}) collective-permute-start(bf16[272,256]{1,0:T(8,128)(2,1)S(1)} %pad_maximum_fusion.part0), channel_id=1, source_target_pairs={{0,2},{1,3},{2,0},{3,1},{4,6},{5,7},{6,4},{7,5},{8,10},{9,11},{10,... | collective-permute-start | bytes 417800 | tf_op jit(solution)/shard_map/ppermute | solution.py:521
  12.6 1.1 %collective-permute-start.4 = (bf16[272,256]{1,0:T(8,128)(2,1)S(1)}, bf16[272,256]{1,0:T(8,128)(2,1)S(1)}, u32[]{:S(2)}, u32[]{:S(2)}) collective-permute-start(bf16[272,256]{1,0:T(8,128)(2,1)S(1)} %pad_maximum_fusion.part0), channel_id=1, source_target_pairs={{0,3},{1,0},{2,1},{3,2},{4,7},{5,4},{6,5},{7,6},{8,11},{9,8},{10,9... | collective-permute-start | bytes 417800 | tf_op jit(solution)/shard_map/ppermute | solution.py:521
  13.7 1.6 %shard_map.120 = (bf16[3,1024,256]{2,1,0:T(8,128)(2,1)S(1)}, bf16[1024,256]{1,0:T(8,128)(2,1)S(1)}, bf16[128,1024]{1,0:T(8,128)(2,1)S(1)}) custom-call(bf16[3,1024,256]{2,1,0:T(8,128)(2,1)} %bitcast.8, bf16[1024,256]{1,0:T(8,128)(2,1)} %gate_weight, bf16[256,1024]{1,0:T(8,128)(2,1)} %weight0.1), custom_call_target="tpu_custom_call" | custom-call | flops 1000000000 | bytes 1048576 | tf_op jit(solution)/shard_map/pallas_call | solution.py:509
  15.3 0.0 collective-permute-done.2.part1
  15.3 3.9 %collective-permute-done.3.part2 = bf16[272,256]{1,0:T(8,128)(2,1)S(1)} collective-permute-done((bf16[272,256]{1,0:T(8,128)(2,1)S(1)}, bf16[272,256]{1,0:T(8,128)(2,1)S(1)}, u32[]{:S(2)}, u32[]{:S(2)}) %collective-permute-start.3) | collective-permute-done | bytes 139296 | tf_op jit(solution)/shard_map/ppermute | solution.py:521
  19.2 0.0 collective-permute-done.4.part3
  19.2 0.0 copy-done
  19.2 0.0 copy-done.2
  19.2 0.0 copy-done.3
  19.2 0.0 copy-done.5
  19.2 4.6 %shard_map.121 = (bf16[32,24,128]{2,1,0:T(8,128)(2,1)}, bf16[272,256]{1,0:T(8,128)(2,1)}, bf16[2,2,256,256]{3,2,1,0:T(8,128)(2,1)}, f32[2,256,256]{2,1,0:T(8,128...) custom-call(bf16[272,256]{1,0:T(8,128)(2,1)S(1)} %pad_maximum_fusion, ...), custom_call_target="tpu_custom_call" | custom-call | flops 1000000000 | bytes 1048576 | tf_op jit(solution)/shard_map/pallas_call | solution.py:509
  23.9 11.9 %all-to-all-start = ((bf16[32,24,128]{2,1,0:T(8,128)(2,1)}), bf16[32,24,128]{2,1,0:T(8,128)(2,1)S(1)}, u32[]{:S(2)}, u32[]{:S(2)}) async-start(bf16[32,24,128]{2,1,0:T(8,128)(2,1)} %get-tuple-element.73), calls=%async_computation | async-start | bytes 393216 | tf_op jit(solution)/shard_map/all_to_all | solution.py:616
  35.8 0.0 copy-start.6
  35.8 1.1 %collective-permute-start.9 = (bf16[128,1024]{1,0:T(8,128)(2,1)S(1)}, bf16[128,1024]{1,0:T(8,128)(2,1)S(1)}, u32[]{:S(2)}, u32[]{:S(2)}) collective-permute-start(bf16[128,1024]{1,0:T(8,128)(2,1)S(1)} %get-tuple-element.84), channel_id=1, source_target_pairs={{0,1},{1,2},{2,3},{3,0},{4,5},{5,6},{6,7},{7,4},{8,9},{9,10},{10,1... | collective-permute-start | bytes 786440 | tf_op jit(solution)/shard_map/ppermute | solution.py:521
  36.8 2.3 %collective-permute-start.10 = (bf16[128,1024]{1,0:T(8,128)(2,1)S(1)}, bf16[128,1024]{1,0:T(8,128)(2,1)S(1)}, u32[]{:S(2)}, u32[]{:S(2)}) collective-permute-start(bf16[128,1024]{1,0:T(8,128)(2,1)S(1)} %get-tuple-element.84), channel_id=1, source_target_pairs={{0,2},{1,3},{2,0},{3,1},{4,6},{5,7},{6,4},{7,5},{8,10},{9,11},{10,... | collective-permute-start | bytes 786440 | tf_op jit(solution)/shard_map/ppermute | solution.py:521
  39.1 0.8 collective-permute-start.11
  40.0 5.2 %all-to-all-done.pieces = bf16[32,24,128]{2,1,0:T(8,128)(2,1)S(1)} async-done(((bf16[32,24,128]{2,1,0:T(8,128)(2,1)}), bf16[32,24,128]{2,1,0:T(8,128)(2,1)S(1)}, u32[]{:S(2)}, u32[]{:S(2)}) %all-to-all-start) | async-done | bytes 196640 | tf_op jit(solution)/shard_map/all_to_all | solution.py:616
  45.2 0.8 shard_map.123
  46.0 4.6 %all-to-all-start.1 = ((bf16[32,16,128]{2,1,0:T(8,128)(2,1)}), bf16[32,16,128]{2,1,0:T(8,128)(2,1)S(1)}, u32[]{:S(2)}, u32[]{:S(2)}) async-start(bf16[32,16,128]{2,1,0:T(8,128)(2,1)} %shard_map.123), calls=%async_computation.1 | async-start | bytes 262144 | tf_op jit(solution)/shard_map/all_to_all | solution.py:644
  50.6 2.7 %collective-permute-start.15 = (bf16[4,128,256]{2,1,0:T(8,128)(2,1)}, bf16[4,128,256]{2,1,0:T(8,128)(2,1)S(1)}, u32[]{:S(2)}, u32[]{:S(2)}) collective-permute-start(bf16[4,128,256]{2,1,0:T(8,128)(2,1)} %get-tuple-element.86), channel_id=1, source_target_pairs={{0,4},{4,0},{1,5},{5,1},{2,6},{6,2},{3,7},{7,3},{8,12},{12,8},{9,1... | collective-permute-start | bytes 786440 | tf_op jit(solution)/shard_map/ppermute | solution.py:621
  53.2 3.4 %shard_map.122 = (bf16[2,256,256]{2,1,0:T(8,128)(2,1)}, f32[2,256,256]{2,1,0:T(8,128)}, f32[2,256,256]{2,1,0:T(8,128)}) custom-call(bf16[272,256]{1,0:T(8,128)(2,1)} %get-tuple-element.62.query_in, bf16[2,2,256,256]{3,2,1,0:T(8,128)(2,1)} %get-tuple-element.63.kv_in, f32[2,256,256]{2,1,0:T(8,128)} %get-tuple-element.64.cum_in, ...), custom_call_target="tpu_custom_call" | custom-call | flops 1000000000 | bytes 1048576 | tf_op jit(solution)/shard_map/pallas_call | solution.py:509
  56.6 0.0 collective-permute-done.9.mine1
  56.6 0.0 copy-start.7
  56.6 0.1 collective-permute-start.12
  56.7 0.0 collective-permute-done.10.mine2
  56.8 0.5 collective-permute-start.13
  57.2 0.0 collective-permute-done.11.mine3
  57.3 0.3 collective-permute-start.14
  57.5 2.2 %all-to-all-done.1.arrived = bf16[32,16,128]{2,1,0:T(8,128)(2,1)S(1)} async-done(((bf16[32,16,128]{2,1,0:T(8,128)(2,1)}), bf16[32,16,128]{2,1,0:T(8,128)(2,1)S(1)}, u32[]{:S(2)}, u32[]{:S(2)}) %all-to-all-start.1) | async-done | bytes 131104 | tf_op jit(solution)/shard_map/all_to_all | solution.py:644
  59.7 2.4 %shard_map.124 = (bf16[128,256]{1,0:T(8,128)(2,1)S(1)}, f32[2,2,64,256]{3,2,1,0:T(8,128)S(1)}, f32[2,2,64,256]{3,2,1,0:T(8,128)S(1)}, bf16[2,128,256]{2,1,0:T(8,...) custom-call(f32[2,4,64,256]{3,2,1,0:T(8,128)} %get-tuple-element.61., ...), custom_call_target="tpu_custom_call" | custom-call | flops 1000000000 | bytes 1048576 | tf_op jit(solution)/shard_map/pallas_call | solution.py:509
  62.1 3.9 %collective-permute-start.5 = (bf16[128,256]{1,0:T(8,128)(2,1)S(1)}, bf16[128,256]{1,0:T(8,128)(2,1)S(1)}, u32[]{:S(2)}, u32[]{:S(2)}) collective-permute-start(bf16[128,256]{1,0:T(8,128)(2,1)S(1)} %get-tuple-element.82), channel_id=1, source_target_pairs={{0,4},{4,0},{1,5},{5,1},{2,6},{6,2},{3,7},{7,3},{8,12},{12,8},{9,1... | collective-permute-start | bytes 196616 | tf_op jit(solution)/shard_map/ppermute | solution.py:674
  66.1 1.0 %shard_map.125 = bf16[128,256]{1,0:T(8,128)(2,1)S(1)} custom-call(f32[2,2,64,256]{3,2,1,0:T(8,128)S(1)} %get-tuple-element.74.reach, bf16[2,128,256]{2,1,0:T(8,128)(2,1)S(1)} %get-tuple-element.75.queries, f32[2,128,256]{2,1,0:T(8,128)S(1)} %get-tuple-element.76.growth, f32[2,128,256]{2,1,0:T(8,128)S(1)} %get-tuple-element.77.scores, ...), custom_call_target="tpu_custom_call" | custom-call | flops 1000000000 | bytes 1048576 | tf_op jit(solution)/shard_map/pallas_call | solution.py:509
  67.0 0.0 copy-done.7
  67.0 0.0 copy-done.8
  67.0 0.0 copy-done.9
  67.1 0.0 collective-permute-done.5
  67.1 0.9 collective-permute-start.6
  67.9 0.0 collective-permute-done.15.passed
  67.9 2.3 %collective-permute-start.7 = (bf16[256,256]{1,0:T(8,128)(2,1)S(1)}, bf16[256,256]{1,0:T(8,128)(2,1)S(1)}, u32[]{:S(2)}, u32[]{:S(2)}) collective-permute-start(bf16[256,256]{1,0:T(8,128)(2,1)S(1)} %pad_maximum_fusion.1.part0), channel_id=1, source_target_pairs={{0,2},{1,3},{2,0},{3,1},{4,6},{5,7},{6,4},{7,5},{8,10},{9,11},{10,... | collective-permute-start | bytes 393224 | tf_op jit(solution)/shard_map/ppermute | solution.py:521
  70.2 0.0 collective-permute-done.12.theirs1
  70.2 0.9 collective-permute-start.8
  71.1 0.0 collective-permute-done.13.theirs2
  71.1 0.0 collective-permute-done.14.theirs3
  71.2 0.7 copy-done.12
  71.8 0.1 copy-done.13
  71.9 2.6 %shard_map.126 = (bf16[4,256,1024]{2,1,0:T(8,128)(2,1)S(1)}, bf16[4,256,256]{2,1,0:T(8,128)(2,1)S(1)}, bf16[1024,1024]{1,0:T(8,128)(2,1)S(1)}) custom-call(bf16[256,1024]{1,0:T(8,128)(2,1)} %weight0.1, bf16[128,1024]{1,0:T(8,128)(2,1)} %copy-done.7, bf16[128,1024]{1,0:T(8,128)(2,1)} %copy-done.8, bf16[128,1024]{1,0:T(8,128)(2,1)} %copy-done.9, ...), custom_call_target="tpu_custom_call" | custom-call | flops 1000000000 | bytes 1048576 | tf_op jit(solution)/shard_map/pallas_call | solution.py:509
  74.5 0.0 collective-permute-done.6.part1
  74.6 1.8 %collective-permute-done.7.part2 = bf16[256,256]{1,0:T(8,128)(2,1)S(1)} collective-permute-done((bf16[256,256]{1,0:T(8,128)(2,1)S(1)}, bf16[256,256]{1,0:T(8,128)(2,1)S(1)}, u32[]{:S(2)}, u32[]{:S(2)}) %collective-permute-start.7) | collective-permute-done | bytes 131104 | tf_op jit(solution)/shard_map/ppermute | solution.py:521
  76.4 0.0 collective-permute-done.8.part3
  76.4 0.0 copy-done.4
  76.4 2.4 %shard_map.127 = (f32[256,256]{1,0:T(8,128)S(1)}, bf16[256,256]{1,0:T(8,128)(2,1)S(1)}, bf16[256,256]{1,0:T(8,128)(2,1)S(1)}, bf16[256,256]{1,0:T(8,128)(2,1)S(1)}) custom-call(bf16[256,256]{1,0:T(8,128)(2,1)S(1)} %pad_maximum_fusion.1.part0, bf16[256,256]{1,0:T(8,128)(2,1)S(1)} %collective-permute-done.6.part1, ...), custom_call_target="tpu_custom_call" | custom-call | flops 2000000000 | bytes 1048576 | tf_op jit(solution)/shard_map/pallas_call | solution.py:509
  78.8 2.1 %collective-permute-start.16 = (bf16[256,256]{1,0:T(8,128)(2,1)S(1)}, bf16[256,256]{1,0:T(8,128)(2,1)S(1)}, u32[]{:S(2)}, u32[]{:S(2)}) collective-permute-start(bf16[256,256]{1,0:T(8,128)(2,1)S(1)} %get-tuple-element.92), channel_id=1, source_target_pairs={{0,1},{1,2},{2,3},{3,0},{4,5},{5,6},{6,7},{7,4},{8,9},{9,10},{10,1... | collective-permute-start | bytes 393224 | tf_op jit(solution)/shard_map/ppermute | solution.py:521
  80.9 2.2 %collective-permute-start.17 = (bf16[256,256]{1,0:T(8,128)(2,1)S(1)}, bf16[256,256]{1,0:T(8,128)(2,1)S(1)}, u32[]{:S(2)}, u32[]{:S(2)}) collective-permute-start(bf16[256,256]{1,0:T(8,128)(2,1)S(1)} %get-tuple-element.93), channel_id=1, source_target_pairs={{0,2},{1,3},{2,0},{3,1},{4,6},{5,7},{6,4},{7,5},{8,10},{9,11},{10,... | collective-permute-start | bytes 393224 | tf_op jit(solution)/shard_map/ppermute | solution.py:521
  83.1 0.3 collective-permute-start.18
  83.4 1.2 %collective-permute-done.16.part1 = bf16[256,256]{1,0:T(8,128)(2,1)S(1)} collective-permute-done((bf16[256,256]{1,0:T(8,128)(2,1)S(1)}, bf16[256,256]{1,0:T(8,128)(2,1)S(1)}, u32[]{:S(2)}, u32[]{:S(2)}) %collective-permute-start.16) | collective-permute-done | bytes 131104 | tf_op jit(solution)/shard_map/ppermute | solution.py:521
  84.7 4.3 %collective-permute-done.17.part2 = bf16[256,256]{1,0:T(8,128)(2,1)S(1)} collective-permute-done((bf16[256,256]{1,0:T(8,128)(2,1)S(1)}, bf16[256,256]{1,0:T(8,128)(2,1)S(1)}, u32[]{:S(2)}, u32[]{:S(2)}) %collective-permute-start.17) | collective-permute-done | bytes 131104 | tf_op jit(solution)/shard_map/ppermute | solution.py:521
  88.9 0.0 collective-permute-done.18.part3
  88.9 0.7 shard_map.128
  (21 shorter events, 0.1 us)
Async XLA Ops:
  0.9 6.3 %collective-permute-start = (bf16[2,8,256]{2,1,0:T(8,128)(2,1)S(1)}, bf16[2,8,256]{2,1,0:T(8,128)(2,1)S(1)}, u32[]{:S(2)}, u32[]{:S(2)}) collective-permute-start(bf16[2,8,256]{2,1,0:T(8,128)(2,1)S(1)} %get-tuple-element.52), channel_id=1, source_target_pairs={{4,8},{12,16},{20,24},{28,32},{36,40},{44,48},{52,56},{60,64},{68,... | collective-permute-start | bytes 24584 | tf_op jit(solution)/shard_map/ppermute | solution.py:549
  7.2 12.0 %copy-start = (f32[2,128]{1,0:T(2,128)S(1)}, f32[2,128]{1,0:T(2,128)}, u32[]{:S(2)}) copy-start(f32[2,128]{1,0:T(2,128)} %extra.1) | copy-start | bytes 3076
  7.2 12.0 %copy-start.2 = (f32[2,4,3,256]{3,1,2,0:T(4,128)S(1)}, f32[2,4,3,256]{3,1,2,0:T(4,128)}, u32[]{:S(2)}) copy-start(f32[2,4,3,256]{3,1,2,0:T(4,128)} %param.16) | copy-start | bytes 73732
  7.2 12.0 %copy-start.3 = (f32[1024]{0:T(1024)S(1)}, f32[1024]{0:T(1024)}, u32[]{:S(2)}) copy-start(f32[1024]{0:T(1024)} %param.13) | copy-start | bytes 12292
  7.2 12.0 %copy-start.5 = (f32[4,64]{1,0:T(4,128)S(1)}, f32[4,64]{1,0:T(4,128)}, u32[]{:S(2)}) copy-start(f32[4,64]{1,0:T(4,128)} %rate.1) | copy-start | bytes 3076
  7.2 1.4 %collective-permute-start.1 = (bf16[144,256]{1,0:T(8,128)(2,1)S(1)}, bf16[144,256]{1,0:T(8,128)(2,1)S(1)}, u32[]{:S(2)}, u32[]{:S(2)}) collective-permute-start(bf16[144,256]{1,0:T(8,128)(2,1)S(1)} %get-tuple-element.53), channel_id=1, source_target_pairs={{0,4},{4,0},{1,5},{5,1},{2,6},{6,2},{3,7},{7,3},{8,12},{12,8},{9,1... | collective-permute-start | bytes 221192 | tf_op jit(solution)/shard_map/ppermute | solution.py:553
  8.6 6.7 %collective-permute-start.2 = (bf16[272,256]{1,0:T(8,128)(2,1)S(1)}, bf16[272,256]{1,0:T(8,128)(2,1)S(1)}, u32[]{:S(2)}, u32[]{:S(2)}) collective-permute-start(bf16[272,256]{1,0:T(8,128)(2,1)S(1)} %pad_maximum_fusion.part0), channel_id=1, source_target_pairs={{0,1},{1,2},{2,3},{3,0},{4,5},{5,6},{6,7},{7,4},{8,9},{9,10},{10,1... | collective-permute-start | bytes 417800 | tf_op jit(solution)/shard_map/ppermute | solution.py:521
  10.0 9.2 %collective-permute-start.3 = (bf16[272,256]{1,0:T(8,128)(2,1)S(1)}, bf16[272,256]{1,0:T(8,128)(2,1)S(1)}, u32[]{:S(2)}, u32[]{:S(2)}) collective-permute-start(bf16[272,256]{1,0:T(8,128)(2,1)S(1)} %pad_maximum_fusion.part0), channel_id=1, source_target_pairs={{0,2},{1,3},{2,0},{3,1},{4,6},{5,7},{6,4},{7,5},{8,10},{9,11},{10,... | collective-permute-start | bytes 417800 | tf_op jit(solution)/shard_map/ppermute | solution.py:521
  12.6 6.6 %collective-permute-start.4 = (bf16[272,256]{1,0:T(8,128)(2,1)S(1)}, bf16[272,256]{1,0:T(8,128)(2,1)S(1)}, u32[]{:S(2)}, u32[]{:S(2)}) collective-permute-start(bf16[272,256]{1,0:T(8,128)(2,1)S(1)} %pad_maximum_fusion.part0), channel_id=1, source_target_pairs={{0,3},{1,0},{2,1},{3,2},{4,7},{5,4},{6,5},{7,6},{8,11},{9,8},{10,9... | collective-permute-start | bytes 417800 | tf_op jit(solution)/shard_map/ppermute | solution.py:521
  23.9 21.3 %all-to-all-start = ((bf16[32,24,128]{2,1,0:T(8,128)(2,1)}), bf16[32,24,128]{2,1,0:T(8,128)(2,1)S(1)}, u32[]{:S(2)}, u32[]{:S(2)}) async-start(bf16[32,24,128]{2,1,0:T(8,128)(2,1)} %get-tuple-element.73), calls=%async_computation | async-start | bytes 393216 | tf_op jit(solution)/shard_map/all_to_all | solution.py:616
  35.8 24.0 %copy-start.6 = (f32[4,64]{1,0:T(4,128)S(1)}, f32[4,64]{1,0:T(4,128)}, u32[]{:S(2)}) copy-start(f32[4,64]{1,0:T(4,128)} %gain.3) | copy-start | bytes 3076
  35.8 20.8 %collective-permute-start.9 = (bf16[128,1024]{1,0:T(8,128)(2,1)S(1)}, bf16[128,1024]{1,0:T(8,128)(2,1)S(1)}, u32[]{:S(2)}, u32[]{:S(2)}) collective-permute-start(bf16[128,1024]{1,0:T(8,128)(2,1)S(1)} %get-tuple-element.84), channel_id=1, source_target_pairs={{0,1},{1,2},{2,3},{3,0},{4,5},{5,6},{6,7},{7,4},{8,9},{9,10},{10,1... | collective-permute-start | bytes 786440 | tf_op jit(solution)/shard_map/ppermute | solution.py:521
  36.8 19.9 %collective-permute-start.10 = (bf16[128,1024]{1,0:T(8,128)(2,1)S(1)}, bf16[128,1024]{1,0:T(8,128)(2,1)S(1)}, u32[]{:S(2)}, u32[]{:S(2)}) collective-permute-start(bf16[128,1024]{1,0:T(8,128)(2,1)S(1)} %get-tuple-element.84), channel_id=1, source_target_pairs={{0,2},{1,3},{2,0},{3,1},{4,6},{5,7},{6,4},{7,5},{8,10},{9,11},{10,... | collective-permute-start | bytes 786440 | tf_op jit(solution)/shard_map/ppermute | solution.py:521
  39.1 18.1 %collective-permute-start.11 = (bf16[128,1024]{1,0:T(8,128)(2,1)S(1)}, bf16[128,1024]{1,0:T(8,128)(2,1)S(1)}, u32[]{:S(2)}, u32[]{:S(2)}) collective-permute-start(bf16[128,1024]{1,0:T(8,128)(2,1)S(1)} %get-tuple-element.84), channel_id=1, source_target_pairs={{0,3},{1,0},{2,1},{3,2},{4,7},{5,4},{6,5},{7,6},{8,11},{9,8},{10,9... | collective-permute-start | bytes 786440 | tf_op jit(solution)/shard_map/ppermute | solution.py:521
  46.0 13.8 %all-to-all-start.1 = ((bf16[32,16,128]{2,1,0:T(8,128)(2,1)}), bf16[32,16,128]{2,1,0:T(8,128)(2,1)S(1)}, u32[]{:S(2)}, u32[]{:S(2)}) async-start(bf16[32,16,128]{2,1,0:T(8,128)(2,1)} %shard_map.123), calls=%async_computation.1 | async-start | bytes 262144 | tf_op jit(solution)/shard_map/all_to_all | solution.py:644
  50.6 17.4 %collective-permute-start.15 = (bf16[4,128,256]{2,1,0:T(8,128)(2,1)}, bf16[4,128,256]{2,1,0:T(8,128)(2,1)S(1)}, u32[]{:S(2)}, u32[]{:S(2)}) collective-permute-start(bf16[4,128,256]{2,1,0:T(8,128)(2,1)} %get-tuple-element.86), channel_id=1, source_target_pairs={{0,4},{4,0},{1,5},{5,1},{2,6},{6,2},{3,7},{7,3},{8,12},{12,8},{9,1... | collective-permute-start | bytes 786440 | tf_op jit(solution)/shard_map/ppermute | solution.py:621
  56.6 10.4 %copy-start.7 = (bf16[128,1024]{1,0:T(8,128)(2,1)}, bf16[128,1024]{1,0:T(8,128)(2,1)S(1)}, u32[]{:S(2)}) copy-start(bf16[128,1024]{1,0:T(8,128)(2,1)S(1)} %collective-permute-done.9.mine1) | copy-start | bytes 786436
  56.6 13.6 %collective-permute-start.12 = (bf16[128,1024]{1,0:T(8,128)(2,1)S(1)}, bf16[128,1024]{1,0:T(8,128)(2,1)S(1)}, u32[]{:S(2)}, u32[]{:S(2)}) collective-permute-start(bf16[128,1024]{1,0:T(8,128)(2,1)S(1)} %collective-permute-done.9.mine1), channel_id=1, source_target_pairs={{0,4},{4,0},{1,5},{5,1},{2,6},{6,2},{3,7},{7,3},{8,12},{12,8},{9,1... | collective-permute-start | bytes 786440 | tf_op jit(solution)/shard_map/ppermute | solution.py:620
  56.8 10.3 %copy-start.8 = (bf16[128,1024]{1,0:T(8,128)(2,1)}, bf16[128,1024]{1,0:T(8,128)(2,1)S(1)}, u32[]{:S(2)}) copy-start(bf16[128,1024]{1,0:T(8,128)(2,1)S(1)} %collective-permute-done.10.mine2) | copy-start | bytes 786436
  56.8 14.4 %collective-permute-start.13 = (bf16[128,1024]{1,0:T(8,128)(2,1)S(1)}, bf16[128,1024]{1,0:T(8,128)(2,1)S(1)}, u32[]{:S(2)}, u32[]{:S(2)}) collective-permute-start(bf16[128,1024]{1,0:T(8,128)(2,1)S(1)} %collective-permute-done.10.mine2), channel_id=1, source_target_pairs={{0,4},{4,0},{1,5},{5,1},{2,6},{6,2},{3,7},{7,3},{8,12},{12,8},{9,1... | collective-permute-start | bytes 786440 | tf_op jit(solution)/shard_map/ppermute | solution.py:620
  57.3 9.8 %copy-start.9 = (bf16[128,1024]{1,0:T(8,128)(2,1)}, bf16[128,1024]{1,0:T(8,128)(2,1)S(1)}, u32[]{:S(2)}) copy-start(bf16[128,1024]{1,0:T(8,128)(2,1)S(1)} %collective-permute-done.11.mine3) | copy-start | bytes 786436
  57.3 13.9 %collective-permute-start.14 = (bf16[128,1024]{1,0:T(8,128)(2,1)S(1)}, bf16[128,1024]{1,0:T(8,128)(2,1)S(1)}, u32[]{:S(2)}, u32[]{:S(2)}) collective-permute-start(bf16[128,1024]{1,0:T(8,128)(2,1)S(1)} %collective-permute-done.11.mine3), channel_id=1, source_target_pairs={{0,4},{4,0},{1,5},{5,1},{2,6},{6,2},{3,7},{7,3},{8,12},{12,8},{9,1... | collective-permute-start | bytes 786440 | tf_op jit(solution)/shard_map/ppermute | solution.py:620
  62.1 4.9 %collective-permute-start.5 = (bf16[128,256]{1,0:T(8,128)(2,1)S(1)}, bf16[128,256]{1,0:T(8,128)(2,1)S(1)}, u32[]{:S(2)}, u32[]{:S(2)}) collective-permute-start(bf16[128,256]{1,0:T(8,128)(2,1)S(1)} %get-tuple-element.82), channel_id=1, source_target_pairs={{0,4},{4,0},{1,5},{5,1},{2,6},{6,2},{3,7},{7,3},{8,12},{12,8},{9,1... | collective-permute-start | bytes 196616 | tf_op jit(solution)/shard_map/ppermute | solution.py:674
  67.1 7.5 %collective-permute-start.6 = (bf16[256,256]{1,0:T(8,128)(2,1)S(1)}, bf16[256,256]{1,0:T(8,128)(2,1)S(1)}, u32[]{:S(2)}, u32[]{:S(2)}) collective-permute-start(bf16[256,256]{1,0:T(8,128)(2,1)S(1)} %pad_maximum_fusion.1.part0), channel_id=1, source_target_pairs={{0,1},{1,2},{2,3},{3,0},{4,5},{5,6},{6,7},{7,4},{8,9},{9,10},{10,1... | collective-permute-start | bytes 393224 | tf_op jit(solution)/shard_map/ppermute | solution.py:521
  67.9 3.2 %copy-start.10 = (bf16[4,128,256]{2,1,0:T(8,128)(2,1)}, bf16[4,128,256]{2,1,0:T(8,128)(2,1)S(1)}, u32[]{:S(2)}) copy-start(bf16[4,128,256]{2,1,0:T(8,128)(2,1)S(1)} %collective-permute-done.15.passed) | copy-start | bytes 786436
  67.9 8.4 %collective-permute-start.7 = (bf16[256,256]{1,0:T(8,128)(2,1)S(1)}, bf16[256,256]{1,0:T(8,128)(2,1)S(1)}, u32[]{:S(2)}, u32[]{:S(2)}) collective-permute-start(bf16[256,256]{1,0:T(8,128)(2,1)S(1)} %pad_maximum_fusion.1.part0), channel_id=1, source_target_pairs={{0,2},{1,3},{2,0},{3,1},{4,6},{5,7},{6,4},{7,5},{8,10},{9,11},{10,... | collective-permute-start | bytes 393224 | tf_op jit(solution)/shard_map/ppermute | solution.py:521
  70.2 0.9 %copy-start.11 = (bf16[128,1024]{1,0:T(8,128)(2,1)}, bf16[128,1024]{1,0:T(8,128)(2,1)S(1)}, u32[]{:S(2)}) copy-start(bf16[128,1024]{1,0:T(8,128)(2,1)S(1)} %collective-permute-done.12.theirs1) | copy-start | bytes 786436
  70.2 6.1 %collective-permute-start.8 = (bf16[256,256]{1,0:T(8,128)(2,1)S(1)}, bf16[256,256]{1,0:T(8,128)(2,1)S(1)}, u32[]{:S(2)}, u32[]{:S(2)}) collective-permute-start(bf16[256,256]{1,0:T(8,128)(2,1)S(1)} %pad_maximum_fusion.1.part0), channel_id=1, source_target_pairs={{0,3},{1,0},{2,1},{3,2},{4,7},{5,4},{6,5},{7,6},{8,11},{9,8},{10,9... | collective-permute-start | bytes 393224 | tf_op jit(solution)/shard_map/ppermute | solution.py:521
  71.1 0.7 copy-start.12
  71.1 0.8 copy-start.13
  71.9 4.5 %copy-start.1 = (bf16[1024,1024]{1,0:T(8,128)(2,1)S(1)}, bf16[1024,1024]{1,0:T(8,128)(2,1)}, u32[]{:S(2)}) copy-start(bf16[1024,1024]{1,0:T(8,128)(2,1)} %up.1) | copy-start | bytes 6291460
  71.9 4.5 %copy-start.4 = (f32[1024]{0:T(1024)S(1)}, f32[1024]{0:T(1024)}, u32[]{:S(2)}) copy-start(f32[1024]{0:T(1024)} %param.21) | copy-start | bytes 12292
  78.8 5.9 %collective-permute-start.16 = (bf16[256,256]{1,0:T(8,128)(2,1)S(1)}, bf16[256,256]{1,0:T(8,128)(2,1)S(1)}, u32[]{:S(2)}, u32[]{:S(2)}) collective-permute-start(bf16[256,256]{1,0:T(8,128)(2,1)S(1)} %get-tuple-element.92), channel_id=1, source_target_pairs={{0,1},{1,2},{2,3},{3,0},{4,5},{5,6},{6,7},{7,4},{8,9},{9,10},{10,1... | collective-permute-start | bytes 393224 | tf_op jit(solution)/shard_map/ppermute | solution.py:521
  80.9 8.0 %collective-permute-start.17 = (bf16[256,256]{1,0:T(8,128)(2,1)S(1)}, bf16[256,256]{1,0:T(8,128)(2,1)S(1)}, u32[]{:S(2)}, u32[]{:S(2)}) collective-permute-start(bf16[256,256]{1,0:T(8,128)(2,1)S(1)} %get-tuple-element.93), channel_id=1, source_target_pairs={{0,2},{1,3},{2,0},{3,1},{4,6},{5,7},{6,4},{7,5},{8,10},{9,11},{10,... | collective-permute-start | bytes 393224 | tf_op jit(solution)/shard_map/ppermute | solution.py:521
  83.1 5.8 %collective-permute-start.18 = (bf16[256,256]{1,0:T(8,128)(2,1)S(1)}, bf16[256,256]{1,0:T(8,128)(2,1)S(1)}, u32[]{:S(2)}, u32[]{:S(2)}) collective-permute-start(bf16[256,256]{1,0:T(8,128)(2,1)S(1)} %get-tuple-element.94), channel_id=1, source_target_pairs={{0,3},{1,0},{2,1},{3,2},{4,7},{5,4},{6,5},{7,6},{8,11},{9,8},{10,9... | collective-permute-start | bytes 393224 | tf_op jit(solution)/shard_map/ppermute | solution.py:521
